TPU v7x, 32 devices: a whole 2x2x4 slice. The times are simulated.
32 devices in a mesh: gx: 8 (over z, y), gy: 4 (over x, core).
Axes of the slice: x: 2, y: 2, z: 4, core: 2. Of those that a mesh axis runs over, the one named last changes fastest.
Arguments:
- electric: float32 [3, 128, 512, 128], P(None, 'gx', 'gy'), may hold values from -6 to 6
- magnetic: float32 [3, 128, 512, 128], P(None, 'gx', 'gy'), may hold values from -6 to 6
- retention: float32 [128, 512, 128], P('gx', 'gy'), may hold values from 0.5 to 1
- coupling: float32 [128, 512, 128], P('gx', 'gy'), may hold values from 0.1 to 0.5
- spectrum_real: float32 [4, 4, 128, 512], P(None, None, 'gx', 'gy'), may hold values from -6 to 6
- spectrum_imag: float32 [4, 4, 128, 512], P(None, None, 'gx', 'gy'), may hold values from -6 to 6
- phases: float32 [4], replicated, may hold values from -3.140625 to 3.140625
Outputs:
- next_electric: float32 [3, 128, 512, 128], P(None, 'gx', 'gy')
- next_magnetic: float32 [3, 128, 512, 128], P(None, 'gx', 'gy')
- next_real: float32 [4, 4, 128, 512], P(None, None, 'gx', 'gy')
- next_imag: float32 [4, 4, 128, 512], P(None, None, 'gx', 'gy')
- far_field: float32 [2, 4, 4, 256, 256], P(None, None, None, 'gx', 'gy')
All inputs are finite; a program needn't handle non-finite values.
Results may differ from a plain program's by a relative error of at most 0.000071.
Values sent between devices are 32-bit elements; how exact they have to be, the bound alone decides.
No kernel may reach another device: no remote copies, remote signals or barrier semaphores. Data moves between devices by JAX's collectives and lax.ppermute only.
A program may use at most 128 MiB of HBM per device.

v0:
```python
import math

import jax
import jax.numpy as jnp
from jax import lax
from jax.sharding import PartitionSpec as P

WAVES = 256
TOP_PLANE = 111


curl_step = 0.5


def passed_along(value, axis, by):
    devices = lax.axis_size(axis)
    pairs = [(i, i + by) for i in range(devices) if 0 <= i + by < devices]
    return lax.ppermute(value, axis, pairs)


def forward_diff(values, along):
    padded = jnp.pad(values, [(0, 1) if which == along else (0, 0) for which in range(values.ndim)])
    return lax.slice_in_dim(padded, 1, values.shape[along] + 1, axis=along) - values


def backward_diff(values, along):
    padded = jnp.pad(values, [(1, 0) if which == along else (0, 0) for which in range(values.ndim)])
    return values - lax.slice_in_dim(padded, 0, values.shape[along], axis=along)


def ahead_diff(values, border, along):
    upper = lax.slice_in_dim(values, 1, values.shape[along], axis=along)
    return jnp.concatenate([upper, border], axis=along) - values


def behind_diff(values, border, along):
    lower = lax.slice_in_dim(values, 0, values.shape[along] - 1, axis=along)
    return values - jnp.concatenate([border, lower], axis=along)


def tables(number, extent, offset):
    wave = 2 * jnp.arange(number, dtype=jnp.int32) + 1 - number
    places = offset + jnp.arange(extent, dtype=jnp.int32)
    folded = wave[:, None] * places[None, :] % (4 * number)
    angles = folded.astype(jnp.float32) * (math.pi / (2 * number))
    return (jnp.cos(angles), jnp.sin(angles))


def first_section(real_part, imag_part, cos_y, sin_y):
    highest = lax.Precision.HIGHEST
    part_real = jnp.einsum("cfxy,ky->cfxk", real_part, cos_y, precision=highest) + jnp.einsum(
        "cfxy,ky->cfxk", imag_part, sin_y, precision=highest
    )
    part_imag = jnp.einsum("cfxy,ky->cfxk", imag_part, cos_y, precision=highest) - jnp.einsum(
        "cfxy,ky->cfxk", real_part, sin_y, precision=highest
    )
    return (part_real, part_imag)


def second_section(part_real, part_imag, cos_x, sin_x):
    highest = lax.Precision.HIGHEST
    far_real = jnp.einsum("jx,cfxk->cfjk", cos_x, part_real, precision=highest) + jnp.einsum(
        "jx,cfxk->cfjk", sin_x, part_imag, precision=highest
    )
    far_imag = jnp.einsum("jx,cfxk->cfjk", cos_x, part_imag, precision=highest) - jnp.einsum(
        "jx,cfxk->cfjk", sin_x, part_real, precision=highest
    )
    return jnp.stack([far_real, far_imag])


def per_device(electric, magnetic, retention, coupling, spectrum_real, spectrum_imag, phases):
    elec_x, elec_y, elec_z = (electric[0], electric[1], electric[2])
    rows_elec = passed_along(electric[1:3, 0:1], "gx", -1)
    cols_elec = passed_along(electric[0:3:2, :, 0:1], "gy", -1)
    mag_x = magnetic[0] - curl_step * (
        ahead_diff(elec_z, cols_elec[1], 1) - forward_diff(elec_y, 2)
    )
    mag_y = magnetic[1] - curl_step * (
        forward_diff(elec_x, 2) - ahead_diff(elec_z, rows_elec[1], 0)
    )
    mag_z = magnetic[2] - curl_step * (
        ahead_diff(elec_y, rows_elec[0], 0) - ahead_diff(elec_x, cols_elec[0], 1)
    )
    next_magnetic = jnp.stack([mag_x, mag_y, mag_z])
    rows_magn = passed_along(next_magnetic[1:3, -1:], "gx", 1)
    cols_magn = passed_along(next_magnetic[0:3:2, :, -1:], "gy", 1)
    new_x = retention * elec_x + coupling * (
        behind_diff(mag_z, cols_magn[1], 1) - backward_diff(mag_y, 2)
    )
    new_y = retention * elec_y + coupling * (
        backward_diff(mag_x, 2) - behind_diff(mag_z, rows_magn[1], 0)
    )
    new_z = retention * elec_z + coupling * (
        behind_diff(mag_y, rows_magn[0], 0) - behind_diff(mag_x, cols_magn[0], 1)
    )
    next_electric = jnp.stack([new_x, new_y, new_z])
    tangent = jnp.stack(
        [
            new_x[:, :, TOP_PLANE],
            new_y[:, :, TOP_PLANE],
            mag_x[:, :, TOP_PLANE],
            mag_y[:, :, TOP_PLANE],
        ]
    )
    next_real = spectrum_real + tangent[:, None] * jnp.cos(phases)[None, :, None, None]
    next_imag = spectrum_imag - tangent[:, None] * jnp.sin(phases)[None, :, None, None]
    local_rows = electric.shape[1]
    local_cols = electric.shape[2]
    scale = 1.0 / math.sqrt(local_rows * lax.axis_size("gx") * local_cols * lax.axis_size("gy"))
    cos_y, sin_y = tables(WAVES, local_cols, lax.axis_index("gy") * local_cols)
    part_real, part_imag = first_section(next_real, next_imag, cos_y, sin_y)
    cos_full, sin_full = tables(WAVES, local_rows * lax.axis_size("gx"), 0)
    reduced = lax.psum_scatter(
        jnp.stack([part_real, part_imag]), "gy", scatter_dimension=4, tiled=True
    )
    columns = lax.all_to_all(reduced, "gx", split_axis=4, concat_axis=3, tiled=True)
    finished = second_section(columns[0], columns[1], cos_full, sin_full)
    whole = lax.all_to_all(finished, "gx", split_axis=3, concat_axis=4, tiled=True)
    far_field = whole * scale
    return (next_electric, next_magnetic, next_real, next_imag, far_field)


def solution(mesh):
    placed = (
        P(None, "gx", "gy", None),
        P(None, "gx", "gy", None),
        P("gx", "gy", None),
        P("gx", "gy", None),
        P(None, None, "gx", "gy"),
        P(None, None, "gx", "gy"),
        P(),
    )
    return jax.shard_map(
        per_device,
        mesh=mesh,
        in_specs=placed,
        out_specs=(
            P(None, "gx", "gy", None),
            P(None, "gx", "gy", None),
            P(None, None, "gx", "gy"),
            P(None, None, "gx", "gy"),
            P(None, None, None, "gx", "gy"),
        ),
        check_vma=False,
    )
```

profile of v0, /device:TPU:0, one launch (start us, length us, event | category | flops | bytes accessed | tf_op | source)
XLA Modules:
  0.0 151.3 jit_solution(2751149047137637543)
XLA Ops:
  7.2 0.0 reduce-scatter.4.cloned.1.call-start
  7.2 0.9 slice.127
  8.1 1.3 collective-permute-start.1
  9.4 0.9 slice.123
  10.4 1.3 collective-permute-start
  11.7 2.3 %slice_bitcast_fusion.2 = f32[16,128,128]{2,1,0:T(8,128)} fusion(f32[3,16,128,128]{3,2,1,0:T(8,128)} %param.7), kind=kLoop, calls=%fused_computation.58 | loop fusion | bytes 2097152 | tf_op jit(solution)/shard_map/squeeze | solution.py:72
  14.0 3.4 %slice_bitcast_fusion.10 = (f32[15,128,128]{2,1,0:T(8,128)}, f32[1,15,128,128]{3,2,1,0:T(8,128)}, f32[15,128,128]{2,1,0:T(8,128)}) fusion(f32[3,16,128,128]{3,2,1,0:T(8,128)} %param.7), kind=kLoop, calls=%fused_computation.139 | loop fusion | bytes 4915200 | tf_op jit(solution)/shard_map/slice | solution.py:32
  17.5 2.8 %fusion.96 = (f32[16,127,128]{2,1,0:T(8,128)}, f32[1,16,127,128]{3,2,1,0:T(8,128)}) fusion(f32[16,128,128]{2,1,0:T(8,128)} %slice_bitcast_fusion.2), kind=kLoop, calls=%fused_computation.142 | loop fusion | bytes 3121152 | tf_op jit(solution)/shard_map/slice | solution.py:32
  20.3 0.0 copy-start.1
  20.4 2.5 %slice_bitcast_fusion = (f32[16,128,128]{2,1,0:T(8,128)S(1)}, f32[1,16,128,128]{3,2,1,0:T(8,128)S(1)}, f32[16,128,128]{2,1,0:T(8,128)S(1)}) fusion(f32[3,16,128,128]{3,2,1,0:T(8,128)S(1)} %copy-done, f32[1,16,1,128]{3,2,1,0:T(1,128)S(1)} %bitcast.155, f32[1,16,127,128]{3,2,1,0:T(8,128)} %get-tuple-element.55, f32[1,1,128,128]{3,2,1,0:T(8,128)S(1)} %get-tuple-element.60, ...), kind=kLoop, calls=%fused_computation.56 | loop fusion | flops 1835008 | bytes 9437184 | tf_op jit(solution)/shard_map/squeeze | solution.py:72
  22.9 0.1 slice.160
  23.0 0.4 copy-done.6
  23.5 0.3 copy-done.7
  23.8 0.3 copy-done.9
  24.1 0.3 copy-done.10
  24.3 1.8 %fusion.22 = (f32[16,128,128]{2,1,0:T(8,128)S(1)}, f32[16,128,128]{2,1,0:T(8,128)S(1)}, f32[16,128,128]{2,1,0:T(8,128)S(1)}) fusion(f32[1,128,128]{2,1,0:T(8,128)S(1)} %get-tuple-element.58, f32[15,128,128]{2,1,0:T(8,128)S(1)} %copy-done.9, f32[16,1,128]{2,1,0:T(1,128)S(1)} %bitcast.156, f32[16,127,128]{2,1,0:T(8,128)S(1)} %copy-done.7, ...), kind=kLoop, calls=%fused_computation.38 | loop fusion | flops 4980736 | bytes 15728640 | tf_op jit(solution)/shard_map/sub | solution.py:81
  26.1 1.2 slice_reduce_fusion
  27.3 0.2 pad_maximum_fusion
  27.6 3.3 %collective-permute-start.2 = (f32[2,16,1,128]{3,2,1,0:T(1,128)S(1)}, f32[2,16,1,128]{3,2,1,0:T(1,128)S(1)}, u32[]{:S(2)}, u32[]{:S(2)}) collective-permute-start(f32[2,16,1,128]{3,2,1,0:T(1,128)S(1)} %slice.139), channel_id=1, source_target_pairs={{0,1},{1,2},{2,3},{4,5},{5,6},{6,7},{8,9},{9,10},{10,11},{12,13},{... | collective-permute-start | bytes 49160 | tf_op jit(solution)/shard_map/ppermute | solution.py:18
  30.9 0.1 slice.168
  31.0 5.7 %collective-permute-start.3 = (f32[2,1,128,128]{3,2,1,0:T(8,128)S(1)}, f32[2,1,128,128]{3,2,1,0:T(8,128)S(1)}, u32[]{:S(2)}, u32[]{:S(2)}) collective-permute-start(f32[2,1,128,128]{3,2,1,0:T(8,128)S(1)} %pad_maximum_fusion.4), channel_id=1, source_target_pairs={{0,4},{4,8},{8,12},{12,16},{16,20},{20,24},{24,28},{1,5},{5,9},{9,... | collective-permute-start | bytes 393224 | tf_op jit(solution)/shard_map/ppermute | solution.py:18
  36.7 0.1 slice.166
  36.8 2.9 %collective-permute-done.3 = f32[2,1,128,128]{3,2,1,0:T(8,128)S(1)} collective-permute-done((f32[2,1,128,128]{3,2,1,0:T(8,128)S(1)}, f32[2,1,128,128]{3,2,1,0:T(8,128)S(1)}, u32[]{:S(2)}, u32[]{:S(2)}) %collective-permute-start.3) | collective-permute-done | bytes 131104 | tf_op jit(solution)/shard_map/ppermute | solution.py:18
  39.8 2.6 %fusion.15 = (f32[16,128,128]{2,1,0:T(8,128)S(1)}, f32[1,16,128,128]{3,2,1,0:T(8,128)}, f32[16,128,128]{2,1,0:T(8,128)S(1)}) fusion(f32[16,128,128]{2,1,0:T(8,128)S(1)} %copy-done.12, f32[16,128,128]{2,1,0:T(8,128)S(1)} %get-tuple-element.44, f32[16,128,128]{2,1,0:T(8,128)S(1)} %get-tuple-element.43, f32[16,127,128]{2,1,0:T(8,128)S(1)} %bitcast.149, ...), kind=kLoop, calls=%fused_computation.26 | loop fusion | flops 5767168 | bytes 15728640 | tf_op jit(solution)/shard_map/add | solution.py:87
  42.5 1.0 copy-done.2
  43.4 1.2 slice_reduce_fusion.2
  44.7 0.1 multiply_subtract_fusion
  44.8 0.0 copy-start.15
  44.8 0.0 copy-start.14
  44.8 0.9 fusion.44
  45.7 0.9 fusion.46
  46.6 0.9 fusion
  47.6 0.9 fusion.1
  48.6 3.4 %copy.200 = f32[2,4,4,16,256]{3,2,1,0,4:T(4,128)} copy(f32[2,4,4,16,256]{4,3,2,1,0:T(8,128)S(1)} %pad_maximum_fusion.2) | data formatting | bytes 1048576
  51.9 5.9 %reshape.43 = f32[256,512]{1,0:T(8,128)} reshape(f32[256,2,4,4,16]{4,3,2,1,0:T(4,128)} %bitcast.146) | data formatting | bytes 1048576
  57.9 0.0 reduce-scatter.4.cloned.1.call-update
  57.9 24.4 %reduce-scatter.4.cloned.1.call-done = f32[64,512]{1,0:T(8,128)} async-done(((f32[256,512]{1,0:T(8,128)}), f32[64,512]{1,0:T(8,128)}) %reduce-scatter.4.cloned.1.call-update) | async-done | bytes 131088
  82.3 1.6 %reshape.44 = f32[64,2,4,4,16]{4,3,2,1,0:T(4,128)S(1)} reshape(f32[64,512]{1,0:T(8,128)} %reduce-scatter.4.cloned.1.call-done) | data formatting | bytes 262144
  83.9 0.1 bitcast_bitcast_fusion
  84.0 0.8 reshape.49
  84.8 12.7 %all_to_all.24 = f32[8,1,4096]{2,1,0:T(1,128)S(1)} all-to-all(f32[8,1,4096]{2,1,0:T(1,128)S(1)} %reshape.49), channel_id=1, replica_groups=mesh['gx'=8,'gy'=4] {'gx'}, dimensions={0} | all-to-all | bytes 262144 | tf_op jit(solution)/shard_map/all_to_all | solution.py:116
  97.5 0.5 broadcast.137
  98.0 0.9 reduce.8
  98.9 0.7 reshape.50
  99.6 0.6 copy.204
  100.2 0.1 fusion.95
  100.3 0.1 copy.191
  100.4 0.2 squeeze.62
  100.6 0.8 fusion.40
  101.4 0.1 copy.192
  101.5 0.2 squeeze.63
  101.7 0.8 fusion.38
  102.6 0.8 fusion.3
  103.4 0.8 fusion.2
  104.3 3.3 %copy.193 = f32[2,4,4,256,8]{4,2,1,0,3:T(4,128)} copy(f32[2,4,4,256,8]{3,4,2,1,0:T(8,128)S(1)} %pad_maximum_fusion.3) | data formatting | bytes 524288 | tf_op jit(solution)/shard_map/stack | solution.py:68
  107.6 7.3 %reshape.51 = f32[8,1,8192]{2,1,0:T(1,128)} reshape(f32[256,2,4,4,8]{4,3,2,1,0:T(4,128)} %bitcast.148) | data formatting | bytes 524288
  114.9 3.7 %all-to-all-start.1 = ((f32[8,1,8192]{2,1,0:T(1,128)}), f32[8,1,8192]{2,1,0:T(1,128)S(1)}, u32[]{:S(2)}, u32[]{:S(2)}) async-start(f32[8,1,8192]{2,1,0:T(1,128)} %reshape.51), calls=%async_computation.1 | async-start | bytes 524288 | tf_op jit(solution)/shard_map/all_to_all | solution.py:118
  118.6 1.9 %pad_maximum_fusion.1 = f32[3,16,128,128]{3,2,1,0:T(8,128)} fusion(f32[1,16,128,128]{3,2,1,0:T(8,128)S(1)} %copy-done.8, f32[1,16,128,128]{3,2,1,0:T(8,128)S(1)} %bitcast.151, f32[1,16,128,128]{3,2,1,0:T(8,128)S(1)} %bitcast.150), kind=kLoop, calls=%fused_computation.1 | loop fusion | flops 1572864 | bytes 6291456 | tf_op jit(solution)/shard_map/stack | solution.py:96
  120.5 6.0 %all-to-all-done.1 = f32[8,1,8192]{2,1,0:T(1,128)S(1)} async-done(((f32[8,1,8192]{2,1,0:T(1,128)}), f32[8,1,8192]{2,1,0:T(1,128)S(1)}, u32[]{:S(2)}, u32[]{:S(2)}) %all-to-all-start.1) | async-done | bytes 262176 | tf_op jit(solution)/shard_map/all_to_all | solution.py:118
  126.5 1.2 reduce.9
  127.7 6.9 %reshape.52 = f32[256,2,4,4,8]{4,3,2,1,0:T(4,128)} reshape(f32[8,8192]{1,0:T(8,128)S(1)} %reduce.9) | data formatting | bytes 524288
  134.6 5.2 %broadcast_multiply_fusion = f32[2,4,4,256,8]{4,2,1,0,3:T(4,128)} fusion(f32[256,2,4,4,8]{4,3,2,1,0:T(4,128)} %reshape.52), kind=kLoop, calls=%fused_computation.2 | loop fusion | flops 65536 | bytes 524288 | tf_op jit(solution)/shard_map/mul | solution.py:119
  139.8 3.6 %copy.194 = f32[2,4,4,8,32,8]{4,5,3,2,1,0:T(8,128)S(1)} copy(f32[2,4,4,8,32,8]{5,2,1,0,4,3:T(4,128)} %bitcast.147) | data formatting | bytes 524288 | tf_op jit(solution)/shard_map/mul | solution.py:119
  143.4 1.1 copy.195
  (45 shorter events, 0.3 us)
Async XLA Ops:
  7.2 75.1 %reduce-scatter.4.cloned.1.call-start = ((), (), s32[]{:S(2)}) async-start(), calls=%async_computation.3 | async-start | bytes 655360
  8.1 12.2 %collective-permute-start.1 = (f32[2,16,1,128]{3,1,2,0:T(8,128)S(1)}, f32[2,16,1,128]{3,1,2,0:T(8,128)S(1)}, u32[]{:S(2)}, u32[]{:S(2)}) collective-permute-start(f32[2,16,1,128]{3,1,2,0:T(8,128)S(1)} %bitcast.162), channel_id=1, source_target_pairs={{1,0},{2,1},{3,2},{5,4},{6,5},{7,6},{9,8},{10,9},{11,10},{13,12},{... | collective-permute-start | bytes 49160 | tf_op jit(solution)/shard_map/ppermute | solution.py:18
  10.4 9.9 %collective-permute-start = (f32[2,1,128,128]{3,2,1,0:T(8,128)S(1)}, f32[2,1,128,128]{3,2,1,0:T(8,128)S(1)}, u32[]{:S(2)}, u32[]{:S(2)}) collective-permute-start(f32[2,1,128,128]{3,2,1,0:T(8,128)S(1)} %slice.123), channel_id=1, source_target_pairs={{4,0},{8,4},{12,8},{16,12},{20,16},{24,20},{28,24},{5,1},{9,5},{13... | collective-permute-start | bytes 393224 | tf_op jit(solution)/shard_map/ppermute | solution.py:18
  11.7 5.8 %copy-start.18 = (f32[4]{0:T(128)S(1)}, f32[4]{0:T(128)}, u32[]{:S(2)}) copy-start(f32[4]{0:T(128)} %param.13) | copy-start | bytes 52
  14.0 6.3 %copy-start = (f32[3,16,128,128]{3,2,1,0:T(8,128)S(1)}, f32[3,16,128,128]{3,2,1,0:T(8,128)}, u32[]{:S(2)}) copy-start(f32[3,16,128,128]{3,2,1,0:T(8,128)} %param.7) | copy-start | bytes 9437188
  20.3 2.7 %copy-start.1 = (f32[16,128,128]{2,1,0:T(8,128)S(1)}, f32[16,128,128]{2,1,0:T(8,128)}, u32[]{:S(2)}) copy-start(f32[16,128,128]{2,1,0:T(8,128)} %slice_bitcast_fusion.2) | copy-start | bytes 3145732
  20.4 3.1 %copy-start.6 = (f32[3,16,128,128]{3,2,1,0:T(8,128)S(1)}, f32[3,16,128,128]{3,2,1,0:T(8,128)}, u32[]{:S(2)}) copy-start(f32[3,16,128,128]{3,2,1,0:T(8,128)} %param.8) | copy-start | bytes 9437188
  20.4 3.4 %copy-start.7 = (f32[16,127,128]{2,1,0:T(8,128)S(1)}, f32[16,127,128]{2,1,0:T(8,128)}, u32[]{:S(2)}) copy-start(f32[16,127,128]{2,1,0:T(8,128)} %get-tuple-element.54) | copy-start | bytes 3121156
  20.4 3.7 %copy-start.9 = (f32[15,128,128]{2,1,0:T(8,128)S(1)}, f32[15,128,128]{2,1,0:T(8,128)}, u32[]{:S(2)}) copy-start(f32[15,128,128]{2,1,0:T(8,128)} %get-tuple-element.46) | copy-start | bytes 2949124
  20.4 4.0 %copy-start.10 = (f32[15,128,128]{2,1,0:T(8,128)S(1)}, f32[15,128,128]{2,1,0:T(8,128)}, u32[]{:S(2)}) copy-start(f32[15,128,128]{2,1,0:T(8,128)} %get-tuple-element.48) | copy-start | bytes 2949124
  27.5 12.3 %copy-start.11 = (f32[3,16,128,128]{3,2,1,0:T(8,128)}, f32[3,16,128,128]{3,2,1,0:T(8,128)S(1)}, u32[]{:S(2)}) copy-start(f32[3,16,128,128]{3,2,1,0:T(8,128)S(1)} %pad_maximum_fusion) | copy-start | bytes 9437188
  27.5 12.2 %copy-start.12 = (f32[16,128,128]{2,1,0:T(8,128)S(1)}, f32[16,128,128]{2,1,0:T(8,128)}, u32[]{:S(2)}) copy-start(f32[16,128,128]{2,1,0:T(8,128)} %param.10) | copy-start | bytes 3145732
  27.5 12.2 %copy-start.13 = (f32[16,128,128]{2,1,0:T(8,128)S(1)}, f32[16,128,128]{2,1,0:T(8,128)}, u32[]{:S(2)}) copy-start(f32[16,128,128]{2,1,0:T(8,128)} %param.9) | copy-start | bytes 3145732
  27.6 9.2 %collective-permute-start.2 = (f32[2,16,1,128]{3,2,1,0:T(1,128)S(1)}, f32[2,16,1,128]{3,2,1,0:T(1,128)S(1)}, u32[]{:S(2)}, u32[]{:S(2)}) collective-permute-start(f32[2,16,1,128]{3,2,1,0:T(1,128)S(1)} %slice.139), channel_id=1, source_target_pairs={{0,1},{1,2},{2,3},{4,5},{5,6},{6,7},{8,9},{9,10},{10,11},{12,13},{... | collective-permute-start | bytes 49160 | tf_op jit(solution)/shard_map/ppermute | solution.py:18
  31.0 8.8 %collective-permute-start.3 = (f32[2,1,128,128]{3,2,1,0:T(8,128)S(1)}, f32[2,1,128,128]{3,2,1,0:T(8,128)S(1)}, u32[]{:S(2)}, u32[]{:S(2)}) collective-permute-start(f32[2,1,128,128]{3,2,1,0:T(8,128)S(1)} %pad_maximum_fusion.4), channel_id=1, source_target_pairs={{0,4},{4,8},{8,12},{12,16},{16,20},{20,24},{24,28},{1,5},{5,9},{9,... | collective-permute-start | bytes 393224 | tf_op jit(solution)/shard_map/ppermute | solution.py:18
  39.8 4.8 %copy-start.16 = (f32[4,4,16,128]{3,2,1,0:T(8,128)S(1)}, f32[4,4,16,128]{3,2,1,0:T(8,128)}, u32[]{:S(2)}) copy-start(f32[4,4,16,128]{3,2,1,0:T(8,128)} %param.12) | copy-start | bytes 393220
  39.8 4.8 %copy-start.17 = (f32[4,4,16,128]{3,2,1,0:T(8,128)S(1)}, f32[4,4,16,128]{3,2,1,0:T(8,128)}, u32[]{:S(2)}) copy-start(f32[4,4,16,128]{3,2,1,0:T(8,128)} %param.11) | copy-start | bytes 393220
  42.5 1.0 copy-start.2
  42.5 2.2 %copy-start.4 = (f32[16,128,128]{2,1,0:T(8,128)}, f32[16,128,128]{2,1,0:T(8,128)S(1)}, u32[]{:S(2)}) copy-start(f32[16,128,128]{2,1,0:T(8,128)S(1)} %get-tuple-element.42) | copy-start | bytes 3145732
  44.8 2.8 %copy-start.15 = (f32[4,4,16,128]{3,2,1,0:T(8,128)}, f32[4,4,16,128]{3,2,1,0:T(8,128)S(1)}, u32[]{:S(2)}) copy-start(f32[4,4,16,128]{3,2,1,0:T(8,128)S(1)} %get-tuple-element.62) | copy-start | bytes 393220
  44.8 7.2 %copy-start.14 = (f32[4,4,16,128]{3,2,1,0:T(8,128)}, f32[4,4,16,128]{3,2,1,0:T(8,128)S(1)}, u32[]{:S(2)}) copy-start(f32[4,4,16,128]{3,2,1,0:T(8,128)S(1)} %get-tuple-element.61) | copy-start | bytes 393220
  107.6 11.0 %copy-start.3 = (f32[16,128,128]{2,1,0:T(8,128)S(1)}, f32[16,128,128]{2,1,0:T(8,128)}, u32[]{:S(2)}) copy-start(f32[16,128,128]{2,1,0:T(8,128)} %copy-done.2) | copy-start | bytes 3145732
  107.6 11.0 %copy-start.5 = (f32[16,128,128]{2,1,0:T(8,128)S(1)}, f32[16,128,128]{2,1,0:T(8,128)}, u32[]{:S(2)}) copy-start(f32[16,128,128]{2,1,0:T(8,128)} %copy-done.4) | copy-start | bytes 3145732
  107.6 11.0 %copy-start.8 = (f32[1,16,128,128]{3,2,1,0:T(8,128)S(1)}, f32[1,16,128,128]{3,2,1,0:T(8,128)}, u32[]{:S(2)}) copy-start(f32[1,16,128,128]{3,2,1,0:T(8,128)} %get-tuple-element.41) | copy-start | bytes 3145732
  114.9 11.6 %all-to-all-start.1 = ((f32[8,1,8192]{2,1,0:T(1,128)}), f32[8,1,8192]{2,1,0:T(1,128)S(1)}, u32[]{:S(2)}, u32[]{:S(2)}) async-start(f32[8,1,8192]{2,1,0:T(1,128)} %reshape.51), calls=%async_computation.1 | async-start | bytes 524288 | tf_op jit(solution)/shard_map/all_to_all | solution.py:118
Sparse Core Ops, SparseCore 0:
  58.0 24.2 reduce-scatter.3
where the time goes:
time: 152 us; the launch traced here: 151 us
  local copies, waits for them, and re-layouts  52 us (34%)
  waiting for transfers between devices  33.3 us (22%)
  other arithmetic  16.4 us (11%)
  starting transfers between devices  15.3 us (10%)
  between operations  14.6 us (10%)
  blocking collectives  12.7 us (8%)
  matrix products  6.97 us (5%)
    unnamed x47, local copies, waits for them, and re-layouts  30.3 us
    unnamed x2, waiting for transfers between devices  24.4 us
    all_to_all x1, blocking collectives, per_device(): lax.all_to_all(reduced, 'gx', split_axis=4, concat_axis=3, tiled=True)  12.7 us
    ppermute x4, starting transfers between devices, passed_along(): return lax.ppermute(value, axis, pairs)  11.6 us
    slice x3, local copies, waits for them, and re-layouts, ahead_diff(): upper = lax.slice_in_dim(values, 1, values.shape[along], axis=along)  6.34 us
    all_to_all x1, waiting for transfers between devices, per_device(): lax.all_to_all(finished, 'gx', split_axis=3, concat_axis=4, tiled=True)  6 us
    mul x1, other arithmetic, per_device(): far_field = whole * scale  5.21 us
    all_to_all x1, starting transfers between devices, per_device(): lax.all_to_all(finished, 'gx', split_axis=3, concat_axis=4, tiled=True)  3.67 us
  transfers between devices with their start and end apart: 6, of which 3 were waited for; matrix products, arithmetic and copies ran while one was open for 8% of the time, Pallas kernels for 0%

commit v1 on v0

--- a/solution.py
+++ b/solution.py
@@ -2,11 +2,13 @@
 
 import jax
 import jax.numpy as jnp
+import numpy as np
 from jax import lax
 from jax.sharding import PartitionSpec as P
 
 WAVES = 256
 TOP_PLANE = 111
+BOTH = ("gx", "gy")
 
 
 curl_step = 0.5
@@ -38,34 +40,62 @@
     return values - jnp.concatenate([border, lower], axis=along)
 
 
-def tables(number, extent, offset):
-    wave = 2 * jnp.arange(number, dtype=jnp.int32) + 1 - number
-    places = offset + jnp.arange(extent, dtype=jnp.int32)
-    folded = wave[:, None] * places[None, :] % (4 * number)
-    angles = folded.astype(jnp.float32) * (math.pi / (2 * number))
-    return (jnp.cos(angles), jnp.sin(angles))
+def wave_tables(number, extent):
+    wave = 2 * np.arange(number) + 1 - number
+    angles = (wave[:, None] * np.arange(extent)[None, :] % (4 * number)) * (math.pi / (2 * number))
+    return np.cos(angles).astype(np.float32), np.sin(angles).astype(np.float32)
 
 
-def first_section(real_part, imag_part, cos_y, sin_y):
-    highest = lax.Precision.HIGHEST
-    part_real = jnp.einsum("cfxy,ky->cfxk", real_part, cos_y, precision=highest) + jnp.einsum(
-        "cfxy,ky->cfxk", imag_part, sin_y, precision=highest
-    )
-    part_imag = jnp.einsum("cfxy,ky->cfxk", imag_part, cos_y, precision=highest) - jnp.einsum(
-        "cfxy,ky->cfxk", real_part, sin_y, precision=highest
-    )
-    return (part_real, part_imag)
+def swapped(value, by):
+    devices = lax.axis_size(BOTH)
+    return lax.ppermute(value, BOTH, [(i, i ^ by) for i in range(devices)])
 
 
-def second_section(part_real, part_imag, cos_x, sin_x):
+def far_of(next_real, next_imag):
     highest = lax.Precision.HIGHEST
-    far_real = jnp.einsum("jx,cfxk->cfjk", cos_x, part_real, precision=highest) + jnp.einsum(
-        "jx,cfxk->cfjk", sin_x, part_imag, precision=highest
-    )
-    far_imag = jnp.einsum("jx,cfxk->cfjk", cos_x, part_imag, precision=highest) - jnp.einsum(
-        "jx,cfxk->cfjk", sin_x, part_real, precision=highest
-    )
-    return jnp.stack([far_real, far_imag])
+    comps, freqs, rows, cols = next_real.shape
+    along_x, along_y = lax.axis_size("gx"), lax.axis_size("gy")
+    devices = along_x * along_y
+    planes = comps * freqs
+    share = devices // planes
+    part_rows = rows // share
+    wide = WAVES // along_y
+    part_wide = wide // share
+    tall = WAVES // along_x
+    place = lax.axis_index(BOTH) % share
+
+    both = jnp.stack([next_real, next_imag]).reshape(2, planes, share, part_rows, cols)
+    both = both.transpose(1, 2, 0, 3, 4).reshape(devices, 2, part_rows, cols)
+    got = lax.all_to_all(both, BOTH, split_axis=0, concat_axis=0, tiled=True)
+    got = got.reshape(along_x, along_y, 2, part_rows, cols)
+
+    cos_y, sin_y = wave_tables(WAVES, cols * along_y)
+    order_k = np.arange(WAVES).reshape(along_y, share, part_wide).transpose(1, 0, 2).reshape(-1)
+    cos_y = cos_y[order_k].reshape(share, -1, along_y, cols)
+    sin_y = sin_y[order_k].reshape(share, -1, along_y, cols)
+    with_cos = jnp.einsum("gbirc,skbc->sigrk", got, cos_y, precision=highest)
+    with_sin = jnp.einsum("gbirc,skbc->sigrk", got, sin_y, precision=highest)
+    partial = jnp.stack([with_cos[:, 0] + with_sin[:, 1], with_cos[:, 1] - with_sin[:, 0]], axis=1)
+
+    pieces = []
+    for by in range(share):
+        piece = lax.dynamic_index_in_dim(partial, place ^ by, 0, keepdims=False)
+        pieces.append(piece if by == 0 else swapped(piece, by))
+    partial = jnp.stack([lax.dynamic_index_in_dim(jnp.stack(pieces), place ^ s, 0, keepdims=False) for s in range(share)])
+
+    cos_x, sin_x = wave_tables(WAVES, rows * along_x)
+    cos_x = cos_x.reshape(WAVES, along_x, share, part_rows)
+    sin_x = sin_x.reshape(WAVES, along_x, share, part_rows)
+    with_cos = jnp.einsum("jgsr,sigrk->ijk", cos_x, partial, precision=highest)
+    with_sin = jnp.einsum("jgsr,sigrk->ijk", sin_x, partial, precision=highest)
+    far = jnp.stack([with_cos[0] + with_sin[1], with_cos[1] - with_sin[0]])
+    far = far * (1.0 / math.sqrt(rows * along_x * cols * along_y))
+
+    far = far.reshape(2, along_x, tall, along_y, part_wide).transpose(1, 3, 0, 2, 4)
+    far = far.reshape(devices, 2, tall, part_wide)
+    far = lax.all_to_all(far, BOTH, split_axis=0, concat_axis=0, tiled=True)
+    far = far.reshape(comps, freqs, share, 2, tall, part_wide).transpose(3, 0, 1, 4, 2, 5)
+    return far.reshape(2, comps, freqs, tall, wide)
 
 
 def per_device(electric, magnetic, retention, coupling, spectrum_real, spectrum_imag, phases):
@@ -104,19 +134,7 @@
     )
     next_real = spectrum_real + tangent[:, None] * jnp.cos(phases)[None, :, None, None]
     next_imag = spectrum_imag - tangent[:, None] * jnp.sin(phases)[None, :, None, None]
-    local_rows = electric.shape[1]
-    local_cols = electric.shape[2]
-    scale = 1.0 / math.sqrt(local_rows * lax.axis_size("gx") * local_cols * lax.axis_size("gy"))
-    cos_y, sin_y = tables(WAVES, local_cols, lax.axis_index("gy") * local_cols)
-    part_real, part_imag = first_section(next_real, next_imag, cos_y, sin_y)
-    cos_full, sin_full = tables(WAVES, local_rows * lax.axis_size("gx"), 0)
-    reduced = lax.psum_scatter(
-        jnp.stack([part_real, part_imag]), "gy", scatter_dimension=4, tiled=True
-    )
-    columns = lax.all_to_all(reduced, "gx", split_axis=4, concat_axis=3, tiled=True)
-    finished = second_section(columns[0], columns[1], cos_full, sin_full)
-    whole = lax.all_to_all(finished, "gx", split_axis=3, concat_axis=4, tiled=True)
-    far_field = whole * scale
+    far_field = far_of(next_real, next_imag)
     return (next_electric, next_magnetic, next_real, next_imag, far_field)
 
 

time: 152 us -> 77 us (0.51)
  local copies, waits for them, and re-layouts: 52 us -> 14.8 us
  between operations: 14.6 us -> 1.12 us
  blocking collectives: 12.7 us -> 0 us
  waiting for transfers between devices: 33.3 us -> 23.4 us
  starting transfers between devices: 15.3 us -> 21.8 us
  other arithmetic: 16.4 us -> 12.3 us
  matrix products: 6.97 us -> 3.05 us
    unnamed x47 -> x28, local copies, waits for them, and re-layouts: 30.3 us -> 1.57 us
    unnamed x2 -> x0, waiting for transfers between devices: 24.4 us -> none
    all_to_all x1 -> x0, blocking collectives: 12.7 us -> none  [per_device(): lax.all_to_all(reduced, 'gx', split_axis=4, concat_axis=3, tiled=True)]
    all_to_all x1 -> x2, waiting for transfers between devices: 6 us -> 17.8 us  [the longest x1 10.6 us: far_of(): got = lax.all_to_all(both, BOTH, split_axis=0, concat_axis=0, tiled=True)]
    all_to_all x1 -> x2, starting transfers between devices: 3.67 us -> 10.5 us  [the longest x1 7.71 us: far_of(): got = lax.all_to_all(both, BOTH, split_axis=0, concat_axis=0, tiled=True)]
    slice x3, local copies, waits for them, and re-layouts: 6.34 us -> 2.33 us  [ahead_diff(): upper = lax.slice_in_dim(values, 1, values.shape[along], axis=along)]
    dot_general x8 -> x4, matrix products: 6.97 us -> 3.05 us  [the longest x1 1.32 us: far_of(): with_cos = jnp.einsum('jgsr,sigrk->ijk', cos_x, partial, precision=highest)]
    mul x1, other arithmetic: 5.21 us -> 1.35 us  [far_of(): far = far * (1.0 / math.sqrt(rows * along_x * cols * along_y))]
  transfers between devices with their start and end apart: 6 -> 7, of which waited for: 3 -> 5; matrix products, arithmetic and copies ran while one was open for 8% -> 10% of each run, Pallas kernels for 0% -> 0%
where the time goes in v1:
time: 77 us; the launch traced here: 76.5 us
  waiting for transfers between devices  23.4 us (30%)
  starting transfers between devices  21.8 us (28%)
  local copies, waits for them, and re-layouts  14.8 us (19%)
  other arithmetic  12.3 us (16%)
  matrix products  3.05 us (4%)
  between operations  1.12 us (1%)
    ppermute x4, starting transfers between devices, passed_along(): return lax.ppermute(value, axis, pairs)  11.3 us
    all_to_all x1, waiting for transfers between devices, far_of(): got = lax.all_to_all(both, BOTH, split_axis=0, concat_axis=0, tiled=True)  10.6 us
    all_to_all x1, starting transfers between devices, far_of(): got = lax.all_to_all(both, BOTH, split_axis=0, concat_axis=0, tiled=True)  7.71 us
    all_to_all x1, waiting for transfers between devices, far_of(): far = lax.all_to_all(far, BOTH, split_axis=0, concat_axis=0, tiled=True)  7.26 us
    ppermute x4, waiting for transfers between devices, passed_along(): return lax.ppermute(value, axis, pairs)  4.3 us
    another operation x1, other arithmetic, per_device(): next_electric = jnp.stack([new_x, new_y, new_z])  3.13 us
    all_to_all x1, starting transfers between devices, far_of(): far = lax.all_to_all(far, BOTH, split_axis=0, concat_axis=0, tiled=True)  2.77 us
    add x1, other arithmetic, per_device(): retention * elec_x  2.67 us
  transfers between devices with their start and end apart: 7, of which 5 were waited for; matrix products, arithmetic and copies ran while one was open for 10% of the time, Pallas kernels for 0%

profile of v1, /device:TPU:0, one launch (start us, length us, event | category | flops | bytes accessed | tf_op | source)
XLA Modules:
  0.0 76.5 jit_solution(16842822667598897966)
XLA Ops:
  0.6 0.9 %slice.139 = f32[2,1,128,128]{3,2,1,0:T(8,128)S(1)} slice(f32[3,16,128,128]{3,2,1,0:T(8,128)} %param.11), slice={[1:3], [0:1], [0:128], [0:128]} | slice | bytes 262144 | tf_op jit(solution)/shard_map/slice | solution.py:103
  1.6 1.3 %collective-permute-start = (f32[2,1,128,128]{3,2,1,0:T(8,128)S(1)}, f32[2,1,128,128]{3,2,1,0:T(8,128)S(1)}, u32[]{:S(2)}, u32[]{:S(2)}) collective-permute-start(f32[2,1,128,128]{3,2,1,0:T(8,128)S(1)} %slice.139), channel_id=1, source_target_pairs={{4,0},{8,4},{12,8},{16,12},{20,16},{24,20},{28,24},{5,1},{9,5},{13... | collective-permute-start | bytes 393224 | tf_op jit(solution)/shard_map/ppermute | solution.py:20
  2.9 0.9 %slice.143 = f32[2,16,1,128]{3,2,1,0:T(1,128)S(1)} slice(f32[3,16,128,128]{3,2,1,0:T(8,128)} %param.11), slice={[0:3:2], [0:16:1], [0:1:1], [0:128:1]} | slice | bytes 32768 | tf_op jit(solution)/shard_map/slice | solution.py:104
  3.8 1.3 %collective-permute-start.1 = (f32[2,16,1,128]{3,1,2,0:T(8,128)S(1)}, f32[2,16,1,128]{3,1,2,0:T(8,128)S(1)}, u32[]{:S(2)}, u32[]{:S(2)}) collective-permute-start(f32[2,16,1,128]{3,1,2,0:T(8,128)S(1)} %bitcast.153), channel_id=1, source_target_pairs={{1,0},{2,1},{3,2},{5,4},{6,5},{7,6},{9,8},{10,9},{11,10},{13,12},{... | collective-permute-start | bytes 49160 | tf_op jit(solution)/shard_map/ppermute | solution.py:20
  5.1 1.3 %slice_bitcast_fusion.2 = f32[16,128,128]{2,1,0:T(8,128)S(1)} fusion(f32[3,16,128,128]{3,2,1,0:T(8,128)} %param.11), kind=kLoop, calls=%fused_computation.53 | loop fusion | bytes 2097152 | tf_op jit(solution)/shard_map/squeeze | solution.py:102
  6.4 0.0 copy-start.12
  6.4 0.0 copy-start
  6.4 0.0 copy-start.1
  6.4 2.0 %slice_bitcast_fusion.10 = (f32[15,128,128]{2,1,0:T(8,128)S(1)}, f32[1,15,128,128]{3,2,1,0:T(8,128)S(1)}, f32[15,128,128]{2,1,0:T(8,128)S(1)}) fusion(f32[3,16,128,128]{3,2,1,0:T(8,128)} %param.11), kind=kLoop, calls=%fused_computation.88 | loop fusion | bytes 4915200 | tf_op jit(solution)/shard_map/slice | solution.py:34
  8.4 0.2 fusion.35
  8.7 0.0 copy-done.12
  8.7 0.0 collective-permute-done.1
  8.8 1.2 %collective-permute-done = f32[2,1,128,128]{3,2,1,0:T(8,128)S(1)} collective-permute-done((f32[2,1,128,128]{3,2,1,0:T(8,128)S(1)}, f32[2,1,128,128]{3,2,1,0:T(8,128)S(1)}, u32[]{:S(2)}, u32[]{:S(2)}) %collective-permute-start) | collective-permute-done | bytes 131104 | tf_op jit(solution)/shard_map/ppermute | solution.py:20
  10.0 0.0 copy-done
  10.0 0.0 copy-done.1
  10.0 0.8 slice_bitcast_fusion
  10.7 0.1 slice.182
  10.9 1.8 %fusion.18 = (f32[16,128,128]{2,1,0:T(8,128)S(1)}, f32[16,128,128]{2,1,0:T(8,128)S(1)}, f32[16,128,128]{2,1,0:T(8,128)S(1)}) fusion(f32[1,128,128]{2,1,0:T(8,128)S(1)} %get-tuple-element.39, f32[15,128,128]{2,1,0:T(8,128)S(1)} %get-tuple-element.21, f32[16,1,128]{2,1,0:T(1,128)S(1)} %bitcast.146, f32[16,127,128]{2,1,0:T(8,128)S(1)} %get-tuple-element.27, ...), kind=kLoop, calls=%fused_computation.33 | loop fusion | flops 4980736 | bytes 15728640 | tf_op jit(solution)/shard_map/sub | solution.py:111
  12.7 1.2 %slice_reduce_fusion = (f32[16,128]{1,0:T(8,128)S(1)}, f32[16,128]{1,0:T(8,128)S(1)}) fusion(f32[16,128,128]{2,1,0:T(8,128)S(1)} %get-tuple-element.19, f32[16,128,128]{2,1,0:T(8,128)S(1)} %get-tuple-element.20), kind=kLoop, calls=%fused_computation.26 | loop fusion | bytes 32768 | tf_op jit(solution)/shard_map/slice | solution.py:132
  13.9 0.3 pad_maximum_fusion
  14.2 0.0 copy-start.2
  14.3 0.0 copy-start.3
  14.3 0.0 copy-start.4
  14.3 3.2 %collective-permute-start.2 = (f32[2,16,1,128]{3,2,1,0:T(1,128)S(1)}, f32[2,16,1,128]{3,2,1,0:T(1,128)S(1)}, u32[]{:S(2)}, u32[]{:S(2)}) collective-permute-start(f32[2,16,1,128]{3,2,1,0:T(1,128)S(1)} %slice.155), channel_id=1, source_target_pairs={{0,1},{1,2},{2,3},{4,5},{5,6},{6,7},{8,9},{9,10},{10,11},{12,13},{... | collective-permute-start | bytes 49160 | tf_op jit(solution)/shard_map/ppermute | solution.py:20
  17.5 0.0 copy-done.2
  17.5 0.1 slice.190
  17.6 5.5 %collective-permute-start.3 = (f32[2,1,128,128]{3,2,1,0:T(8,128)S(1)}, f32[2,1,128,128]{3,2,1,0:T(8,128)S(1)}, u32[]{:S(2)}, u32[]{:S(2)}) collective-permute-start(f32[2,1,128,128]{3,2,1,0:T(8,128)S(1)} %pad_maximum_fusion.3), channel_id=1, source_target_pairs={{0,4},{4,8},{8,12},{12,16},{16,20},{20,24},{24,28},{1,5},{5,9},{9,... | collective-permute-start | bytes 393224 | tf_op jit(solution)/shard_map/ppermute | solution.py:20
  23.1 0.1 slice.188
  23.2 0.0 collective-permute-done.2
  23.2 3.1 %collective-permute-done.3 = f32[2,1,128,128]{3,2,1,0:T(8,128)S(1)} collective-permute-done((f32[2,1,128,128]{3,2,1,0:T(8,128)S(1)}, f32[2,1,128,128]{3,2,1,0:T(8,128)S(1)}, u32[]{:S(2)}, u32[]{:S(2)}) %collective-permute-start.3) | collective-permute-done | bytes 131104 | tf_op jit(solution)/shard_map/ppermute | solution.py:20
  26.4 0.0 copy-done.3
  26.4 0.0 copy-done.4
  26.4 0.0 copy-start.9
  26.4 0.0 copy-start.10
  26.4 2.7 %fusion.11 = (f32[16,128,128]{2,1,0:T(8,128)S(1)}, f32[1,16,128,128]{3,2,1,0:T(8,128)}, f32[16,128,128]{2,1,0:T(8,128)S(1)}) fusion(f32[16,128,128]{2,1,0:T(8,128)S(1)} %copy-done.3, f32[16,128,128]{2,1,0:T(8,128)S(1)} %get-tuple-element.19, f32[16,128,128]{2,1,0:T(8,128)S(1)} %get-tuple-element.18, f32[16,127,128]{2,1,0:T(8,128)S(1)} %bitcast.136, ...), kind=kLoop, calls=%fused_computation.21 | loop fusion | flops 5767168 | bytes 15728640 | tf_op jit(solution)/shard_map/add | solution.py:117
  29.1 1.2 %slice_reduce_fusion.2 = (f32[16,128]{1,0:T(8,128)S(1)}, f32[16,128]{1,0:T(8,128)S(1)}) fusion(f32[16,128,128]{2,1,0:T(8,128)S(1)} %get-tuple-element.17, f32[16,128,128]{2,1,0:T(8,128)S(1)} %get-tuple-element.15), kind=kLoop, calls=%fused_computation.28 | loop fusion | bytes 32768 | tf_op jit(solution)/shard_map/slice | solution.py:130
  30.3 0.0 copy-done.9
  30.3 0.1 multiply_subtract_fusion
  30.4 0.0 copy-start.8
  30.4 0.0 copy-start.7
  30.4 0.8 %pad_maximum_fusion.2 = f32[2,16,2,8,128]{4,3,0,2,1:T(8,128)} fusion(f32[1,16,2,8,128]{4,3,0,2,1:T(8,128)S(1)} %bitcast.143, f32[1,16,2,8,128]{4,3,0,2,1:T(8,128)S(1)} %bitcast.144), kind=kLoop, calls=%fused_computation.55 | loop fusion | flops 65536 | bytes 524288 | tf_op jit(solution)/shard_map/stack | solution.py:67
  31.2 7.7 %all-to-all-start = ((f32[32,2,8,128]{3,2,1,0:T(8,128)}), f32[32,2,8,128]{3,2,1,0:T(8,128)S(1)}, u32[]{:S(2)}, u32[]{:S(2)}) async-start(f32[32,2,8,128]{3,2,1,0:T(8,128)} %bitcast.32), calls=%async_computation | async-start | bytes 524288 | tf_op jit(solution)/shard_map/all_to_all | solution.py:69
  38.9 10.6 %all-to-all-done = f32[32,2,8,128]{3,2,1,0:T(8,128)S(1)} async-done(((f32[32,2,8,128]{3,2,1,0:T(8,128)}), f32[32,2,8,128]{3,2,1,0:T(8,128)S(1)}, u32[]{:S(2)}, u32[]{:S(2)}) %all-to-all-start) | async-done | bytes 262176 | tf_op jit(solution)/shard_map/all_to_all | solution.py:69
  49.5 0.7 convolution_bitcast_fusion.2
  50.2 0.0 copy-done.5
  50.2 0.7 convolution_bitcast_fusion.3
  50.9 0.1 collective-permute-start.4
  51.0 1.2 %collective-permute-done.4 = f32[2,8,8,128]{3,2,0,1:T(8,128)S(1)} collective-permute-done((f32[2,8,8,128]{3,2,0,1:T(8,128)S(1)}, f32[2,8,8,128]{3,2,0,1:T(8,128)S(1)}, u32[]{:S(2)}, u32[]{:S(2)}) %collective-permute-start.4) | collective-permute-done | bytes 65568 | tf_op jit(solution)/shard_map/ppermute | solution.py:51
  52.2 1.3 %convolution_bitcast_fusion.1 = f32[2,256,128]{1,2,0:T(8,128)S(1)} fusion(f32[256,8,2,8,1]{0,3,2,4,1:T(8,128)} %constant.64, f32[1,2,8,8,128]{4,3,0,1,2:T(8,128)S(1)} %get-tuple-element.34, f32[1,2,8,8,128]{4,3,0,1,2:T(8,128)S(1)} %get-tuple-element.33), kind=kOutput, calls=%fused_computation.7 | convolution fusion | flops 100696064 | bytes 524288 | tf_op jit(solution)/shard_map/jgsr,sigrk->ijk/dot_general | solution.py:89
  53.6 0.4 convolution_bitcast_fusion
  54.0 0.2 stack.81
  54.2 1.0 %copy.194 = f32[1,8,32,4,32]{4,2,0,3,1:T(8,128)} copy(f32[1,8,32,4,32]{2,1,4,3,0:T(8,128)S(1)} %stack.81) | data formatting | bytes 262144 | tf_op jit(solution)/shard_map/stack | solution.py:91
  55.2 0.2 stack.82
  55.4 1.0 %copy.195 = f32[1,8,32,4,32]{4,2,0,3,1:T(8,128)} copy(f32[1,8,32,4,32]{2,1,4,3,0:T(8,128)S(1)} %stack.82) | data formatting | bytes 262144 | tf_op jit(solution)/shard_map/stack | solution.py:91
  56.4 1.4 %maximum_multiply_fusion = f32[2,8,32,4,32]{4,2,0,3,1:T(8,128)S(1)} fusion(f32[1,8,32,4,32]{4,2,0,3,1:T(8,128)} %copy.195, f32[1,8,32,4,32]{4,2,0,3,1:T(8,128)} %copy.194), kind=kLoop, calls=%fused_computation.50 | loop fusion | flops 131072 | bytes 524288 | tf_op jit(solution)/shard_map/mul | solution.py:92
  57.8 1.2 %reshape.64 = f32[32,1,2048]{2,1,0:T(1,128)} reshape(f32[32,2,32,32]{3,2,1,0:T(8,128)S(1)} %bitcast.139) | data formatting | bytes 524288
  58.9 2.8 %all-to-all-start.1 = ((f32[32,1,2048]{2,1,0:T(1,128)}), f32[32,1,2048]{2,1,0:T(1,128)S(1)}, u32[]{:S(2)}, u32[]{:S(2)}) async-start(f32[32,1,2048]{2,1,0:T(1,128)} %reshape.64), calls=%async_computation.1 | async-start | bytes 524288 | tf_op jit(solution)/shard_map/all_to_all | solution.py:96
  61.7 3.1 %pad_maximum_fusion.1 = f32[3,16,128,128]{3,2,1,0:T(8,128)} fusion(f32[1,16,128,128]{3,2,1,0:T(8,128)} %get-tuple-element.16, f32[1,16,128,128]{3,2,1,0:T(8,128)S(1)} %bitcast.138, f32[1,16,128,128]{3,2,1,0:T(8,128)S(1)} %bitcast.137), kind=kLoop, calls=%fused_computation.1 | loop fusion | flops 1572864 | bytes 6291456 | tf_op jit(solution)/shard_map/stack | solution.py:126
  64.9 7.3 %all-to-all-done.1 = f32[32,1,2048]{2,1,0:T(1,128)S(1)} async-done(((f32[32,1,2048]{2,1,0:T(1,128)}), f32[32,1,2048]{2,1,0:T(1,128)S(1)}, u32[]{:S(2)}, u32[]{:S(2)}) %all-to-all-start.1) | async-done | bytes 262176 | tf_op jit(solution)/shard_map/all_to_all | solution.py:96
  72.1 0.5 broadcast.29
  72.6 1.3 %reduce.8 = f32[32,2048]{1,0:T(8,128)S(1)} reduce(f32[32,1,2048]{2,1,0:T(1,128)S(1)} %all-to-all-done.1, f32[]{:T(128)} %broadcast.29), dimensions={1}, to_apply=%all_to_all.7.reduce_sub_computation | reduce | bytes 524292 | tf_op jit(solution)/shard_map/all_to_all | solution.py:96
  73.9 0.3 reshape.65
  74.2 0.8 %copy.196 = f32[2,4,4,32,2,32]{5,4,3,2,1,0:T(2,128)S(1)} copy(f32[2,4,4,32,2,32]{5,3,0,4,2,1:T(8,128)S(1)} %bitcast.140) | data formatting | bytes 524288 | tf_op jit(solution)/shard_map/transpose | solution.py:97
  75.1 1.4 %reshape.49 = f32[2,4,4,32,64]{4,3,2,1,0:T(8,128)} reshape(f32[2,4,4,32,2,32]{5,4,3,2,1,0:T(2,128)S(1)} %copy.196) | data formatting | bytes 524288 | tf_op jit(solution)/shard_map/reshape | solution.py:98
  (20 shorter events, 0.2 us)
Async XLA Ops:
  1.6 8.4 %collective-permute-start = (f32[2,1,128,128]{3,2,1,0:T(8,128)S(1)}, f32[2,1,128,128]{3,2,1,0:T(8,128)S(1)}, u32[]{:S(2)}, u32[]{:S(2)}) collective-permute-start(f32[2,1,128,128]{3,2,1,0:T(8,128)S(1)} %slice.139), channel_id=1, source_target_pairs={{4,0},{8,4},{12,8},{16,12},{20,16},{24,20},{28,24},{5,1},{9,5},{13... | collective-permute-start | bytes 393224 | tf_op jit(solution)/shard_map/ppermute | solution.py:20
  3.8 5.0 %collective-permute-start.1 = (f32[2,16,1,128]{3,1,2,0:T(8,128)S(1)}, f32[2,16,1,128]{3,1,2,0:T(8,128)S(1)}, u32[]{:S(2)}, u32[]{:S(2)}) collective-permute-start(f32[2,16,1,128]{3,1,2,0:T(8,128)S(1)} %bitcast.153), channel_id=1, source_target_pairs={{1,0},{2,1},{3,2},{5,4},{6,5},{7,6},{9,8},{10,9},{11,10},{13,12},{... | collective-permute-start | bytes 49160 | tf_op jit(solution)/shard_map/ppermute | solution.py:20
  6.4 2.3 %copy-start.12 = (f32[4]{0:T(128)S(1)}, f32[4]{0:T(128)}, u32[]{:S(2)}) copy-start(f32[4]{0:T(128)} %param.17) | copy-start | bytes 52
  6.4 3.5 %copy-start = (f32[3,16,128,128]{3,2,1,0:T(8,128)S(1)}, f32[3,16,128,128]{3,2,1,0:T(8,128)}, u32[]{:S(2)}) copy-start(f32[3,16,128,128]{3,2,1,0:T(8,128)} %param.11) | copy-start | bytes 9437188
  6.4 3.5 %copy-start.1 = (f32[3,16,128,128]{3,2,1,0:T(8,128)S(1)}, f32[3,16,128,128]{3,2,1,0:T(8,128)}, u32[]{:S(2)}) copy-start(f32[3,16,128,128]{3,2,1,0:T(8,128)} %param.12) | copy-start | bytes 9437188
  14.2 3.2 %copy-start.2 = (f32[3,16,128,128]{3,2,1,0:T(8,128)}, f32[3,16,128,128]{3,2,1,0:T(8,128)S(1)}, u32[]{:S(2)}) copy-start(f32[3,16,128,128]{3,2,1,0:T(8,128)S(1)} %pad_maximum_fusion) | copy-start | bytes 9437188
  14.3 12.1 %copy-start.3 = (f32[16,128,128]{2,1,0:T(8,128)S(1)}, f32[16,128,128]{2,1,0:T(8,128)}, u32[]{:S(2)}) copy-start(f32[16,128,128]{2,1,0:T(8,128)} %param.14) | copy-start | bytes 3145732
  14.3 12.1 %copy-start.4 = (f32[16,128,128]{2,1,0:T(8,128)S(1)}, f32[16,128,128]{2,1,0:T(8,128)}, u32[]{:S(2)}) copy-start(f32[16,128,128]{2,1,0:T(8,128)} %param.13) | copy-start | bytes 3145732
  14.3 8.9 %collective-permute-start.2 = (f32[2,16,1,128]{3,2,1,0:T(1,128)S(1)}, f32[2,16,1,128]{3,2,1,0:T(1,128)S(1)}, u32[]{:S(2)}, u32[]{:S(2)}) collective-permute-start(f32[2,16,1,128]{3,2,1,0:T(1,128)S(1)} %slice.155), channel_id=1, source_target_pairs={{0,1},{1,2},{2,3},{4,5},{5,6},{6,7},{8,9},{9,10},{10,11},{12,13},{... | collective-permute-start | bytes 49160 | tf_op jit(solution)/shard_map/ppermute | solution.py:20
  17.6 8.8 %collective-permute-start.3 = (f32[2,1,128,128]{3,2,1,0:T(8,128)S(1)}, f32[2,1,128,128]{3,2,1,0:T(8,128)S(1)}, u32[]{:S(2)}, u32[]{:S(2)}) collective-permute-start(f32[2,1,128,128]{3,2,1,0:T(8,128)S(1)} %pad_maximum_fusion.3), channel_id=1, source_target_pairs={{0,4},{4,8},{8,12},{12,16},{16,20},{20,24},{24,28},{1,5},{5,9},{9,... | collective-permute-start | bytes 393224 | tf_op jit(solution)/shard_map/ppermute | solution.py:20
  26.4 3.9 %copy-start.9 = (f32[4,4,16,128]{3,2,1,0:T(8,128)S(1)}, f32[4,4,16,128]{3,2,1,0:T(8,128)}, u32[]{:S(2)}) copy-start(f32[4,4,16,128]{3,2,1,0:T(8,128)} %param.16) | copy-start | bytes 393220
  26.4 3.9 %copy-start.10 = (f32[4,4,16,128]{3,2,1,0:T(8,128)S(1)}, f32[4,4,16,128]{3,2,1,0:T(8,128)}, u32[]{:S(2)}) copy-start(f32[4,4,16,128]{3,2,1,0:T(8,128)} %param.15) | copy-start | bytes 393220
  29.1 20.4 %copy-start.6 = (f32[2,128,4,128,1,1]{3,1,2,0,5,4:T(8,128)S(1)}, f32[2,128,4,128,1,1]{3,1,2,0,5,4:T(8,128)}, u32[]{:S(2)}) copy-start(f32[2,128,4,128,1,1]{3,1,2,0,5,4:T(8,128)} %constant.63) | copy-start | bytes 1572868
  29.1 21.1 %copy-start.5 = (f32[2,128,4,128,1,1]{3,1,2,0,5,4:T(8,128)S(1)}, f32[2,128,4,128,1,1]{3,1,2,0,5,4:T(8,128)}, u32[]{:S(2)}) copy-start(f32[2,128,4,128,1,1]{3,1,2,0,5,4:T(8,128)} %constant.62) | copy-start | bytes 1572868
  30.4 0.8 %copy-start.8 = (f32[4,4,16,128]{3,2,1,0:T(8,128)}, f32[4,4,16,128]{3,2,1,0:T(8,128)S(1)}, u32[]{:S(2)}) copy-start(f32[4,4,16,128]{3,2,1,0:T(8,128)S(1)} %get-tuple-element.43) | copy-start | bytes 393220
  30.4 23.8 %copy-start.7 = (f32[4,4,16,128]{3,2,1,0:T(8,128)}, f32[4,4,16,128]{3,2,1,0:T(8,128)S(1)}, u32[]{:S(2)}) copy-start(f32[4,4,16,128]{3,2,1,0:T(8,128)S(1)} %get-tuple-element.42) | copy-start | bytes 393220
  31.2 18.3 %all-to-all-start = ((f32[32,2,8,128]{3,2,1,0:T(8,128)}), f32[32,2,8,128]{3,2,1,0:T(8,128)S(1)}, u32[]{:S(2)}, u32[]{:S(2)}) async-start(f32[32,2,8,128]{3,2,1,0:T(8,128)} %bitcast.32), calls=%async_computation | async-start | bytes 524288 | tf_op jit(solution)/shard_map/all_to_all | solution.py:69
  49.5 4.1 %copy-start.11 = (f32[256,8,2,8,1]{0,3,2,4,1:T(8,128)S(1)}, f32[256,8,2,8,1]{0,3,2,4,1:T(8,128)}, u32[]{:S(2)}) copy-start(f32[256,8,2,8,1]{0,3,2,4,1:T(8,128)} %constant.65) | copy-start | bytes 393220
  50.9 1.3 %collective-permute-start.4 = (f32[2,8,8,128]{3,2,0,1:T(8,128)S(1)}, f32[2,8,8,128]{3,2,0,1:T(8,128)S(1)}, u32[]{:S(2)}, u32[]{:S(2)}) collective-permute-start(f32[2,8,8,128]{3,2,0,1:T(8,128)S(1)} %get-tuple-element.35), channel_id=1, source_target_pairs={{0,1},{1,0},{2,3},{3,2},{4,5},{5,4},{6,7},{7,6},{8,9},{9,8},{10,11... | collective-permute-start | bytes 196616 | tf_op jit(solution)/shard_map/ppermute | solution.py:51
  58.9 13.2 %all-to-all-start.1 = ((f32[32,1,2048]{2,1,0:T(1,128)}), f32[32,1,2048]{2,1,0:T(1,128)S(1)}, u32[]{:S(2)}, u32[]{:S(2)}) async-start(f32[32,1,2048]{2,1,0:T(1,128)} %reshape.64), calls=%async_computation.1 | async-start | bytes 524288 | tf_op jit(solution)/shard_map/all_to_all | solution.py:96

commit v2 on v1

--- a/solution.py
+++ b/solution.py
@@ -4,12 +4,15 @@
 import jax.numpy as jnp
 import numpy as np
 from jax import lax
+from jax.experimental import pallas as pl
+from jax.experimental.pallas import tpu as pltpu
 from jax.sharding import PartitionSpec as P
 
 WAVES = 256
 TOP_PLANE = 111
 BOTH = ("gx", "gy")
-
+LANES = 128
+SUBLANES = 8
 
 curl_step = 0.5
 
@@ -20,6 +23,34 @@
     return lax.ppermute(value, axis, pairs)
 
 
+def passed_across(value, by_x, by_y):
+    along_x, along_y = lax.axis_size("gx"), lax.axis_size("gy")
+    pairs = [
+        (x * along_y + y, (x + by_x) * along_y + y + by_y)
+        for x in range(along_x)
+        for y in range(along_y)
+        if 0 <= x + by_x < along_x and 0 <= y + by_y < along_y
+    ]
+    return lax.ppermute(value, BOTH, pairs)
+
+
+def swapped(value, by):
+    devices = lax.axis_size(BOTH)
+    return lax.ppermute(value, BOTH, [(i, i ^ by) for i in range(devices)])
+
+
+def wave_tables(number, extent):
+    wave = 2 * np.arange(number) + 1 - number
+    angles = (wave[:, None] * np.arange(extent)[None, :] % (4 * number)) * (math.pi / (2 * number))
+    return np.cos(angles), np.sin(angles)
+
+
+def in_two(table):
+    high = table.astype(np.float32).astype(jnp.bfloat16)
+    low = (table - high.astype(np.float64)).astype(np.float32).astype(jnp.bfloat16)
+    return jnp.asarray(high), jnp.asarray(low)
+
+
 def forward_diff(values, along):
     padded = jnp.pad(values, [(0, 1) if which == along else (0, 0) for which in range(values.ndim)])
     return lax.slice_in_dim(padded, 1, values.shape[along] + 1, axis=along) - values
@@ -38,17 +69,6 @@
 def behind_diff(values, border, along):
     lower = lax.slice_in_dim(values, 0, values.shape[along] - 1, axis=along)
     return values - jnp.concatenate([border, lower], axis=along)
-
-
-def wave_tables(number, extent):
-    wave = 2 * np.arange(number) + 1 - number
-    angles = (wave[:, None] * np.arange(extent)[None, :] % (4 * number)) * (math.pi / (2 * number))
-    return np.cos(angles).astype(np.float32), np.sin(angles).astype(np.float32)
-
-
-def swapped(value, by):
-    devices = lax.axis_size(BOTH)
-    return lax.ppermute(value, BOTH, [(i, i ^ by) for i in range(devices)])
 
 
 def far_of(next_real, next_imag):
@@ -69,7 +89,7 @@
     got = lax.all_to_all(both, BOTH, split_axis=0, concat_axis=0, tiled=True)
     got = got.reshape(along_x, along_y, 2, part_rows, cols)
 
-    cos_y, sin_y = wave_tables(WAVES, cols * along_y)
+    cos_y, sin_y = (table.astype(np.float32) for table in wave_tables(WAVES, cols * along_y))
     order_k = np.arange(WAVES).reshape(along_y, share, part_wide).transpose(1, 0, 2).reshape(-1)
     cos_y = cos_y[order_k].reshape(share, -1, along_y, cols)
     sin_y = sin_y[order_k].reshape(share, -1, along_y, cols)
@@ -81,9 +101,12 @@
     for by in range(share):
         piece = lax.dynamic_index_in_dim(partial, place ^ by, 0, keepdims=False)
         pieces.append(piece if by == 0 else swapped(piece, by))
-    partial = jnp.stack([lax.dynamic_index_in_dim(jnp.stack(pieces), place ^ s, 0, keepdims=False) for s in range(share)])
-
-    cos_x, sin_x = wave_tables(WAVES, rows * along_x)
+    pieces = jnp.stack(pieces)
+    partial = jnp.stack(
+        [lax.dynamic_index_in_dim(pieces, place ^ s, 0, keepdims=False) for s in range(share)]
+    )
+
+    cos_x, sin_x = (table.astype(np.float32) for table in wave_tables(WAVES, rows * along_x))
     cos_x = cos_x.reshape(WAVES, along_x, share, part_rows)
     sin_x = sin_x.reshape(WAVES, along_x, share, part_rows)
     with_cos = jnp.einsum("jgsr,sigrk->ijk", cos_x, partial, precision=highest)
@@ -98,7 +121,7 @@
     return far.reshape(2, comps, freqs, tall, wide)
 
 
-def per_device(electric, magnetic, retention, coupling, spectrum_real, spectrum_imag, phases):
+def general_step(electric, magnetic, retention, coupling, spectrum_real, spectrum_imag, phases):
     elec_x, elec_y, elec_z = (electric[0], electric[1], electric[2])
     rows_elec = passed_along(electric[1:3, 0:1], "gx", -1)
     cols_elec = passed_along(electric[0:3:2, :, 0:1], "gy", -1)
@@ -134,8 +157,462 @@
     )
     next_real = spectrum_real + tangent[:, None] * jnp.cos(phases)[None, :, None, None]
     next_imag = spectrum_imag - tangent[:, None] * jnp.sin(phases)[None, :, None, None]
-    far_field = far_of(next_real, next_imag)
+    return (next_electric, next_magnetic, next_real, next_imag, far_of(next_real, next_imag))
+
+
+def spot(shape, axis):
+    return lax.broadcasted_iota(jnp.int32, shape, axis)
+
+
+def moved(value, by, axis):
+    by = by % value.shape[axis]
+    return value if by == 0 else pltpu.roll(value, by, axis)
+
+
+def after(value, axis, border=0.0):
+    size = value.shape[axis]
+    return jnp.where(spot(value.shape, axis) == size - 1, border, moved(value, -1, axis))
+
+
+def before(value, axis, border=0.0):
+    return jnp.where(spot(value.shape, axis) == 0, border, moved(value, 1, axis))
+
+
+def whole_vmem():
+    return pl.BlockSpec(memory_space=pltpu.VMEM)
+
+
+def whole_smem():
+    return pl.BlockSpec(memory_space=pltpu.SMEM)
+
+
+PICKED = ((0, -1, 3), (1, -1, 3), (2, -1, 2), (3, -1, 2), (4, -1, 2), (5, 0, 1), (6, 0, 1), (7, 0, 1))
+
+
+def spread_kernel(
+    edge, cosine, sine, elec, magn, ret, coup, real, imag,
+    out, rows_elec, rows_magn, cols_elec, cols_magn, corner_up, corner_down, planes, edges,
+):
+    step = pl.program_id(0)
+    steps = pl.num_programs(0)
+    deep = elec.shape[1]
+    rows = planes.shape[0]
+    lane = spot((LANES, LANES), 1)
+    for at in range(deep):
+        arrays = [elec[0, at], elec[1, at], elec[2, at], magn[0, at], magn[1, at], magn[2, at], ret[at], coup[at]]
+        packed = None
+        start = 0
+        for which, first, count in PICKED:
+            turned = moved(arrays[which], start - TOP_PLANE - first, 1)
+            packed = turned if packed is None else jnp.where(lane < start, packed, turned)
+            start += count
+        planes[step * deep + at] = packed.T[0:16]
+        edges[0, pl.ds(step * deep + at, 1), :] = elec[0, at, -1:, :]
+        edges[1, pl.ds(step * deep + at, 1), :] = elec[1, at, -1:, :]
+        edges[2, pl.ds(step * deep + at, 1), :] = magn[2, at, -1:, :]
+        cols_elec[0, pl.ds(step * deep + at, 1), :] = elec[0, at, 0:1, :]
+        cols_elec[1, pl.ds(step * deep + at, 1), :] = elec[2, at, 0:1, :]
+        line = elec[1, at, -1:, :]
+        cols_magn[0, pl.ds(step * deep + at, 1), :] = (
+            magn[0, at, -1:, :] + curl_step * elec[2, at, -1:, :] + curl_step * (after(line, 1) - line)
+        )
+
+    @pl.when(step == 0)
+    def _():
+        rows_elec[0] = elec[1, 0]
+        rows_elec[1] = elec[2, 0]
+        corner_up[...] = jnp.broadcast_to(elec[1, 0, -1:, :], corner_up.shape)
+
+    @pl.when(step == steps - 1)
+    def _():
+        last = deep - 1
+        ex, ey, ez = elec[0, last], elec[1, last], elec[2, last]
+        rows_magn[0] = magn[1, last] - curl_step * (after(ex, 1) - ex) - curl_step * ez
+        rows_magn[1] = magn[2, last] + curl_step * ey + curl_step * (after(ex, 0) - ex)
+        corner_down[...] = jnp.broadcast_to(elec[0, last, 0:1, :], corner_down.shape)
+        end_x, end_y, end_z = edges[0], edges[1], edges[2]
+        cols_magn[1] = end_z - curl_step * (after(end_y, 0) - end_y) - curl_step * end_x
+
+        ex_m, ex_p, ex_q, ey_m, ey_p, ey_q, ez_m, ez_p, hx_m, hx_p, hy_m, hy_p, hz_p, keep, gain = (
+            planes[:, which, :] for which in range(15)
+        )
+        hx_p = hx_p - curl_step * ((after(ez_p, 1) - ez_p) - (ey_q - ey_p))
+        hx_m = hx_m - curl_step * ((after(ez_m, 1) - ez_m) - (ey_p - ey_m))
+        hy_p = hy_p - curl_step * ((ex_q - ex_p) - (after(ez_p, 0) - ez_p))
+        hy_m = hy_m - curl_step * ((ex_p - ex_m) - (after(ez_m, 0) - ez_m))
+        hz_p = hz_p - curl_step * ((after(ey_p, 0) - ey_p) - (after(ex_p, 1) - ex_p))
+        edge_x, edge_y = curl_step * edge[0], curl_step * edge[1]
+        tangent = (
+            keep * ex_p + gain * ((hz_p - before(hz_p, 1, edge_y * ex_p)) - (hy_p - hy_m)),
+            keep * ey_p + gain * ((hx_p - hx_m) - (hz_p - before(hz_p, 0, -edge_x * ey_p))),
+            hx_p,
+            hy_p,
+        )
+        ez_jump = curl_step * (ez_p - ez_m)
+        push = -curl_step * ey_p
+        none = jnp.zeros_like(ex_p)
+        one = jnp.ones_like(ex_p)
+        row_up = (push - before(push, 1) - ez_jump, -push, none, curl_step * ez_p)
+        row_down = (none, hz_p, none, none)
+        col_left = (
+            curl_step * ex_p,
+            -ez_jump - curl_step * ex_p + before(curl_step * ex_p, 0),
+            -curl_step * ez_p,
+            none,
+        )
+        col_right = (-hz_p, none, none, none)
+        wide = lax.broadcasted_iota(jnp.int32, (LANES, LANES), 1)
+        tall = lax.broadcasted_iota(jnp.int32, (SUBLANES, LANES), 0)
+        lanes = lax.broadcasted_iota(jnp.int32, (SUBLANES, LANES), 1)
+        pad = jnp.zeros((LANES - rows, LANES), jnp.float32)
+
+        def upright(lines):
+            block = None
+            for which, (value, column) in enumerate(lines):
+                value = moved(value, which - column, 1)
+                block = value if block is None else jnp.where(wide[0:rows] < which, block, value)
+            return jnp.concatenate([block, pad], axis=0).T[0:SUBLANES]
+
+        end = LANES - 1
+        for comp in range(4):
+            factor = gain if comp < 2 else one
+            upright_lines = upright(
+                [(none, 0), (none, 0), (none, 0), (none, 0), (col_left[comp], 0), (col_right[comp], end), (factor, end), (factor, 0)]
+            )
+            extra = jnp.where(tall >= 4, upright_lines, 0.0)
+            extra = jnp.where(tall == 0, row_up[comp][0:1], extra)
+            extra = jnp.where(tall == 1, row_down[comp][rows - 1 :], extra)
+            extra = jnp.where(tall == 2, factor[rows - 1 :], extra)
+            extra = jnp.where(tall == 3, factor[0:1], extra)
+            if comp == 0:
+                spare = moved(-push[0:1], rows - end, 1)
+                extra = jnp.where((tall == 5) & (lanes == rows), spare, extra)
+            if comp == 1:
+                spare = moved(curl_step * ex_p[rows - 1 :], rows, 1)
+                extra = jnp.where((tall == 4) & (lanes == rows), spare, extra)
+            freqs = real.shape[1]
+            for freq in range(freqs):
+                new_real = real[comp, freq] + tangent[comp] * cosine[freq]
+                new_imag = imag[comp, freq] - tangent[comp] * sine[freq]
+                for half in range(2):
+                    to = (comp * freqs + freq) * 2 + half
+                    out[to, 0:8] = new_real[half * 8 : half * 8 + 8]
+                    out[to, 8:16] = new_imag[half * 8 : half * 8 + 8]
+                    out[to, 16:24] = extra
+
+
+def spread(edge, electric, magnetic, retention, coupling, spectrum_real, spectrum_imag, cosine, sine):
+    _, rows, cols, deep = electric.shape
+    comps, freqs = spectrum_real.shape[:2]
+    slab = 4
+    vector = pl.BlockSpec((3, slab, cols, deep), lambda i: (0, i, 0, 0))
+    scalar = pl.BlockSpec((slab, cols, deep), lambda i: (i, 0, 0))
+    kind = jnp.float32
+    return pl.pallas_call(
+        spread_kernel,
+        grid=(rows // slab,),
+        in_specs=[whole_smem(), whole_smem(), whole_smem(), vector, vector, scalar, scalar, whole_vmem(), whole_vmem()],
+        out_specs=[whole_vmem()] * 7,
+        out_shape=[
+            jax.ShapeDtypeStruct((comps * freqs * 2, 24, cols), kind),
+            jax.ShapeDtypeStruct((2, cols, deep), kind),
+            jax.ShapeDtypeStruct((2, cols, deep), kind),
+            jax.ShapeDtypeStruct((2, rows, deep), kind),
+            jax.ShapeDtypeStruct((2, rows, deep), kind),
+            jax.ShapeDtypeStruct((SUBLANES, deep), kind),
+            jax.ShapeDtypeStruct((SUBLANES, deep), kind),
+        ],
+        scratch_shapes=[pltpu.VMEM((rows, 16, LANES), kind), pltpu.VMEM((3, rows, LANES), kind)],
+        name="spread",
+    )(edge, cosine, sine, electric, magnetic, retention, coupling, spectrum_real, spectrum_imag)
+
+
+def split_high(value):
+    high = value.astype(jnp.bfloat16)
+    return high, (value - high.astype(jnp.float32)).astype(jnp.bfloat16)
+
+
+def dot(a, b):
+    return jnp.dot(a, b, preferred_element_type=jnp.float32)
+
+
+def along_y_kernel(at, cosine, sine, got, high, low, mine, other, lines):
+    along_x, along_y = got.shape[0], got.shape[1]
+    blocks = along_x * along_y
+    half = at[0] % 2
+    freq = (at[0] // 2) % cosine.shape[0]
+    weight_real = cosine[freq]
+    weight_imag = -sine[freq]
+    is_last = jnp.where(half == 1, 1.0, 0.0)
+    is_first = jnp.where(half == 0, 1.0, 0.0)
+
+    def column(which):
+        return jnp.concatenate([got[x, :, 16 + which, :] for x in range(along_x)], axis=0)
+
+    block = spot((blocks, LANES), 0)
+    lane = spot((blocks, LANES), 1)
+    inner = block % along_y
+    rows = 16
+    from_right = jnp.where(inner == along_y - 1, 0.0, moved(column(4), -1, 0))
+    from_left = jnp.where(inner == 0, 0.0, moved(column(5), 1, 0))
+    right_up = jnp.where(block < along_y, 0.0, moved(from_right, along_y, 0))
+    left_down = jnp.where(block >= blocks - along_y, 0.0, moved(from_left, -along_y, 0))
+    from_right = from_right + jnp.where(lane == 0, moved(right_up, -rows, 1), 0.0)
+    from_left = from_left + jnp.where(lane == rows - 1, moved(left_down, -1, 1), 0.0)
+    last_col = column(6) * from_right
+    first_col = column(7) * from_left
+    pad = jnp.zeros((LANES - 2 * blocks, LANES), jnp.float32)
+    upright = jnp.concatenate([last_col, first_col, pad], axis=0).T
+    cols = jnp.where(half == 0, upright[0:8], upright[8:16])
+
+    low_row = spot((SUBLANES, LANES), 0)
+    low_lane = spot((SUBLANES, LANES), 1)
+    for x in range(along_x):
+        for y in range(along_y):
+            here = x * along_y + y
+            delta = jnp.where(low_lane == LANES - 1, moved(cols, LANES - 1 - here, 1), 0.0)
+            delta = delta + jnp.where(low_lane == 0, moved(cols, -blocks - here, 1), 0.0)
+            if x + 1 < along_x:
+                row = got[x, y, 18:19, :] * got[x + 1, y, 16:17, :] * is_last
+                delta = delta + jnp.where(low_row == SUBLANES - 1, row, 0.0)
+            if x > 0:
+                row = got[x, y, 19:20, :] * got[x - 1, y, 17:18, :] * is_first
+                delta = delta + jnp.where(low_row == 0, row, 0.0)
+            span = slice(y * LANES, (y + 1) * LANES)
+            lines[x * 16 : x * 16 + 8, span] = got[x, y, 0:8, :] + weight_real * delta
+            lines[x * 16 + 8 : x * 16 + 16, span] = got[x, y, 8:16, :] + weight_imag * delta
+
+    lines_high, lines_low = split_high(lines[...])
+    total = dot(lines_high, high[...]) + (dot(lines_low, high[...]) + dot(lines_high, low[...]))
+    waves = total.shape[1] // 2
+    piece = waves // 2
+    for x in range(along_x):
+        top = total[x * 16 : x * 16 + 8]
+        bottom = total[x * 16 + 8 : x * 16 + 16]
+        new_real = top[:, :waves] + bottom[:, waves:]
+        new_imag = bottom[:, :waves] - top[:, waves:]
+        span = slice(x * 8, x * 8 + 8)
+        mine[span, :piece] = jnp.where(half == 0, new_real[:, :piece], new_real[:, piece:])
+        mine[span, piece:] = jnp.where(half == 0, new_imag[:, :piece], new_imag[:, piece:])
+        other[span, :piece] = jnp.where(half == 0, new_real[:, piece:], new_real[:, :piece])
+        other[span, piece:] = jnp.where(half == 0, new_imag[:, piece:], new_imag[:, :piece])
+
+
+def along_y_sums(place, cosine, sine, got, cols, along_x, along_y):
+    wide = WAVES // along_y
+    order = np.arange(WAVES).reshape(along_y, 2, wide // 2).transpose(1, 0, 2).reshape(-1)
+    cos_y, sin_y = wave_tables(WAVES, cols * along_y)
+    high, low = in_two(np.concatenate([cos_y[order].T, sin_y[order].T], axis=1))
+    shape = jax.ShapeDtypeStruct((along_x * 8, WAVES), jnp.float32)
+    return pl.pallas_call(
+        along_y_kernel,
+        in_specs=[whole_smem()] * 3 + [whole_vmem()] * 3,
+        out_specs=[whole_vmem()] * 2,
+        out_shape=[shape, shape],
+        scratch_shapes=[pltpu.VMEM((along_x * 16, along_y * LANES), jnp.float32)],
+        name="along_y",
+    )(place, cosine, sine, got.reshape(along_x, along_y, 24, cols), high, low)
+
+
+def along_x_kernel(along_x, at, mine, other, high, low, out):
+    half = at[0] % 2
+    lines = jnp.concatenate(
+        [jnp.where(half == 0, mine[...], other[...]), jnp.where(half == 0, other[...], mine[...])], axis=0
+    )
+    lines_high, lines_low = split_high(lines)
+    total = dot(high[...], lines_high) + (dot(high[...], lines_low) + dot(low[...], lines_high))
+    waves = total.shape[0] // 2
+    piece = total.shape[1] // 2
+    far = (
+        total[:waves, :piece] + total[waves:, piece:],
+        total[:waves, piece:] - total[waves:, :piece],
+    )
+    tall = waves // along_x
+    stacks = tall // SUBLANES
+    along_y = out.shape[0] // along_x
+    wide = piece // along_y
+    lane = spot((SUBLANES, LANES), 1)
+    for x in range(along_x):
+        for part in range(2):
+            tiles = [far[part][x * tall + q * 8 : x * tall + q * 8 + 8] for q in range(stacks)]
+            for y in range(along_y):
+                block = None
+                for q in range(stacks):
+                    tile = moved(tiles[q], (q - y) * wide, 1)
+                    block = tile if block is None else jnp.where(lane < q * wide, block, tile)
+                out[x * along_y + y, part * 8 : part * 8 + 8] = block
+
+
+def along_x_sums(place, mine, other, rows, scale, along_x, devices):
+    cos_x, sin_x = wave_tables(WAVES, rows * along_x)
+    table = np.concatenate([cos_x, sin_x], axis=0) * scale
+    table = table.reshape(2 * WAVES, along_x, 2, 8).transpose(0, 2, 1, 3).reshape(2 * WAVES, rows * along_x)
+    high, low = in_two(table)
+    return pl.pallas_call(
+        lambda *refs: along_x_kernel(along_x, *refs),
+        in_specs=[whole_smem()] + [whole_vmem()] * 4,
+        out_specs=whole_vmem(),
+        out_shape=jax.ShapeDtypeStruct((devices, 16, LANES), jnp.float32),
+        name="along_x",
+    )(place, mine, other, high, low)
+
+
+def placed_kernel(got, out):
+    planes, tall, wide = out.shape[1:]
+    piece = wide // 2
+    lane = spot((SUBLANES, LANES), 1)
+    for plane in range(planes):
+        for part in range(2):
+            first = got[2 * plane, part * 8 : part * 8 + 8]
+            second = got[2 * plane + 1, part * 8 : part * 8 + 8]
+            for q in range(tall // SUBLANES):
+                tile = jnp.where(lane < piece, moved(first, -q * piece, 1), moved(second, piece - q * piece, 1))
+                out[part, plane, q * 8 : q * 8 + 8, :] = tile[:, :wide]
+
+
+def placed_far(got, comps, freqs, tall, wide):
+    far = pl.pallas_call(
+        placed_kernel,
+        in_specs=[whole_vmem()],
+        out_specs=whole_vmem(),
+        out_shape=jax.ShapeDtypeStruct((2, comps * freqs, tall, wide), jnp.float32),
+        name="placed",
+    )(got)
+    return far.reshape(2, comps, freqs, tall, wide)
+
+
+def yee_kernel(
+    edge, cosine, sine, elec, ahead, magn, ret, coup, rows_elec, rows_magn, cols_elec, cols_magn, corner_up, corner_down,
+    real, imag, new_elec, new_magn, new_real, new_imag, carried, tops,
+):
+    step = pl.program_id(0)
+    steps = pl.num_programs(0)
+    deep = elec.shape[1]
+    inner_x = edge[0]
+    inner_y = edge[1]
+    row = spot((LANES, LANES), 0)
+    lane = spot((LANES, LANES), 1)
+
+    @pl.when(step == 0)
+    def _():
+        spare = jnp.where(row == LANES - 1, curl_step * corner_down[0:1, :], 0.0)
+        carried[0] = (rows_magn[0] + curl_step * elec[2, 0]) * inner_x
+        carried[1] = (rows_magn[1] - curl_step * elec[1, 0] + spare) * inner_x
+
+    at_end = step == steps - 1
+    for at in range(deep):
+        here = pl.ds(step * deep + at, 1)
+        ex, ey, ez = elec[0, at], elec[1, at], elec[2, at]
+        if at + 1 < deep:
+            ey_next, ez_next = elec[1, at + 1], elec[2, at + 1]
+        else:
+            ey_next = jnp.where(at_end, rows_elec[0], ahead[1, 0])
+            ez_next = jnp.where(at_end, rows_elec[1], ahead[2, 0])
+        hx = magn[0, at] - curl_step * ((after(ez, 0, cols_elec[1, here, :]) - ez) - (after(ey, 1) - ey))
+        hy = magn[1, at] - curl_step * ((after(ex, 1) - ex) - (ez_next - ez))
+        hz = magn[2, at] - curl_step * ((ey_next - ey) - (after(ex, 0, cols_elec[0, here, :]) - ex))
+        new_magn[0, at] = hx
+        new_magn[1, at] = hy
+        new_magn[2, at] = hz
+        side_x = (cols_magn[0, here, :] - curl_step * ez[0:1]) * inner_y
+        side_z = cols_magn[1, here, :] + curl_step * ex[0:1]
+        if at + 1 == deep:
+            side_z = side_z - jnp.where(at_end, curl_step * corner_up[0:1, :], 0.0)
+        side_z = side_z * inner_y
+        keep, gain = ret[at], coup[at]
+        new_x = keep * ex + gain * ((hz - before(hz, 0, side_z)) - (hy - before(hy, 1)))
+        new_y = keep * ey + gain * ((hx - before(hx, 1)) - (hz - carried[1]))
+        new_z = keep * ez + gain * ((hy - carried[0]) - (hx - before(hx, 0, side_x)))
+        new_elec[0, at] = new_x
+        new_elec[1, at] = new_y
+        new_elec[2, at] = new_z
+        carried[0] = hy
+        carried[1] = hz
+        packed = None
+        for which, value in enumerate((new_x, new_y, hx, hy)):
+            turned = moved(value, which - TOP_PLANE, 1)
+            packed = turned if packed is None else jnp.where(lane < which, packed, turned)
+        tops[step * deep + at] = packed.T[0:SUBLANES]
+
+    @pl.when(at_end)
+    def _():
+        for comp in range(4):
+            tangent = tops[:, comp, :]
+            for freq in range(real.shape[1]):
+                new_real[comp, freq] = real[comp, freq] + tangent * cosine[freq]
+                new_imag[comp, freq] = imag[comp, freq] - tangent * sine[freq]
+
+
+def yee(edge, cosine, sine, electric, magnetic, retention, coupling, halos, spectrum_real, spectrum_imag):
+    _, rows, cols, deep = electric.shape
+    slab = 2
+    steps = rows // slab
+    vector = pl.BlockSpec((3, slab, cols, deep), lambda i: (0, i, 0, 0))
+    ahead = pl.BlockSpec((3, 1, cols, deep), lambda i: (0, jnp.minimum((i + 1) * slab, rows - 1), 0, 0))
+    scalar = pl.BlockSpec((slab, cols, deep), lambda i: (i, 0, 0))
+    kind = jnp.float32
+    return pl.pallas_call(
+        yee_kernel,
+        grid=(steps,),
+        in_specs=[whole_smem()] * 3 + [vector, ahead, vector, scalar, scalar] + [whole_vmem()] * 8,
+        out_specs=[vector, vector, whole_vmem(), whole_vmem()],
+        out_shape=[
+            jax.ShapeDtypeStruct(electric.shape, kind),
+            jax.ShapeDtypeStruct(magnetic.shape, kind),
+            jax.ShapeDtypeStruct(spectrum_real.shape, kind),
+            jax.ShapeDtypeStruct(spectrum_imag.shape, kind),
+        ],
+        scratch_shapes=[pltpu.VMEM((2, cols, deep), kind), pltpu.VMEM((rows, SUBLANES, LANES), kind)],
+        cost_estimate=pl.CostEstimate(flops=60 * electric.size, bytes_accessed=20 * electric.size, transcendentals=0),
+        name="yee",
+    )(edge, cosine, sine, electric, electric, magnetic, retention, coupling, *halos, spectrum_real, spectrum_imag)
+
+
+def tiled_step(electric, magnetic, retention, coupling, spectrum_real, spectrum_imag, phases):
+    comps, freqs, rows, cols = spectrum_real.shape
+    along_x, along_y = lax.axis_size("gx"), lax.axis_size("gy")
+    devices = along_x * along_y
+    cosine, sine = jnp.cos(phases), jnp.sin(phases)
+    place = lax.axis_index(BOTH).astype(jnp.int32).reshape(1)
+    edge = jnp.stack([lax.axis_index("gx") > 0, lax.axis_index("gy") > 0]).astype(jnp.float32)
+    sent, rows_elec, rows_magn, cols_elec, cols_magn, corner_up, corner_down = spread(
+        edge, electric, magnetic, retention, coupling, spectrum_real, spectrum_imag, cosine, sine
+    )
+    got = lax.all_to_all(sent, BOTH, split_axis=0, concat_axis=0, tiled=True)
+    halos = (
+        passed_along(rows_elec, "gx", -1),
+        passed_along(rows_magn, "gx", 1),
+        passed_along(cols_elec, "gy", -1),
+        passed_along(cols_magn, "gy", 1),
+        passed_across(corner_up, -1, 1),
+        passed_across(corner_down, 1, -1),
+    )
+    mine, other = along_y_sums(place, cosine, sine, got, cols, along_x, along_y)
+    other = swapped(other, 1)
+    scale = 1.0 / math.sqrt(rows * along_x * cols * along_y)
+    far = along_x_sums(place, mine, other, rows, scale, along_x, devices)
+    far = lax.all_to_all(far, BOTH, split_axis=0, concat_axis=0, tiled=True)
+    next_electric, next_magnetic, next_real, next_imag = yee(
+        edge, cosine, sine, electric, magnetic, retention, coupling, halos, spectrum_real, spectrum_imag
+    )
+    far_field = placed_far(far, comps, freqs, WAVES // along_x, WAVES // along_y)
     return (next_electric, next_magnetic, next_real, next_imag, far_field)
+
+
+def per_device(*arrays):
+    comps, freqs, rows, cols = arrays[4].shape
+    depth = arrays[0].shape[3]
+    along_x, along_y = lax.axis_size("gx"), lax.axis_size("gy")
+    wide, tall = WAVES // along_y, WAVES // along_x
+    fits = (
+        comps == 4
+        and along_x * along_y == 2 * comps * freqs
+        and (rows, cols, depth) == (2 * SUBLANES, LANES, LANES)
+        and WAVES == 2 * LANES
+        and (wide // 2) * (tall // SUBLANES) == LANES
+        and 0 < TOP_PLANE < depth - 1
+    )
+    return tiled_step(*arrays) if fits else general_step(*arrays)
 
 
 def solution(mesh):

time: 77 us -> 78.4 us (1.018)
  the two profiles are of different devices: /device:TPU:0 before, /device:TPU:5 now
where the time goes in v2:
time: 78.4 us; the launch traced here: 77.7 us
  starting transfers between devices  26.7 us (34%)
  Pallas kernels  24.3 us (31%)
  waiting for transfers between devices  20.6 us (26%)
  local copies, waits for them, and re-layouts  4.65 us (6%)
  between operations  0.88 us (1%)
    ppermute x4, starting transfers between devices, passed_along(): return lax.ppermute(value, axis, pairs)  12 us
    all_to_all x1, waiting for transfers between devices, tiled_step(): got = lax.all_to_all(sent, BOTH, split_axis=0, concat_axis=0, tiled=True)  11.7 us
    pallas_call x1, Pallas kernels, yee(): pl.pallas_call(yee_kernel, grid=(steps,), in_specs=[whole_smem()] * 3 + [...  10.6 us
    ppermute x2, waiting for transfers between devices, passed_across(): return lax.ppermute(value, BOTH, pairs)  7.76 us
    pallas_call x1, Pallas kernels, spread(): pl.pallas_call(spread_kernel, grid=(rows // slab,), in_specs=[whole_smem(...  6.8 us
    all_to_all x1, starting transfers between devices, tiled_step(): got = lax.all_to_all(sent, BOTH, split_axis=0, concat_axis=0, tiled=True)  6.39 us
    ppermute x2, starting transfers between devices, passed_across(): return lax.ppermute(value, BOTH, pairs)  3.86 us
    all_to_all x1, starting transfers between devices, tiled_step(): far = lax.all_to_all(far, BOTH, split_axis=0, concat_axis=0, tiled=True)  3.38 us
  transfers between devices with their start and end apart: 9, of which 4 were waited for; matrix products, arithmetic and copies ran while one was open for 0% of the time, Pallas kernels for 14%

profile of v2, /device:TPU:5, one launch (start us, length us, event | category | flops | bytes accessed | tf_op | source)
XLA Modules:
  0.0 77.7 jit_solution(7740386059040773840)
XLA Ops:
  0.6 1.3 %fusion = (f32[4]{0:T(128)}, f32[4]{0:T(128)}) fusion(f32[4]{0:T(128)} %param.17), kind=kLoop, calls=%fused_computation.1 | loop fusion | bytes 48 | tf_op jit(solution)/shard_map/sin | solution.py:575
  1.9 0.6 add_convert_fusion.edge
  2.5 6.8 %spread.1 = (f32[32,24,128]{2,1,0:T(8,128)}, f32[2,128,128]{2,1,0:T(8,128)}, f32[2,128,128]{2,1,0:T(8,128)}, f32[2,16,128]{2,1,0:T(8,128)}, f32[2,16,128]{2,1,0:...) custom-call(f32[2]{0:T(128)} %add_convert_fusion.edge, f32[4]{0:T(128)} %get-tuple-element.32.cosine, ...), custom_call_target="tpu_custom_call" | custom-call | tf_op jit(solution)/shard_map/spread/pallas_call | solution.py:311
  9.3 0.0 copy-start.10
  9.3 0.0 copy-start.9
  9.4 0.0 copy-start.12
  9.4 0.0 copy-start.11
  9.4 0.0 copy-start.14
  9.4 0.0 copy-start.13
  9.4 6.4 %all-to-all-start = ((f32[32,24,128]{2,1,0:T(8,128)}), f32[32,24,128]{2,1,0:T(8,128)S(1)}, u32[]{:S(2)}, u32[]{:S(2)}) async-start(f32[32,24,128]{2,1,0:T(8,128)} %get-tuple-element.28), calls=%async_computation | async-start | bytes 786432 | tf_op jit(solution)/shard_map/all_to_all | solution.py:581
  15.8 11.7 %all-to-all-done = f32[32,24,128]{2,1,0:T(8,128)S(1)} async-done(((f32[32,24,128]{2,1,0:T(8,128)}), f32[32,24,128]{2,1,0:T(8,128)S(1)}, u32[]{:S(2)}, u32[]{:S(2)}) %all-to-all-start) | async-done | bytes 393248 | tf_op jit(solution)/shard_map/all_to_all | solution.py:581
  27.5 0.0 copy-start
  27.5 0.7 copy-done
  28.2 2.6 %along_y.1 = (f32[64,256]{1,0:T(8,128)}, f32[64,256]{1,0:T(8,128)}) custom-call(s32[1]{0:T(128)} %bitcast.2.at.refs_0_, f32[4]{0:T(128)} %get-tuple-element.32.cosine, f32[4]{0:T(128)} %get-tuple-element.31.sine, f32[8,4,24,128]{3,2,1,0:T(8,128)} %bitcast.5, bf16[512,512]{1,0:T(8,128)(2,1)} %constant.21.clone.high, bf16[512,512]{1,0:T(8,128)(2,1)} %constant.22.clone.low), custom_call_target="tpu_custom_call" | custom-call | tf_op jit(solution)/shard_map/along_y/pallas_call | solution.py:407
  30.8 1.1 %collective-permute-start.6 = (f32[64,256]{1,0:T(8,128)}, f32[64,256]{1,0:T(8,128)S(1)}, u32[]{:S(2)}, u32[]{:S(2)}) collective-permute-start(f32[64,256]{1,0:T(8,128)} %get-tuple-element.30), channel_id=1, source_target_pairs={{0,1},{1,0},{2,3},{3,2},{4,5},{5,4},{6,7},{7,6},{8,9},{9,8},{10,11... | collective-permute-start | bytes 196616 | tf_op jit(solution)/shard_map/ppermute | solution.py:39
  31.9 1.1 %collective-permute-done.6.refs_2_ = f32[64,256]{1,0:T(8,128)S(1)} collective-permute-done((f32[64,256]{1,0:T(8,128)}, f32[64,256]{1,0:T(8,128)S(1)}, u32[]{:S(2)}, u32[]{:S(2)}) %collective-permute-start.6) | collective-permute-done | bytes 65568 | tf_op jit(solution)/shard_map/ppermute | solution.py:39
  33.0 0.0 copy-start.4
  33.0 0.6 copy-done.4
  33.6 2.3 %along_x.1 = f32[32,16,128]{2,1,0:T(8,128)} custom-call(s32[1]{0:T(128)} %bitcast.2.at.refs_0_, f32[64,256]{1,0:T(8,128)} %get-tuple-element.29.refs_1_, f32[64,256]{1,0:T(8,128)} %copy-done.4, bf16[512,128]{1,0:T(8,128)(2,1)} %constant.23.clone.refs_3_, bf16[512,128]{1,0:T(8,128)(2,1)} %constant.24.clone.refs_4_), custom_call_target="tpu_custom_call" | custom-call | tf_op jit(solution)/shard_map/along_x/pallas_call | solution.py:451
  35.9 3.4 %all-to-all-start.1 = ((f32[32,16,128]{2,1,0:T(8,128)}), f32[32,16,128]{2,1,0:T(8,128)S(1)}, u32[]{:S(2)}, u32[]{:S(2)}) async-start(f32[32,16,128]{2,1,0:T(8,128)} %along_x.1), calls=%async_computation.1 | async-start | bytes 524288 | tf_op jit(solution)/shard_map/all_to_all | solution.py:594
  39.3 0.0 copy-done.10
  39.3 2.0 %collective-permute-start = (f32[2,128,128]{2,1,0:T(8,128)S(1)}, f32[2,128,128]{2,1,0:T(8,128)S(1)}, u32[]{:S(2)}, u32[]{:S(2)}) collective-permute-start(f32[2,128,128]{2,1,0:T(8,128)S(1)} %copy-done.10), channel_id=1, source_target_pairs={{4,0},{8,4},{12,8},{16,12},{20,16},{24,20},{28,24},{5,1},{9,5},{13... | collective-permute-start | bytes 393224 | tf_op jit(solution)/shard_map/ppermute | solution.py:23
  41.3 0.0 copy-done.9
  41.4 4.2 %collective-permute-start.1 = (f32[2,128,128]{2,1,0:T(8,128)S(1)}, f32[2,128,128]{2,1,0:T(8,128)S(1)}, u32[]{:S(2)}, u32[]{:S(2)}) collective-permute-start(f32[2,128,128]{2,1,0:T(8,128)S(1)} %copy-done.9), channel_id=1, source_target_pairs={{0,4},{4,8},{8,12},{12,16},{16,20},{20,24},{24,28},{1,5},{5,9},{9,... | collective-permute-start | bytes 393224 | tf_op jit(solution)/shard_map/ppermute | solution.py:23
  45.5 0.0 copy-done.12
  45.5 2.9 %collective-permute-start.2 = (f32[2,16,128]{2,1,0:T(8,128)S(1)}, f32[2,16,128]{2,1,0:T(8,128)S(1)}, u32[]{:S(2)}, u32[]{:S(2)}) collective-permute-start(f32[2,16,128]{2,1,0:T(8,128)S(1)} %copy-done.12), channel_id=1, source_target_pairs={{1,0},{2,1},{3,2},{5,4},{6,5},{7,6},{9,8},{10,9},{11,10},{13,12},{... | collective-permute-start | bytes 49160 | tf_op jit(solution)/shard_map/ppermute | solution.py:23
  48.4 0.0 copy-done.11
  48.4 3.0 %collective-permute-start.3 = (f32[2,16,128]{2,1,0:T(8,128)S(1)}, f32[2,16,128]{2,1,0:T(8,128)S(1)}, u32[]{:S(2)}, u32[]{:S(2)}) collective-permute-start(f32[2,16,128]{2,1,0:T(8,128)S(1)} %copy-done.11), channel_id=1, source_target_pairs={{0,1},{1,2},{2,3},{4,5},{5,6},{6,7},{8,9},{9,10},{10,11},{12,13},{... | collective-permute-start | bytes 49160 | tf_op jit(solution)/shard_map/ppermute | solution.py:23
  51.4 0.0 copy-done.14
  51.4 1.9 %collective-permute-start.4 = (f32[8,128]{1,0:T(8,128)S(1)}, f32[8,128]{1,0:T(8,128)S(1)}, u32[]{:S(2)}, u32[]{:S(2)}) collective-permute-start(f32[8,128]{1,0:T(8,128)S(1)} %copy-done.14), channel_id=1, source_target_pairs={{4,1},{5,2},{6,3},{8,5},{9,6},{10,7},{12,9},{13,10},{14,11},{16,13... | collective-permute-start | bytes 12296 | tf_op jit(solution)/shard_map/ppermute | solution.py:34
  53.3 3.9 %collective-permute-done.4.corner_up = f32[8,128]{1,0:T(8,128)S(1)} collective-permute-done((f32[8,128]{1,0:T(8,128)S(1)}, f32[8,128]{1,0:T(8,128)S(1)}, u32[]{:S(2)}, u32[]{:S(2)}) %collective-permute-start.4) | collective-permute-done | bytes 4128 | tf_op jit(solution)/shard_map/ppermute | solution.py:34
  57.2 0.0 copy-start.7
  57.2 0.0 copy-done.13
  57.2 1.9 %collective-permute-start.5 = (f32[8,128]{1,0:T(8,128)S(1)}, f32[8,128]{1,0:T(8,128)S(1)}, u32[]{:S(2)}, u32[]{:S(2)}) collective-permute-start(f32[8,128]{1,0:T(8,128)S(1)} %copy-done.13), channel_id=1, source_target_pairs={{1,4},{2,5},{3,6},{5,8},{6,9},{7,10},{9,12},{10,13},{11,14},{13,16... | collective-permute-start | bytes 12296 | tf_op jit(solution)/shard_map/ppermute | solution.py:34
  59.2 3.9 %collective-permute-done.5.corner_down = f32[8,128]{1,0:T(8,128)S(1)} collective-permute-done((f32[8,128]{1,0:T(8,128)S(1)}, f32[8,128]{1,0:T(8,128)S(1)}, u32[]{:S(2)}, u32[]{:S(2)}) %collective-permute-start.5) | collective-permute-done | bytes 4128 | tf_op jit(solution)/shard_map/ppermute | solution.py:34
  63.1 0.0 copy-start.8
  63.1 0.0 collective-permute-done.2.cols_elec
  63.1 0.0 copy-start.5
  63.1 0.0 collective-permute-done.3.cols_magn
  63.1 0.0 copy-start.6
  63.1 0.0 collective-permute-done.rows_elec
  63.1 0.0 copy-start.2
  63.1 0.0 collective-permute-done.1.rows_magn
  63.1 0.0 copy-done.7
  63.1 0.5 copy-done.8
  63.7 0.0 copy-done.5
  63.7 0.0 copy-done.6
  63.7 0.1 copy-done.2
  63.7 0.0 copy-start.3
  63.8 0.6 copy-done.3
  64.4 10.6 %yee.1 = (f32[3,16,128,128]{3,2,1,0:T(8,128)}, f32[3,16,128,128]{3,2,1,0:T(8,128)}, f32[4,4,16,128]{3,2,1,0:T(8,128)}, f32[4,4,16,128]{3,2,1,0:T(8,128)}) custom-call(f32[2]{0:T(128)} %add_convert_fusion.edge, f32[4]{0:T(128)} %get-tuple-element.32.cosine, f32[4]{0:T(128)} %get-tuple-element.31.sine, f32[3,16,128,128]{3,2,1,0:T(8,128)} %ahead.1, ...), custom_call_target="tpu_custom_call" | custom-call | flops 47185920 | bytes 15728640 | tf_op jit(solution)/shard_map/yee/pallas_call | solution.py:554
  75.0 0.0 all-to-all-done.1.got
  75.0 0.0 copy-start.1
  75.0 0.7 copy-done.1
  75.7 2.0 %placed.1 = f32[2,16,32,64]{3,2,1,0:T(8,128)} custom-call(f32[32,16,128]{2,1,0:T(8,128)} %copy-done.1), custom_call_target="tpu_custom_call" | custom-call | tf_op jit(solution)/shard_map/placed/pallas_call | solution.py:474
Async XLA Ops:
  9.3 30.0 %copy-start.10 = (f32[2,128,128]{2,1,0:T(8,128)S(1)}, f32[2,128,128]{2,1,0:T(8,128)}, u32[]{:S(2)}) copy-start(f32[2,128,128]{2,1,0:T(8,128)} %get-tuple-element.18) | copy-start | bytes 393220
  9.3 32.0 %copy-start.9 = (f32[2,128,128]{2,1,0:T(8,128)S(1)}, f32[2,128,128]{2,1,0:T(8,128)}, u32[]{:S(2)}) copy-start(f32[2,128,128]{2,1,0:T(8,128)} %get-tuple-element.19) | copy-start | bytes 393220
  9.4 36.2 %copy-start.12 = (f32[2,16,128]{2,1,0:T(8,128)S(1)}, f32[2,16,128]{2,1,0:T(8,128)}, u32[]{:S(2)}) copy-start(f32[2,16,128]{2,1,0:T(8,128)} %get-tuple-element.20) | copy-start | bytes 49156
  9.4 39.0 %copy-start.11 = (f32[2,16,128]{2,1,0:T(8,128)S(1)}, f32[2,16,128]{2,1,0:T(8,128)}, u32[]{:S(2)}) copy-start(f32[2,16,128]{2,1,0:T(8,128)} %get-tuple-element.21) | copy-start | bytes 49156
  9.4 42.0 %copy-start.14 = (f32[8,128]{1,0:T(8,128)S(1)}, f32[8,128]{1,0:T(8,128)}, u32[]{:S(2)}) copy-start(f32[8,128]{1,0:T(8,128)} %get-tuple-element.22) | copy-start | bytes 12292
  9.4 47.9 %copy-start.13 = (f32[8,128]{1,0:T(8,128)S(1)}, f32[8,128]{1,0:T(8,128)}, u32[]{:S(2)}) copy-start(f32[8,128]{1,0:T(8,128)} %get-tuple-element.23) | copy-start | bytes 12292
  9.4 18.1 %all-to-all-start = ((f32[32,24,128]{2,1,0:T(8,128)}), f32[32,24,128]{2,1,0:T(8,128)S(1)}, u32[]{:S(2)}, u32[]{:S(2)}) async-start(f32[32,24,128]{2,1,0:T(8,128)} %get-tuple-element.28), calls=%async_computation | async-start | bytes 786432 | tf_op jit(solution)/shard_map/all_to_all | solution.py:581
  27.5 0.7 copy-start
  30.8 2.2 %collective-permute-start.6 = (f32[64,256]{1,0:T(8,128)}, f32[64,256]{1,0:T(8,128)S(1)}, u32[]{:S(2)}, u32[]{:S(2)}) collective-permute-start(f32[64,256]{1,0:T(8,128)} %get-tuple-element.30), channel_id=1, source_target_pairs={{0,1},{1,0},{2,3},{3,2},{4,5},{5,4},{6,7},{7,6},{8,9},{9,8},{10,11... | collective-permute-start | bytes 196616 | tf_op jit(solution)/shard_map/ppermute | solution.py:39
  33.0 0.6 copy-start.4
  35.9 39.1 %all-to-all-start.1 = ((f32[32,16,128]{2,1,0:T(8,128)}), f32[32,16,128]{2,1,0:T(8,128)S(1)}, u32[]{:S(2)}, u32[]{:S(2)}) async-start(f32[32,16,128]{2,1,0:T(8,128)} %along_x.1), calls=%async_computation.1 | async-start | bytes 524288 | tf_op jit(solution)/shard_map/all_to_all | solution.py:594
  39.3 23.8 %collective-permute-start = (f32[2,128,128]{2,1,0:T(8,128)S(1)}, f32[2,128,128]{2,1,0:T(8,128)S(1)}, u32[]{:S(2)}, u32[]{:S(2)}) collective-permute-start(f32[2,128,128]{2,1,0:T(8,128)S(1)} %copy-done.10), channel_id=1, source_target_pairs={{4,0},{8,4},{12,8},{16,12},{20,16},{24,20},{28,24},{5,1},{9,5},{13... | collective-permute-start | bytes 393224 | tf_op jit(solution)/shard_map/ppermute | solution.py:23
  41.4 21.8 %collective-permute-start.1 = (f32[2,128,128]{2,1,0:T(8,128)S(1)}, f32[2,128,128]{2,1,0:T(8,128)S(1)}, u32[]{:S(2)}, u32[]{:S(2)}) collective-permute-start(f32[2,128,128]{2,1,0:T(8,128)S(1)} %copy-done.9), channel_id=1, source_target_pairs={{0,4},{4,8},{8,12},{12,16},{16,20},{20,24},{24,28},{1,5},{5,9},{9,... | collective-permute-start | bytes 393224 | tf_op jit(solution)/shard_map/ppermute | solution.py:23
  45.5 17.5 %collective-permute-start.2 = (f32[2,16,128]{2,1,0:T(8,128)S(1)}, f32[2,16,128]{2,1,0:T(8,128)S(1)}, u32[]{:S(2)}, u32[]{:S(2)}) collective-permute-start(f32[2,16,128]{2,1,0:T(8,128)S(1)} %copy-done.12), channel_id=1, source_target_pairs={{1,0},{2,1},{3,2},{5,4},{6,5},{7,6},{9,8},{10,9},{11,10},{13,12},{... | collective-permute-start | bytes 49160 | tf_op jit(solution)/shard_map/ppermute | solution.py:23
  48.4 14.7 %collective-permute-start.3 = (f32[2,16,128]{2,1,0:T(8,128)S(1)}, f32[2,16,128]{2,1,0:T(8,128)S(1)}, u32[]{:S(2)}, u32[]{:S(2)}) collective-permute-start(f32[2,16,128]{2,1,0:T(8,128)S(1)} %copy-done.11), channel_id=1, source_target_pairs={{0,1},{1,2},{2,3},{4,5},{5,6},{6,7},{8,9},{9,10},{10,11},{12,13},{... | collective-permute-start | bytes 49160 | tf_op jit(solution)/shard_map/ppermute | solution.py:23
  51.4 5.8 %collective-permute-start.4 = (f32[8,128]{1,0:T(8,128)S(1)}, f32[8,128]{1,0:T(8,128)S(1)}, u32[]{:S(2)}, u32[]{:S(2)}) collective-permute-start(f32[8,128]{1,0:T(8,128)S(1)} %copy-done.14), channel_id=1, source_target_pairs={{4,1},{5,2},{6,3},{8,5},{9,6},{10,7},{12,9},{13,10},{14,11},{16,13... | collective-permute-start | bytes 12296 | tf_op jit(solution)/shard_map/ppermute | solution.py:34
  57.2 5.9 %copy-start.7 = (f32[8,128]{1,0:T(8,128)}, f32[8,128]{1,0:T(8,128)S(1)}, u32[]{:S(2)}) copy-start(f32[8,128]{1,0:T(8,128)S(1)} %collective-permute-done.4.corner_up) | copy-start | bytes 12292
  57.2 5.8 %collective-permute-start.5 = (f32[8,128]{1,0:T(8,128)S(1)}, f32[8,128]{1,0:T(8,128)S(1)}, u32[]{:S(2)}, u32[]{:S(2)}) collective-permute-start(f32[8,128]{1,0:T(8,128)S(1)} %copy-done.13), channel_id=1, source_target_pairs={{1,4},{2,5},{3,6},{5,8},{6,9},{7,10},{9,12},{10,13},{11,14},{13,16... | collective-permute-start | bytes 12296 | tf_op jit(solution)/shard_map/ppermute | solution.py:34
  63.1 0.6 copy-start.8
  63.1 0.6 copy-start.5
  63.1 0.6 copy-start.6
  63.1 0.7 copy-start.2
  63.7 0.6 copy-start.3
  75.0 0.7 copy-start.1

commit v3 on v2

--- a/solution.py
+++ b/solution.py
@@ -8,6 +8,7 @@
 from jax.experimental.pallas import tpu as pltpu
 from jax.sharding import PartitionSpec as P
 
+
 WAVES = 256
 TOP_PLANE = 111
 BOTH = ("gx", "gy")
@@ -21,17 +22,6 @@
     devices = lax.axis_size(axis)
     pairs = [(i, i + by) for i in range(devices) if 0 <= i + by < devices]
     return lax.ppermute(value, axis, pairs)
-
-
-def passed_across(value, by_x, by_y):
-    along_x, along_y = lax.axis_size("gx"), lax.axis_size("gy")
-    pairs = [
-        (x * along_y + y, (x + by_x) * along_y + y + by_y)
-        for x in range(along_x)
-        for y in range(along_y)
-        if 0 <= x + by_x < along_x and 0 <= y + by_y < along_y
-    ]
-    return lax.ppermute(value, BOTH, pairs)
 
 
 def swapped(value, by):
@@ -182,6 +172,22 @@
     return pl.BlockSpec(memory_space=pltpu.VMEM)
 
 
+def kept(value):
+    return pltpu.with_memory_space_constraint(value, pltpu.VMEM)
+
+
+def far_kept(value):
+    return pltpu.with_memory_space_constraint(value, pltpu.HBM)
+
+
+def room(shape, dtype=jnp.float32):
+    return pltpu.VMEM(shape, dtype)
+
+
+def limited(size=24):
+    return pltpu.CompilerParams(vmem_limit_bytes=size * 1024 * 1024)
+
+
 def whole_smem():
     return pl.BlockSpec(memory_space=pltpu.SMEM)
 
@@ -190,8 +196,8 @@
 
 
 def spread_kernel(
-    edge, cosine, sine, elec, magn, ret, coup, real, imag,
-    out, rows_elec, rows_magn, cols_elec, cols_magn, corner_up, corner_down, planes, edges,
+    edge, cosine, sine, elec, magn, ret, coup, real_far, imag_far,
+    out, rows_elec, rows_magn, cols_elec, cols_magn, planes, edges, corners, real, imag, arrived,
 ):
     step = pl.program_id(0)
     steps = pl.num_programs(0)
@@ -217,11 +223,16 @@
             magn[0, at, -1:, :] + curl_step * elec[2, at, -1:, :] + curl_step * (after(line, 1) - line)
         )
 
+    real_copy = pltpu.make_async_copy(real_far, real, arrived.at[0])
+    imag_copy = pltpu.make_async_copy(imag_far, imag, arrived.at[1])
+
     @pl.when(step == 0)
     def _():
+        real_copy.start()
+        imag_copy.start()
         rows_elec[0] = elec[1, 0]
         rows_elec[1] = elec[2, 0]
-        corner_up[...] = jnp.broadcast_to(elec[1, 0, -1:, :], corner_up.shape)
+        corners[0:1, :] = elec[1, 0, -1:, :]
 
     @pl.when(step == steps - 1)
     def _():
@@ -229,7 +240,7 @@
         ex, ey, ez = elec[0, last], elec[1, last], elec[2, last]
         rows_magn[0] = magn[1, last] - curl_step * (after(ex, 1) - ex) - curl_step * ez
         rows_magn[1] = magn[2, last] + curl_step * ey + curl_step * (after(ex, 0) - ex)
-        corner_down[...] = jnp.broadcast_to(elec[0, last, 0:1, :], corner_down.shape)
+        corners[1:2, :] = elec[0, last, 0:1, :]
         end_x, end_y, end_z = edges[0], edges[1], edges[2]
         cols_magn[1] = end_z - curl_step * (after(end_y, 0) - end_y) - curl_step * end_x
 
@@ -274,22 +285,22 @@
             return jnp.concatenate([block, pad], axis=0).T[0:SUBLANES]
 
         end = LANES - 1
+        real_copy.wait()
+        imag_copy.wait()
         for comp in range(4):
             factor = gain if comp < 2 else one
-            upright_lines = upright(
-                [(none, 0), (none, 0), (none, 0), (none, 0), (col_left[comp], 0), (col_right[comp], end), (factor, end), (factor, 0)]
-            )
-            extra = jnp.where(tall >= 4, upright_lines, 0.0)
-            extra = jnp.where(tall == 0, row_up[comp][0:1], extra)
+            columns = upright([(col_left[comp], 0), (col_right[comp], end), (factor, end), (factor, 0)])
+            columns = sum(moved(columns[which : which + 1], which * rows, 1) for which in range(4))
+            if comp < 2:
+                spare = moved(-push[0:1], -end, 1) if comp == 0 else curl_step * ex_p[rows - 1 :]
+                columns = jnp.where(lanes[0:1] == 4 * rows, moved(spare, 4 * rows, 1), columns)
+            extra = jnp.where(tall == 0, row_up[comp][0:1], 0.0)
             extra = jnp.where(tall == 1, row_down[comp][rows - 1 :], extra)
             extra = jnp.where(tall == 2, factor[rows - 1 :], extra)
             extra = jnp.where(tall == 3, factor[0:1], extra)
-            if comp == 0:
-                spare = moved(-push[0:1], rows - end, 1)
-                extra = jnp.where((tall == 5) & (lanes == rows), spare, extra)
-            if comp == 1:
-                spare = moved(curl_step * ex_p[rows - 1 :], rows, 1)
-                extra = jnp.where((tall == 4) & (lanes == rows), spare, extra)
+            extra = jnp.where(tall == 4, columns, extra)
+            extra = jnp.where(tall == 5, corners[0:1, :], extra)
+            extra = jnp.where(tall == 6, corners[1:2, :], extra)
             freqs = real.shape[1]
             for freq in range(freqs):
                 new_real = real[comp, freq] + tangent[comp] * cosine[freq]
@@ -311,20 +322,22 @@
     return pl.pallas_call(
         spread_kernel,
         grid=(rows // slab,),
-        in_specs=[whole_smem(), whole_smem(), whole_smem(), vector, vector, scalar, scalar, whole_vmem(), whole_vmem()],
-        out_specs=[whole_vmem()] * 7,
+        in_specs=[whole_smem(), whole_smem(), whole_smem(), vector, vector, scalar, scalar] + [pl.BlockSpec(memory_space=pl.ANY)] * 2,
+        out_specs=[whole_vmem()] * 5,
+        compiler_params=limited(),
         out_shape=[
-            jax.ShapeDtypeStruct((comps * freqs * 2, 24, cols), kind),
-            jax.ShapeDtypeStruct((2, cols, deep), kind),
-            jax.ShapeDtypeStruct((2, cols, deep), kind),
-            jax.ShapeDtypeStruct((2, rows, deep), kind),
-            jax.ShapeDtypeStruct((2, rows, deep), kind),
-            jax.ShapeDtypeStruct((SUBLANES, deep), kind),
-            jax.ShapeDtypeStruct((SUBLANES, deep), kind),
+            pltpu.HBM((comps * freqs * 2, 24, cols), kind),
+            room((2, cols, deep)),
+            room((2, cols, deep)),
+            room((2, rows, deep)),
+            room((2, rows, deep)),
         ],
-        scratch_shapes=[pltpu.VMEM((rows, 16, LANES), kind), pltpu.VMEM((3, rows, LANES), kind)],
+        scratch_shapes=[
+            room((rows, 16, LANES)), room((3, rows, LANES)), room((2, LANES)),
+            room(spectrum_real.shape), room(spectrum_imag.shape), pltpu.SemaphoreType.DMA((2,)),
+        ],
         name="spread",
-    )(edge, cosine, sine, electric, magnetic, retention, coupling, spectrum_real, spectrum_imag)
+    )(edge, cosine, sine, *(far_kept(a) for a in (electric, magnetic, retention, coupling, spectrum_real, spectrum_imag)))
 
 
 def split_high(value):
@@ -346,21 +359,24 @@
     is_last = jnp.where(half == 1, 1.0, 0.0)
     is_first = jnp.where(half == 0, 1.0, 0.0)
 
-    def column(which):
-        return jnp.concatenate([got[x, :, 16 + which, :] for x in range(along_x)], axis=0)
-
+    packed = jnp.concatenate([got[x, :, 20, :] for x in range(along_x)], axis=0)
     block = spot((blocks, LANES), 0)
     lane = spot((blocks, LANES), 1)
     inner = block % along_y
     rows = 16
-    from_right = jnp.where(inner == along_y - 1, 0.0, moved(column(4), -1, 0))
-    from_left = jnp.where(inner == 0, 0.0, moved(column(5), 1, 0))
-    right_up = jnp.where(block < along_y, 0.0, moved(from_right, along_y, 0))
-    left_down = jnp.where(block >= blocks - along_y, 0.0, moved(from_left, -along_y, 0))
-    from_right = from_right + jnp.where(lane == 0, moved(right_up, -rows, 1), 0.0)
-    from_left = from_left + jnp.where(lane == rows - 1, moved(left_down, -1, 1), 0.0)
-    last_col = column(6) * from_right
-    first_col = column(7) * from_left
+
+    def lines_at(value, which):
+        return jnp.where(lane < rows, moved(value, -which * rows, 1), 0.0)
+
+    from_right = jnp.where(inner == along_y - 1, 0.0, moved(packed, -1, 0))
+    from_left = jnp.where(inner == 0, 0.0, moved(packed, 1, 0))
+    comp = at[0] // (2 * cosine.shape[0])
+    right_up = jnp.where((block >= along_y) & (comp == 1), moved(from_right, along_y, 0), 0.0)
+    left_down = jnp.where((block < blocks - along_y) & (comp == 0), moved(from_left, -along_y, 0), 0.0)
+    from_right = lines_at(from_right, 0) + jnp.where(lane == 0, moved(right_up, -4 * rows, 1), 0.0)
+    from_left = lines_at(from_left, 1) + jnp.where(lane == rows - 1, moved(left_down, -3 * rows - 1, 1), 0.0)
+    last_col = lines_at(packed, 2) * from_right
+    first_col = lines_at(packed, 3) * from_left
     pad = jnp.zeros((LANES - 2 * blocks, LANES), jnp.float32)
     upright = jnp.concatenate([last_col, first_col, pad], axis=0).T
     cols = jnp.where(half == 0, upright[0:8], upright[8:16])
@@ -403,15 +419,16 @@
     order = np.arange(WAVES).reshape(along_y, 2, wide // 2).transpose(1, 0, 2).reshape(-1)
     cos_y, sin_y = wave_tables(WAVES, cols * along_y)
     high, low = in_two(np.concatenate([cos_y[order].T, sin_y[order].T], axis=1))
-    shape = jax.ShapeDtypeStruct((along_x * 8, WAVES), jnp.float32)
+    shape = room((along_x * 8, WAVES))
     return pl.pallas_call(
         along_y_kernel,
         in_specs=[whole_smem()] * 3 + [whole_vmem()] * 3,
         out_specs=[whole_vmem()] * 2,
         out_shape=[shape, shape],
-        scratch_shapes=[pltpu.VMEM((along_x * 16, along_y * LANES), jnp.float32)],
+        scratch_shapes=[room((along_x * 16, along_y * LANES))],
+        compiler_params=limited(),
         name="along_y",
-    )(place, cosine, sine, got.reshape(along_x, along_y, 24, cols), high, low)
+    )(place, cosine, sine, kept(got.reshape(along_x, along_y, 24, cols)), kept(high), kept(low))
 
 
 def along_x_kernel(along_x, at, mine, other, high, low, out):
@@ -452,9 +469,10 @@
         lambda *refs: along_x_kernel(along_x, *refs),
         in_specs=[whole_smem()] + [whole_vmem()] * 4,
         out_specs=whole_vmem(),
-        out_shape=jax.ShapeDtypeStruct((devices, 16, LANES), jnp.float32),
+        out_shape=pltpu.HBM((devices, 16, LANES), jnp.float32),
+        compiler_params=limited(),
         name="along_x",
-    )(place, mine, other, high, low)
+    )(place, kept(mine), kept(other), kept(high), kept(low))
 
 
 def placed_kernel(got, out):
@@ -476,13 +494,14 @@
         in_specs=[whole_vmem()],
         out_specs=whole_vmem(),
         out_shape=jax.ShapeDtypeStruct((2, comps * freqs, tall, wide), jnp.float32),
+        compiler_params=limited(),
         name="placed",
-    )(got)
+    )(kept(got))
     return far.reshape(2, comps, freqs, tall, wide)
 
 
 def yee_kernel(
-    edge, cosine, sine, elec, ahead, magn, ret, coup, rows_elec, rows_magn, cols_elec, cols_magn, corner_up, corner_down,
+    edge, place, cosine, sine, elec, ahead, magn, ret, coup, rows_elec, rows_magn, cols_elec, cols_magn, got,
     real, imag, new_elec, new_magn, new_real, new_imag, carried, tops,
 ):
     step = pl.program_id(0)
@@ -490,12 +509,14 @@
     deep = elec.shape[1]
     inner_x = edge[0]
     inner_y = edge[1]
+    corner_up = got[place[1], 21:22, :] * edge[2]
+    corner_down = got[place[2], 22:23, :] * edge[3]
     row = spot((LANES, LANES), 0)
     lane = spot((LANES, LANES), 1)
 
     @pl.when(step == 0)
     def _():
-        spare = jnp.where(row == LANES - 1, curl_step * corner_down[0:1, :], 0.0)
+        spare = jnp.where(row == LANES - 1, curl_step * corner_down, 0.0)
         carried[0] = (rows_magn[0] + curl_step * elec[2, 0]) * inner_x
         carried[1] = (rows_magn[1] - curl_step * elec[1, 0] + spare) * inner_x
 
@@ -517,7 +538,7 @@
         side_x = (cols_magn[0, here, :] - curl_step * ez[0:1]) * inner_y
         side_z = cols_magn[1, here, :] + curl_step * ex[0:1]
         if at + 1 == deep:
-            side_z = side_z - jnp.where(at_end, curl_step * corner_up[0:1, :], 0.0)
+            side_z = side_z - jnp.where(at_end, curl_step * corner_up, 0.0)
         side_z = side_z * inner_y
         keep, gain = ret[at], coup[at]
         new_x = keep * ex + gain * ((hz - before(hz, 0, side_z)) - (hy - before(hy, 1)))
@@ -543,7 +564,7 @@
                 new_imag[comp, freq] = imag[comp, freq] - tangent * sine[freq]
 
 
-def yee(edge, cosine, sine, electric, magnetic, retention, coupling, halos, spectrum_real, spectrum_imag):
+def yee(edge, place, cosine, sine, electric, magnetic, retention, coupling, halos, got, spectrum_real, spectrum_imag):
     _, rows, cols, deep = electric.shape
     slab = 2
     steps = rows // slab
@@ -554,7 +575,8 @@
     return pl.pallas_call(
         yee_kernel,
         grid=(steps,),
-        in_specs=[whole_smem()] * 3 + [vector, ahead, vector, scalar, scalar] + [whole_vmem()] * 8,
+        in_specs=[whole_smem()] * 4 + [vector, ahead, vector, scalar, scalar] + [whole_vmem()] * 7,
+        compiler_params=limited(),
         out_specs=[vector, vector, whole_vmem(), whole_vmem()],
         out_shape=[
             jax.ShapeDtypeStruct(electric.shape, kind),
@@ -565,7 +587,11 @@
         scratch_shapes=[pltpu.VMEM((2, cols, deep), kind), pltpu.VMEM((rows, SUBLANES, LANES), kind)],
         cost_estimate=pl.CostEstimate(flops=60 * electric.size, bytes_accessed=20 * electric.size, transcendentals=0),
         name="yee",
-    )(edge, cosine, sine, electric, electric, magnetic, retention, coupling, *halos, spectrum_real, spectrum_imag)
+    )(
+        edge, place, cosine, sine,
+        *(far_kept(a) for a in (electric, electric, magnetic, retention, coupling)),
+        *(kept(halo) for halo in halos), kept(got), far_kept(spectrum_real), far_kept(spectrum_imag),
+    )
 
 
 def tiled_step(electric, magnetic, retention, coupling, spectrum_real, spectrum_imag, phases):
@@ -573,9 +599,13 @@
     along_x, along_y = lax.axis_size("gx"), lax.axis_size("gy")
     devices = along_x * along_y
     cosine, sine = jnp.cos(phases), jnp.sin(phases)
-    place = lax.axis_index(BOTH).astype(jnp.int32).reshape(1)
-    edge = jnp.stack([lax.axis_index("gx") > 0, lax.axis_index("gy") > 0]).astype(jnp.float32)
-    sent, rows_elec, rows_magn, cols_elec, cols_magn, corner_up, corner_down = spread(
+    at_x, at_y = lax.axis_index("gx"), lax.axis_index("gy")
+    here = lax.axis_index(BOTH)
+    inner = (at_x > 0, at_y > 0, (at_x + 1 < along_x) & (at_y > 0), (at_x > 0) & (at_y + 1 < along_y))
+    edge = jnp.stack(inner).astype(jnp.float32)
+    up, down = jnp.minimum(here + along_y - 1, devices - 1), jnp.maximum(here - along_y + 1, 0)
+    place = jnp.stack([here, up, down]).astype(jnp.int32)
+    sent, rows_elec, rows_magn, cols_elec, cols_magn = spread(
         edge, electric, magnetic, retention, coupling, spectrum_real, spectrum_imag, cosine, sine
     )
     got = lax.all_to_all(sent, BOTH, split_axis=0, concat_axis=0, tiled=True)
@@ -584,8 +614,6 @@
         passed_along(rows_magn, "gx", 1),
         passed_along(cols_elec, "gy", -1),
         passed_along(cols_magn, "gy", 1),
-        passed_across(corner_up, -1, 1),
-        passed_across(corner_down, 1, -1),
     )
     mine, other = along_y_sums(place, cosine, sine, got, cols, along_x, along_y)
     other = swapped(other, 1)
@@ -593,7 +621,8 @@
     far = along_x_sums(place, mine, other, rows, scale, along_x, devices)
     far = lax.all_to_all(far, BOTH, split_axis=0, concat_axis=0, tiled=True)
     next_electric, next_magnetic, next_real, next_imag = yee(
-        edge, cosine, sine, electric, magnetic, retention, coupling, halos, spectrum_real, spectrum_imag
+        edge, place, cosine, sine, electric, magnetic, retention, coupling, halos, got,
+        spectrum_real, spectrum_imag,
     )
     far_field = placed_far(far, comps, freqs, WAVES // along_x, WAVES // along_y)
     return (next_electric, next_magnetic, next_real, next_imag, far_field)

time: 78.4 us -> 60.4 us (0.77)
  the two profiles are of different devices: /device:TPU:5 before, /device:TPU:6 now
where the time goes in v3:
time: 60.4 us; the launch traced here: 59.9 us
  Pallas kernels  21.4 us (35%)
  starting transfers between devices  21.1 us (35%)
  waiting for transfers between devices  15.7 us (26%)
  between operations  0.78 us (1%)
  local copies, waits for them, and re-layouts  0.71 us (1%)
    all_to_all x1, waiting for transfers between devices, tiled_step(): got = lax.all_to_all(sent, BOTH, split_axis=0, concat_axis=0, tiled=True)  11.8 us
    ppermute x4, starting transfers between devices, passed_along(): return lax.ppermute(value, axis, pairs)  11.1 us
    pallas_call x1, Pallas kernels, yee(): pl.pallas_call(yee_kernel, grid=(steps,), in_specs=[whole_smem()] * 4 + [...  10.5 us
    pallas_call x1, Pallas kernels, spread(): pl.pallas_call(spread_kernel, grid=(rows // slab,), in_specs=[whole_smem(...  6.85 us
    all_to_all x1, starting transfers between devices, tiled_step(): got = lax.all_to_all(sent, BOTH, split_axis=0, concat_axis=0, tiled=True)  6.08 us
    all_to_all x1, starting transfers between devices, tiled_step(): far = lax.all_to_all(far, BOTH, split_axis=0, concat_axis=0, tiled=True)  3.89 us
    ppermute x4, waiting for transfers between devices, passed_along(): return lax.ppermute(value, axis, pairs)  2.64 us
    pallas_call x1, Pallas kernels, along_x_sums(): pl.pallas_call(lambda *refs: along_x_kernel(along_x, *refs), in_specs=[wh...  1.81 us
  transfers between devices with their start and end apart: 7, of which 3 were waited for; matrix products, arithmetic and copies ran while one was open for 0% of the time, Pallas kernels for 18%

profile of v3, /device:TPU:6, one launch (start us, length us, event | category | flops | bytes accessed | tf_op | source)
XLA Modules:
  0.0 59.9 jit_solution(1533414213555757275)
XLA Ops:
  0.6 0.7 %fusion = (f32[4]{0:T(128)S(1)}, f32[4]{0:T(128)S(1)}) fusion(f32[4]{0:T(128)} %param.17), kind=kLoop, calls=%fused_computation.2 | loop fusion | bytes 48 | tf_op jit(solution)/shard_map/sin | solution.py:601
  1.4 0.1 add_convert_fusion.edge
  1.4 0.0 copy-start
  1.4 0.0 copy-start.1
  1.4 0.0 copy-start.2
  1.4 0.0 copy-start.3
  1.5 6.9 %spread.1 = (f32[32,24,128]{2,1,0:T(8,128)}, f32[2,128,128]{2,1,0:T(8,128)S(1)}, f32[2,128,128]{2,1,0:T(8,128)S(1)}, f32[2,16,128]{2,1,0:T(8,128)S(1)}, f32[2,16,128]{2,1,0:T(8,128)S(1)}) custom-call(f32[4]{0:T(128)S(1)} %add_convert_fusion.edge, f32[4]{0:T(128)S(1)} %get-tuple-element.28.cosine, f32[4]{0:T(128)S(1)} %get-tuple-element.27.sine, ...), custom_call_target="tpu_custom_call" | custom-call | tf_op jit(solution)/shard_map/spread/pallas_call | solution.py:322
  8.3 6.1 %all-to-all-start = ((f32[32,24,128]{2,1,0:T(8,128)}), f32[32,24,128]{2,1,0:T(8,128)S(1)}, u32[]{:S(2)}, u32[]{:S(2)}) async-start(f32[32,24,128]{2,1,0:T(8,128)} %get-tuple-element.20), calls=%async_computation | async-start | bytes 786432 | tf_op jit(solution)/shard_map/all_to_all | solution.py:611
  14.4 0.1 pad_add_fusion.place.at.refs_0_
  14.5 11.8 %all-to-all-done.got = f32[32,24,128]{2,1,0:T(8,128)S(1)} async-done(((f32[32,24,128]{2,1,0:T(8,128)}), f32[32,24,128]{2,1,0:T(8,128)S(1)}, u32[]{:S(2)}, u32[]{:S(2)}) %all-to-all-start) | async-done | bytes 393248 | tf_op jit(solution)/shard_map/all_to_all | solution.py:611
  26.3 0.0 copy-done
  26.3 0.0 copy-done.1
  26.3 1.2 %along_y.1 = (f32[64,256]{1,0:T(8,128)S(1)}, f32[64,256]{1,0:T(8,128)S(1)}) custom-call(s32[3]{0:T(128)S(1)} %pad_add_fusion.place.at.refs_0_, f32[4]{0:T(128)S(1)} %get-tuple-element.28.cosine, f32[4]{0:T(128)S(1)} %get-tuple-element.27.sine, f32[8,4,24,128]{3,2,1,0:T(8,128)S(1)} %bitcast.9, bf16[512,512]{1,0:T(8,128)(2,1)S(1)} %copy-done, ...), custom_call_target="tpu_custom_call" | custom-call | tf_op jit(solution)/shard_map/along_y/pallas_call | solution.py:423
  27.5 0.1 collective-permute-start.4
  27.5 1.2 %collective-permute-done.4.refs_2_ = f32[64,256]{1,0:T(8,128)S(1)} collective-permute-done((f32[64,256]{1,0:T(8,128)S(1)}, f32[64,256]{1,0:T(8,128)S(1)}, u32[]{:S(2)}, u32[]{:S(2)}) %collective-permute-start.4) | collective-permute-done | bytes 65568 | tf_op jit(solution)/shard_map/ppermute | solution.py:29
  28.8 0.0 copy-done.2
  28.8 0.0 copy-done.3
  28.8 1.8 %along_x.1 = f32[32,16,128]{2,1,0:T(8,128)} custom-call(s32[3]{0:T(128)S(1)} %pad_add_fusion.place.at.refs_0_, f32[64,256]{1,0:T(8,128)S(1)} %get-tuple-element.25.refs_1_, f32[64,256]{1,0:T(8,128)S(1)} %collective-permute-done.4.refs_2_, bf16[512,128]{1,0:T(8,128)(2,1)S(1)} %copy-done.2, bf16[512,128]{1,0:T(8,128)(2,1)S(1)} %copy-done.3), custom_call_target="tpu_custom_call" | custom-call | tf_op jit(solution)/shard_map/along_x/pallas_call | solution.py:468
  30.6 3.9 %all-to-all-start.1 = ((f32[32,16,128]{2,1,0:T(8,128)}), f32[32,16,128]{2,1,0:T(8,128)S(1)}, u32[]{:S(2)}, u32[]{:S(2)}) async-start(f32[32,16,128]{2,1,0:T(8,128)} %along_x.1), calls=%async_computation.1 | async-start | bytes 524288 | tf_op jit(solution)/shard_map/all_to_all | solution.py:622
  34.5 2.5 %collective-permute-start = (f32[2,128,128]{2,1,0:T(8,128)S(1)}, f32[2,128,128]{2,1,0:T(8,128)S(1)}, u32[]{:S(2)}, u32[]{:S(2)}) collective-permute-start(f32[2,128,128]{2,1,0:T(8,128)S(1)} %get-tuple-element.16), channel_id=1, source_target_pairs={{4,0},{8,4},{12,8},{16,12},{20,16},{24,20},{28,24},{5,1},{9,5},{13... | collective-permute-start | bytes 393224 | tf_op jit(solution)/shard_map/ppermute | solution.py:24
  37.0 4.3 %collective-permute-start.1 = (f32[2,128,128]{2,1,0:T(8,128)S(1)}, f32[2,128,128]{2,1,0:T(8,128)S(1)}, u32[]{:S(2)}, u32[]{:S(2)}) collective-permute-start(f32[2,128,128]{2,1,0:T(8,128)S(1)} %get-tuple-element.17), channel_id=1, source_target_pairs={{0,4},{4,8},{8,12},{12,16},{16,20},{20,24},{24,28},{1,5},{5,9},{9,... | collective-permute-start | bytes 393224 | tf_op jit(solution)/shard_map/ppermute | solution.py:24
  41.3 1.9 %collective-permute-start.2 = (f32[2,16,128]{2,1,0:T(8,128)S(1)}, f32[2,16,128]{2,1,0:T(8,128)S(1)}, u32[]{:S(2)}, u32[]{:S(2)}) collective-permute-start(f32[2,16,128]{2,1,0:T(8,128)S(1)} %get-tuple-element.18), channel_id=1, source_target_pairs={{1,0},{2,1},{3,2},{5,4},{6,5},{7,6},{9,8},{10,9},{11,10},{13,12},{... | collective-permute-start | bytes 49160 | tf_op jit(solution)/shard_map/ppermute | solution.py:24
  43.2 2.4 %collective-permute-start.3 = (f32[2,16,128]{2,1,0:T(8,128)S(1)}, f32[2,16,128]{2,1,0:T(8,128)S(1)}, u32[]{:S(2)}, u32[]{:S(2)}) collective-permute-start(f32[2,16,128]{2,1,0:T(8,128)S(1)} %get-tuple-element.19), channel_id=1, source_target_pairs={{0,1},{1,2},{2,3},{4,5},{5,6},{6,7},{8,9},{9,10},{10,11},{12,13},{... | collective-permute-start | bytes 49160 | tf_op jit(solution)/shard_map/ppermute | solution.py:24
  45.6 0.0 collective-permute-done.2.cols_elec
  45.6 2.6 %collective-permute-done.3.cols_magn = f32[2,16,128]{2,1,0:T(8,128)S(1)} collective-permute-done((f32[2,16,128]{2,1,0:T(8,128)S(1)}, f32[2,16,128]{2,1,0:T(8,128)S(1)}, u32[]{:S(2)}, u32[]{:S(2)}) %collective-permute-start.3) | collective-permute-done | bytes 16416 | tf_op jit(solution)/shard_map/ppermute | solution.py:24
  48.2 0.0 collective-permute-done.rows_elec
  48.2 0.0 collective-permute-done.1.rows_magn
  48.3 10.5 %yee.1 = (f32[3,16,128,128]{3,2,1,0:T(8,128)}, f32[3,16,128,128]{3,2,1,0:T(8,128)}, f32[4,4,16,128]{3,2,1,0:T(8,128)}, f32[4,4,16,128]{3,2,1,0:T(8,128)}) custom-call(f32[4]{0:T(128)S(1)} %add_convert_fusion.edge, s32[3]{0:T(128)S(1)} %pad_add_fusion.place.at.refs_0_, f32[4]{0:T(128)S(1)} %get-tuple-element.28.cosine, f32[4]{0:T(128)S(1)} %get-tuple-element.27.sine, ...), custom_call_target="tpu_custom_call" | custom-call | flops 47185920 | bytes 15728640 | tf_op jit(solution)/shard_map/yee/pallas_call | solution.py:575
  58.8 0.0 all-to-all-done.1.got
  58.8 1.1 %placed.1 = f32[2,16,32,64]{3,2,1,0:T(8,128)} custom-call(f32[32,16,128]{2,1,0:T(8,128)S(1)} %all-to-all-done.1.got), custom_call_target="tpu_custom_call" | custom-call | tf_op jit(solution)/shard_map/placed/pallas_call | solution.py:492
Async XLA Ops:
  1.4 24.9 %copy-start = (bf16[512,512]{1,0:T(8,128)(2,1)S(1)}, bf16[512,512]{1,0:T(8,128)(2,1)}, u32[]{:S(2)}) copy-start(bf16[512,512]{1,0:T(8,128)(2,1)} %constant.33.clone.high) | copy-start | bytes 1572868
  1.4 24.9 %copy-start.1 = (bf16[512,512]{1,0:T(8,128)(2,1)S(1)}, bf16[512,512]{1,0:T(8,128)(2,1)}, u32[]{:S(2)}) copy-start(bf16[512,512]{1,0:T(8,128)(2,1)} %constant.34.clone.low) | copy-start | bytes 1572868
  1.4 27.3 %copy-start.2 = (bf16[512,128]{1,0:T(8,128)(2,1)S(1)}, bf16[512,128]{1,0:T(8,128)(2,1)}, u32[]{:S(2)}) copy-start(bf16[512,128]{1,0:T(8,128)(2,1)} %constant.35.clone.refs_3_) | copy-start | bytes 393220
  1.4 27.3 %copy-start.3 = (bf16[512,128]{1,0:T(8,128)(2,1)S(1)}, bf16[512,128]{1,0:T(8,128)(2,1)}, u32[]{:S(2)}) copy-start(bf16[512,128]{1,0:T(8,128)(2,1)} %constant.36.clone.refs_4_) | copy-start | bytes 393220
  8.3 18.0 %all-to-all-start = ((f32[32,24,128]{2,1,0:T(8,128)}), f32[32,24,128]{2,1,0:T(8,128)S(1)}, u32[]{:S(2)}, u32[]{:S(2)}) async-start(f32[32,24,128]{2,1,0:T(8,128)} %get-tuple-element.20), calls=%async_computation | async-start | bytes 786432 | tf_op jit(solution)/shard_map/all_to_all | solution.py:611
  27.5 1.3 %collective-permute-start.4 = (f32[64,256]{1,0:T(8,128)S(1)}, f32[64,256]{1,0:T(8,128)S(1)}, u32[]{:S(2)}, u32[]{:S(2)}) collective-permute-start(f32[64,256]{1,0:T(8,128)S(1)} %get-tuple-element.26), channel_id=1, source_target_pairs={{0,1},{1,0},{2,3},{3,2},{4,5},{5,4},{6,7},{7,6},{8,9},{9,8},{10,11... | collective-permute-start | bytes 196616 | tf_op jit(solution)/shard_map/ppermute | solution.py:29
  30.6 28.2 %all-to-all-start.1 = ((f32[32,16,128]{2,1,0:T(8,128)}), f32[32,16,128]{2,1,0:T(8,128)S(1)}, u32[]{:S(2)}, u32[]{:S(2)}) async-start(f32[32,16,128]{2,1,0:T(8,128)} %along_x.1), calls=%async_computation.1 | async-start | bytes 524288 | tf_op jit(solution)/shard_map/all_to_all | solution.py:622
  34.5 13.7 %collective-permute-start = (f32[2,128,128]{2,1,0:T(8,128)S(1)}, f32[2,128,128]{2,1,0:T(8,128)S(1)}, u32[]{:S(2)}, u32[]{:S(2)}) collective-permute-start(f32[2,128,128]{2,1,0:T(8,128)S(1)} %get-tuple-element.16), channel_id=1, source_target_pairs={{4,0},{8,4},{12,8},{16,12},{20,16},{24,20},{28,24},{5,1},{9,5},{13... | collective-permute-start | bytes 393224 | tf_op jit(solution)/shard_map/ppermute | solution.py:24
  37.0 11.3 %collective-permute-start.1 = (f32[2,128,128]{2,1,0:T(8,128)S(1)}, f32[2,128,128]{2,1,0:T(8,128)S(1)}, u32[]{:S(2)}, u32[]{:S(2)}) collective-permute-start(f32[2,128,128]{2,1,0:T(8,128)S(1)} %get-tuple-element.17), channel_id=1, source_target_pairs={{0,4},{4,8},{8,12},{12,16},{16,20},{20,24},{24,28},{1,5},{5,9},{9,... | collective-permute-start | bytes 393224 | tf_op jit(solution)/shard_map/ppermute | solution.py:24
  41.3 4.3 %collective-permute-start.2 = (f32[2,16,128]{2,1,0:T(8,128)S(1)}, f32[2,16,128]{2,1,0:T(8,128)S(1)}, u32[]{:S(2)}, u32[]{:S(2)}) collective-permute-start(f32[2,16,128]{2,1,0:T(8,128)S(1)} %get-tuple-element.18), channel_id=1, source_target_pairs={{1,0},{2,1},{3,2},{5,4},{6,5},{7,6},{9,8},{10,9},{11,10},{13,12},{... | collective-permute-start | bytes 49160 | tf_op jit(solution)/shard_map/ppermute | solution.py:24
  43.2 5.1 %collective-permute-start.3 = (f32[2,16,128]{2,1,0:T(8,128)S(1)}, f32[2,16,128]{2,1,0:T(8,128)S(1)}, u32[]{:S(2)}, u32[]{:S(2)}) collective-permute-start(f32[2,16,128]{2,1,0:T(8,128)S(1)} %get-tuple-element.19), channel_id=1, source_target_pairs={{0,1},{1,2},{2,3},{4,5},{5,6},{6,7},{8,9},{9,10},{10,11},{12,13},{... | collective-permute-start | bytes 49160 | tf_op jit(solution)/shard_map/ppermute | solution.py:24

commit v4 on v3

--- a/solution.py
+++ b/solution.py
@@ -22,6 +22,12 @@
     devices = lax.axis_size(axis)
     pairs = [(i, i + by) for i in range(devices) if 0 <= i + by < devices]
     return lax.ppermute(value, axis, pairs)
+
+
+def traded(value, axis, odd):
+    devices = lax.axis_size(axis)
+    pairs = [(i, i + 1 if i % 2 == odd else i - 1) for i in range(devices)]
+    return lax.ppermute(value, axis, [(i, to) for i, to in pairs if 0 <= to < devices])
 
 
 def swapped(value, by):
@@ -188,77 +194,114 @@
     return pltpu.CompilerParams(vmem_limit_bytes=size * 1024 * 1024)
 
 
-def whole_smem():
-    return pl.BlockSpec(memory_space=pltpu.SMEM)
-
-
+PLACES = LANES // SUBLANES
 PICKED = ((0, -1, 3), (1, -1, 3), (2, -1, 2), (3, -1, 2), (4, -1, 2), (5, 0, 1), (6, 0, 1), (7, 0, 1))
 
 
+def arrivals(chunk, deep, sources, targets, arrived):
+    span = pl.ds(chunk * deep, deep)
+    pairs = []
+    for source, target in zip(sources, targets):
+        lead = [(i, span) for i in range(source.shape[0])] if len(source.shape) == 4 else [(span,)]
+        pairs += [(source.at[at], target.at[at]) for at in lead]
+    return [pltpu.make_async_copy(*pair, arrived.at[chunk, i]) for i, pair in enumerate(pairs)]
+
+
 def spread_kernel(
-    edge, cosine, sine, elec, magn, ret, coup, real_far, imag_far,
-    out, rows_elec, rows_magn, cols_elec, cols_magn, planes, edges, corners, real, imag, arrived,
+    phases_far, elec_far, magn_far, ret_far, coup_far, real_far, imag_far,
+    out_far, rows_first, rows_second, cols_first, cols_second, trig, known,
+    elec, magn, ret, coup, cols_elec, cols_magn, planes, ends, out, real, imag, phases, arrived, small, leaving,
 ):
-    step = pl.program_id(0)
-    steps = pl.num_programs(0)
-    deep = elec.shape[1]
-    rows = planes.shape[0]
+    chunks = arrived.shape[0]
+    rows = ret.shape[0]
+    deep = rows // chunks
+    freqs = real.shape[1]
+
+    def copies(chunk):
+        return arrivals(chunk, deep, (elec_far, magn_far, ret_far, coup_far), (elec, magn, ret, coup), arrived)
+
+    extras = [
+        pltpu.make_async_copy(phases_far, phases, small.at[0]),
+        pltpu.make_async_copy(real_far, real, small.at[1]),
+        pltpu.make_async_copy(imag_far, imag, small.at[2]),
+    ]
+    extras[0].start()
+    for chunk in range(chunks):
+        for copy in copies(chunk):
+            copy.start()
+    extras[1].start()
+    extras[2].start()
+    extras[0].wait()
+    turn_row = spot((SUBLANES, LANES), 0)
+    angle = jnp.zeros((SUBLANES, LANES), jnp.float32)
+    for freq in range(freqs):
+        angle = jnp.where(turn_row == freq, phases[freq], angle)
+    trig[0] = jnp.cos(angle)
+    trig[1] = jnp.sin(angle)
     lane = spot((LANES, LANES), 1)
-    for at in range(deep):
+
+    packed = None
+    for at in range(rows):
+        if at % deep == 0:
+            for copy in copies(at // deep):
+                copy.wait()
         arrays = [elec[0, at], elec[1, at], elec[2, at], magn[0, at], magn[1, at], magn[2, at], ret[at], coup[at]]
-        packed = None
-        start = 0
+        start = at % SUBLANES * PLACES
         for which, first, count in PICKED:
             turned = moved(arrays[which], start - TOP_PLANE - first, 1)
             packed = turned if packed is None else jnp.where(lane < start, packed, turned)
             start += count
-        planes[step * deep + at] = packed.T[0:16]
-        edges[0, pl.ds(step * deep + at, 1), :] = elec[0, at, -1:, :]
-        edges[1, pl.ds(step * deep + at, 1), :] = elec[1, at, -1:, :]
-        edges[2, pl.ds(step * deep + at, 1), :] = magn[2, at, -1:, :]
-        cols_elec[0, pl.ds(step * deep + at, 1), :] = elec[0, at, 0:1, :]
-        cols_elec[1, pl.ds(step * deep + at, 1), :] = elec[2, at, 0:1, :]
+        if at % SUBLANES == SUBLANES - 1:
+            planes[at // SUBLANES] = packed.T
+            packed = None
+        ends[0, at : at + 1, :] = elec[0, at, -1:, :]
+        ends[1, at : at + 1, :] = elec[1, at, -1:, :]
+        ends[2, at : at + 1, :] = magn[2, at, -1:, :]
+        cols_elec[0, at : at + 1, :] = elec[0, at, 0:1, :]
+        cols_elec[1, at : at + 1, :] = elec[2, at, 0:1, :]
         line = elec[1, at, -1:, :]
-        cols_magn[0, pl.ds(step * deep + at, 1), :] = (
+        cols_magn[0, at : at + 1, :] = (
             magn[0, at, -1:, :] + curl_step * elec[2, at, -1:, :] + curl_step * (after(line, 1) - line)
         )
 
-    real_copy = pltpu.make_async_copy(real_far, real, arrived.at[0])
-    imag_copy = pltpu.make_async_copy(imag_far, imag, arrived.at[1])
-
-    @pl.when(step == 0)
-    def _():
-        real_copy.start()
-        imag_copy.start()
-        rows_elec[0] = elec[1, 0]
-        rows_elec[1] = elec[2, 0]
-        corners[0:1, :] = elec[1, 0, -1:, :]
-
-    @pl.when(step == steps - 1)
-    def _():
-        last = deep - 1
-        ex, ey, ez = elec[0, last], elec[1, last], elec[2, last]
-        rows_magn[0] = magn[1, last] - curl_step * (after(ex, 1) - ex) - curl_step * ez
-        rows_magn[1] = magn[2, last] + curl_step * ey + curl_step * (after(ex, 0) - ex)
-        corners[1:2, :] = elec[0, last, 0:1, :]
-        end_x, end_y, end_z = edges[0], edges[1], edges[2]
-        cols_magn[1] = end_z - curl_step * (after(end_y, 0) - end_y) - curl_step * end_x
-
+    last = rows - 1
+    ex, ey, ez = elec[0, last], elec[1, last], elec[2, last]
+    upward = (elec[1, 0], elec[2, 0])
+    downward = (
+        magn[1, last] - curl_step * (after(ex, 1) - ex) - curl_step * ez,
+        magn[2, last] + curl_step * ey + curl_step * (after(ex, 0) - ex),
+    )
+    even = lax.axis_index("gx") % 2 == 0
+    for i in range(2):
+        rows_first[i] = jnp.where(even, downward[i], upward[i])
+        rows_second[i] = jnp.where(even, upward[i], downward[i])
+    end_x, end_y, end_z = ends[0], ends[1], ends[2]
+    cols_magn[1] = end_z - curl_step * (after(end_y, 0) - end_y) - curl_step * end_x
+    even = lax.axis_index("gy") % 2 == 0
+    cols_first[...] = jnp.where(even, cols_magn[...], cols_elec[...])
+    cols_second[...] = jnp.where(even, cols_elec[...], cols_magn[...])
+    corner_up, corner_down = elec[1, 0, -1:, :], elec[0, last, 0:1, :]
+
+    if rows:
         ex_m, ex_p, ex_q, ey_m, ey_p, ey_q, ez_m, ez_p, hx_m, hx_p, hy_m, hy_p, hz_p, keep, gain = (
-            planes[:, which, :] for which in range(15)
+            jnp.concatenate([planes[group, pl.ds(which, SUBLANES, stride=PLACES), :] for group in range(rows // SUBLANES)])
+            for which in range(15)
         )
         hx_p = hx_p - curl_step * ((after(ez_p, 1) - ez_p) - (ey_q - ey_p))
         hx_m = hx_m - curl_step * ((after(ez_m, 1) - ez_m) - (ey_p - ey_m))
         hy_p = hy_p - curl_step * ((ex_q - ex_p) - (after(ez_p, 0) - ez_p))
         hy_m = hy_m - curl_step * ((ex_p - ex_m) - (after(ez_m, 0) - ez_m))
         hz_p = hz_p - curl_step * ((after(ey_p, 0) - ey_p) - (after(ex_p, 1) - ex_p))
-        edge_x, edge_y = curl_step * edge[0], curl_step * edge[1]
+        edge_x = jnp.where(lax.axis_index("gx") > 0, curl_step, 0.0)
+        edge_y = jnp.where(lax.axis_index("gy") > 0, curl_step, 0.0)
         tangent = (
             keep * ex_p + gain * ((hz_p - before(hz_p, 1, edge_y * ex_p)) - (hy_p - hy_m)),
             keep * ey_p + gain * ((hx_p - hx_m) - (hz_p - before(hz_p, 0, -edge_x * ey_p))),
             hx_p,
             hy_p,
         )
+        for which, value in enumerate((*tangent, gain)):
+            known[which] = value
         ez_jump = curl_step * (ez_p - ez_m)
         push = -curl_step * ey_p
         none = jnp.zeros_like(ex_p)
@@ -285,8 +328,9 @@
             return jnp.concatenate([block, pad], axis=0).T[0:SUBLANES]
 
         end = LANES - 1
-        real_copy.wait()
-        imag_copy.wait()
+        extras[1].wait()
+        extras[2].wait()
+        departures = []
         for comp in range(4):
             factor = gain if comp < 2 else one
             columns = upright([(col_left[comp], 0), (col_right[comp], end), (factor, end), (factor, 0)])
@@ -299,45 +343,62 @@
             extra = jnp.where(tall == 2, factor[rows - 1 :], extra)
             extra = jnp.where(tall == 3, factor[0:1], extra)
             extra = jnp.where(tall == 4, columns, extra)
-            extra = jnp.where(tall == 5, corners[0:1, :], extra)
-            extra = jnp.where(tall == 6, corners[1:2, :], extra)
-            freqs = real.shape[1]
+            extra = jnp.where(tall == 5, corner_up, extra)
+            extra = jnp.where(tall == 6, corner_down, extra)
             for freq in range(freqs):
-                new_real = real[comp, freq] + tangent[comp] * cosine[freq]
-                new_imag = imag[comp, freq] - tangent[comp] * sine[freq]
+                new_real = real[comp, freq] + tangent[comp] * trig[0, freq : freq + 1, :]
+                new_imag = imag[comp, freq] - tangent[comp] * trig[1, freq : freq + 1, :]
                 for half in range(2):
                     to = (comp * freqs + freq) * 2 + half
                     out[to, 0:8] = new_real[half * 8 : half * 8 + 8]
                     out[to, 8:16] = new_imag[half * 8 : half * 8 + 8]
                     out[to, 16:24] = extra
-
-
-def spread(edge, electric, magnetic, retention, coupling, spectrum_real, spectrum_imag, cosine, sine):
+            span = pl.ds(comp * freqs * 2, freqs * 2)
+            departures.append(pltpu.make_async_copy(out.at[span], out_far.at[span], leaving.at[comp]))
+            departures[-1].start()
+        for departure in departures:
+            departure.wait()
+
+
+def spread(electric, magnetic, retention, coupling, spectrum_real, spectrum_imag, phases):
     _, rows, cols, deep = electric.shape
     comps, freqs = spectrum_real.shape[:2]
-    slab = 4
-    vector = pl.BlockSpec((3, slab, cols, deep), lambda i: (0, i, 0, 0))
-    scalar = pl.BlockSpec((slab, cols, deep), lambda i: (i, 0, 0))
-    kind = jnp.float32
+    chunks = 4
+    sent = (comps * freqs * 2, 24, cols)
+    inputs = (phases, electric, magnetic, retention, coupling, spectrum_real, spectrum_imag)
     return pl.pallas_call(
         spread_kernel,
-        grid=(rows // slab,),
-        in_specs=[whole_smem(), whole_smem(), whole_smem(), vector, vector, scalar, scalar] + [pl.BlockSpec(memory_space=pl.ANY)] * 2,
-        out_specs=[whole_vmem()] * 5,
+        in_specs=[pl.BlockSpec(memory_space=pl.ANY)] * 7,
+        out_specs=[pl.BlockSpec(memory_space=pl.ANY)] + [whole_vmem()] * 6,
         compiler_params=limited(),
         out_shape=[
-            pltpu.HBM((comps * freqs * 2, 24, cols), kind),
+            pltpu.HBM(sent, jnp.float32),
             room((2, cols, deep)),
             room((2, cols, deep)),
             room((2, rows, deep)),
             room((2, rows, deep)),
+            room((2, SUBLANES, LANES)),
+            room((comps + 1, rows, cols)),
         ],
         scratch_shapes=[
-            room((rows, 16, LANES)), room((3, rows, LANES)), room((2, LANES)),
-            room(spectrum_real.shape), room(spectrum_imag.shape), pltpu.SemaphoreType.DMA((2,)),
+            room(electric.shape),
+            room(magnetic.shape),
+            room(retention.shape),
+            room(coupling.shape),
+            room((2, rows, deep)),
+            room((2, rows, deep)),
+            room((rows // SUBLANES, LANES, LANES)),
+            room((3, rows, LANES)),
+            room(sent),
+            room(spectrum_real.shape),
+            room(spectrum_imag.shape),
+            pltpu.SMEM((freqs,), jnp.float32),
+            pltpu.SemaphoreType.DMA((chunks, 8)),
+            pltpu.SemaphoreType.DMA((3,)),
+            pltpu.SemaphoreType.DMA((comps,)),
         ],
         name="spread",
-    )(edge, cosine, sine, *(far_kept(a) for a in (electric, magnetic, retention, coupling, spectrum_real, spectrum_imag)))
+    )(*(far_kept(value) for value in inputs))
 
 
 def split_high(value):
@@ -349,13 +410,15 @@
     return jnp.dot(a, b, preferred_element_type=jnp.float32)
 
 
-def along_y_kernel(at, cosine, sine, got, high, low, mine, other, lines):
+def along_y_kernel(got, trig, high, low, mine, other, lines):
     along_x, along_y = got.shape[0], got.shape[1]
     blocks = along_x * along_y
-    half = at[0] % 2
-    freq = (at[0] // 2) % cosine.shape[0]
-    weight_real = cosine[freq]
-    weight_imag = -sine[freq]
+    at = lax.axis_index(BOTH)
+    half = at % 2
+    freqs = got.shape[0] * got.shape[1] // 8
+    freq = (at // 2) % freqs
+    weight_real = trig[0, pl.ds(freq, 1), :]
+    weight_imag = -trig[1, pl.ds(freq, 1), :]
     is_last = jnp.where(half == 1, 1.0, 0.0)
     is_first = jnp.where(half == 0, 1.0, 0.0)
 
@@ -370,7 +433,7 @@
 
     from_right = jnp.where(inner == along_y - 1, 0.0, moved(packed, -1, 0))
     from_left = jnp.where(inner == 0, 0.0, moved(packed, 1, 0))
-    comp = at[0] // (2 * cosine.shape[0])
+    comp = at // (2 * freqs)
     right_up = jnp.where((block >= along_y) & (comp == 1), moved(from_right, along_y, 0), 0.0)
     left_down = jnp.where((block < blocks - along_y) & (comp == 0), moved(from_left, -along_y, 0), 0.0)
     from_right = lines_at(from_right, 0) + jnp.where(lane == 0, moved(right_up, -4 * rows, 1), 0.0)
@@ -414,7 +477,7 @@
         other[span, piece:] = jnp.where(half == 0, new_imag[:, piece:], new_imag[:, :piece])
 
 
-def along_y_sums(place, cosine, sine, got, cols, along_x, along_y):
+def along_y_sums(got, trig, cols, along_x, along_y):
     wide = WAVES // along_y
     order = np.arange(WAVES).reshape(along_y, 2, wide // 2).transpose(1, 0, 2).reshape(-1)
     cos_y, sin_y = wave_tables(WAVES, cols * along_y)
@@ -422,17 +485,17 @@
     shape = room((along_x * 8, WAVES))
     return pl.pallas_call(
         along_y_kernel,
-        in_specs=[whole_smem()] * 3 + [whole_vmem()] * 3,
+        in_specs=[whole_vmem()] * 4,
         out_specs=[whole_vmem()] * 2,
         out_shape=[shape, shape],
         scratch_shapes=[room((along_x * 16, along_y * LANES))],
         compiler_params=limited(),
         name="along_y",
-    )(place, cosine, sine, kept(got.reshape(along_x, along_y, 24, cols)), kept(high), kept(low))
-
-
-def along_x_kernel(along_x, at, mine, other, high, low, out):
-    half = at[0] % 2
+    )(kept(got.reshape(along_x, along_y, 24, cols)), kept(trig), kept(high), kept(low))
+
+
+def along_x_kernel(along_x, mine, other, high, low, out):
+    half = lax.axis_index(BOTH) % 2
     lines = jnp.concatenate(
         [jnp.where(half == 0, mine[...], other[...]), jnp.where(half == 0, other[...], mine[...])], axis=0
     )
@@ -460,19 +523,19 @@
                 out[x * along_y + y, part * 8 : part * 8 + 8] = block
 
 
-def along_x_sums(place, mine, other, rows, scale, along_x, devices):
+def along_x_sums(mine, other, rows, scale, along_x, devices):
     cos_x, sin_x = wave_tables(WAVES, rows * along_x)
     table = np.concatenate([cos_x, sin_x], axis=0) * scale
     table = table.reshape(2 * WAVES, along_x, 2, 8).transpose(0, 2, 1, 3).reshape(2 * WAVES, rows * along_x)
     high, low = in_two(table)
     return pl.pallas_call(
         lambda *refs: along_x_kernel(along_x, *refs),
-        in_specs=[whole_smem()] + [whole_vmem()] * 4,
+        in_specs=[whole_vmem()] * 4,
         out_specs=whole_vmem(),
         out_shape=pltpu.HBM((devices, 16, LANES), jnp.float32),
         compiler_params=limited(),
         name="along_x",
-    )(place, kept(mine), kept(other), kept(high), kept(low))
+    )(kept(mine), kept(other), kept(high), kept(low))
 
 
 def placed_kernel(got, out):
@@ -501,96 +564,169 @@
 
 
 def yee_kernel(
-    edge, place, cosine, sine, elec, ahead, magn, ret, coup, rows_elec, rows_magn, cols_elec, cols_magn, got,
-    real, imag, new_elec, new_magn, new_real, new_imag, carried, tops,
+    elec_far, magn_far, ret_far, coup_far, rows_first, rows_second, cols_first, cols_second, got, trig, known, real, imag,
+    new_elec, new_magn, new_real, new_imag, elec, magn, ret, coup, carried, side, arrived,
+    rows_elec, rows_magn, cols_elec, cols_magn,
 ):
     step = pl.program_id(0)
     steps = pl.num_programs(0)
-    deep = elec.shape[1]
-    inner_x = edge[0]
-    inner_y = edge[1]
-    corner_up = got[place[1], 21:22, :] * edge[2]
-    corner_down = got[place[2], 22:23, :] * edge[3]
+    rows, cols = ret.shape[:2]
+    deep = new_elec.shape[1]
+    at_x, at_y = lax.axis_index("gx"), lax.axis_index("gy")
+    along_x, along_y = lax.axis_size("gx"), lax.axis_size("gy")
+    here = lax.axis_index(BOTH)
+    up = jnp.minimum(here + along_y - 1, along_x * along_y - 1)
+    down = jnp.maximum(here - along_y + 1, 0)
+    inner_x = jnp.where(at_x > 0, 1.0, 0.0)
+    inner_y = jnp.where(at_y > 0, 1.0, 0.0)
+    corner_up = got[pl.ds(up, 1), 21, :] * jnp.where((at_x + 1 < along_x) & (at_y > 0), curl_step, 0.0)
+    corner_down = got[pl.ds(down, 1), 22, :] * jnp.where((at_x > 0) & (at_y + 1 < along_y), curl_step, 0.0)
     row = spot((LANES, LANES), 0)
     lane = spot((LANES, LANES), 1)
+    chunks = arrived.shape[0]
+    thick = rows // chunks
+    front = SUBLANES
+
+    def copies(chunk):
+        return arrivals(
+            chunk, thick, (elec_far, magn_far, ret_far, coup_far), (elec.at[:, :, 0:cols], magn, ret, coup), arrived
+        )
 
     @pl.when(step == 0)
     def _():
-        spare = jnp.where(row == LANES - 1, curl_step * corner_down, 0.0)
-        carried[0] = (rows_magn[0] + curl_step * elec[2, 0]) * inner_x
-        carried[1] = (rows_magn[1] - curl_step * elec[1, 0] + spare) * inner_x
+        for chunk in range(chunks):
+            for copy in copies(chunk):
+                copy.start()
+        even = at_x % 2 == 0
+        rows_elec[...] = jnp.where(even, rows_first[...], rows_second[...])
+        rows_magn[...] = jnp.where(even, rows_second[...], rows_first[...])
+        even = at_y % 2 == 0
+        cols_elec[...] = jnp.where(even, cols_first[...], cols_second[...])
+        cols_magn[...] = jnp.where(even, cols_second[...], cols_first[...])
+        for at in range(rows):
+            elec[0, at, cols : cols + 1, :] = cols_elec[0, at : at + 1, :]
+            elec[2, at, cols : cols + 1, :] = cols_elec[1, at : at + 1, :]
+
+        lines = None
+        for which, (value, plane) in enumerate(((rows_elec[0], 0), (rows_elec[1], 0), (rows_elec[1], -1), (rows_magn[1], 0))):
+            turned = moved(value, which - TOP_PLANE - plane, 1)
+            lines = turned if lines is None else jnp.where(lane < which, lines, turned)
+        lines = lines.T
+        ey_row, ez_row, ez_row_below, hz_row = (lines[which : which + 1] for which in range(4))
+        ey_row, ez_row, ez_row_below = curl_step * ey_row, curl_step * ez_row, curl_step * ez_row_below
+        tall = spot((rows, LANES), 0)
+        wide = spot((rows, LANES), 1)
+        end = LANES - 1
+
+        def at_right(value, plane=0):
+            return jnp.where(wide == end, moved(value, end - TOP_PLANE - plane, 1), 0.0)
+
+        def at_left(value):
+            return jnp.where(wide == 0, moved(value, -TOP_PLANE, 1), 0.0)
+
+        ex_right = curl_step * at_right(cols_elec[0])
+        ez_right = curl_step * at_right(cols_elec[1])
+        ez_right_below = curl_step * at_right(cols_elec[1], -1)
+        corner_left = jnp.where(wide[0:1] == 0, moved(corner_up, -TOP_PLANE, 1), 0.0)
+        corner_right = jnp.where(wide[0:1] == end, moved(corner_down, end - TOP_PLANE, 1), 0.0)
+        ey_row_left = before(ey_row, 1) + corner_left
+        gain = known[4]
+        push_x = ex_right - at_left(cols_magn[1]) * inner_y
+        push_x = push_x + jnp.where(tall == rows - 1, ey_row_left - ey_row - (ez_row - ez_row_below), 0.0)
+        push_y = before(ex_right, 0) - ex_right - (ez_right - ez_right_below)
+        push_y = push_y + jnp.where(tall == rows - 1, ey_row, 0.0)
+        push_y = push_y + jnp.where(tall == 0, hz_row * inner_x + corner_right, 0.0)
+        tangents = (
+            known[0] + gain * push_x,
+            known[1] + gain * push_y,
+            known[2] - ez_right,
+            known[3] + jnp.where(tall == rows - 1, ez_row, 0.0),
+        )
+        for comp, tangent in enumerate(tangents):
+            for freq in range(real.shape[1]):
+                new_real[comp, freq] = real[comp, freq] + tangent * trig[0, freq : freq + 1, :]
+                new_imag[comp, freq] = imag[comp, freq] - tangent * trig[1, freq : freq + 1, :]
+
+        for copy in copies(0):
+            copy.wait()
+        spare = jnp.where(row == cols - 1, corner_down, 0.0)
+        carried[0] = (rows_magn[0] + curl_step * elec[2, 0, 0:cols]) * inner_x
+        carried[1] = (rows_magn[1] - curl_step * elec[1, 0, 0:cols] + spare) * inner_x
+
+    ahead = (step + 1) * deep
+
+    @pl.when((ahead % thick == 0) & (ahead < rows))
+    def _():
+        for copy in copies(ahead // thick):
+            copy.wait()
 
     at_end = step == steps - 1
-    for at in range(deep):
-        here = pl.ds(step * deep + at, 1)
-        ex, ey, ez = elec[0, at], elec[1, at], elec[2, at]
-        if at + 1 < deep:
-            ey_next, ez_next = elec[1, at + 1], elec[2, at + 1]
+    for inner in range(deep):
+        at = step * deep + inner
+        line = pl.ds(at, 1)
+        ex, ey, ez = elec[0, at, 0:cols], elec[1, at, 0:cols], elec[2, at, 0:cols]
+        if inner + 1 < deep:
+            ey_next, ez_next = elec[1, at + 1, 0:cols], elec[2, at + 1, 0:cols]
         else:
-            ey_next = jnp.where(at_end, rows_elec[0], ahead[1, 0])
-            ez_next = jnp.where(at_end, rows_elec[1], ahead[2, 0])
-        hx = magn[0, at] - curl_step * ((after(ez, 0, cols_elec[1, here, :]) - ez) - (after(ey, 1) - ey))
+            then = jnp.minimum(at + 1, rows - 1)
+            ey_next = jnp.where(at_end, rows_elec[0], elec[1, then, 0:cols])
+            ez_next = jnp.where(at_end, rows_elec[1], elec[2, then, 0:cols])
+        hx = magn[0, at] - curl_step * ((elec[2, at, 1 : cols + 1] - ez) - (after(ey, 1) - ey))
         hy = magn[1, at] - curl_step * ((after(ex, 1) - ex) - (ez_next - ez))
-        hz = magn[2, at] - curl_step * ((ey_next - ey) - (after(ex, 0, cols_elec[0, here, :]) - ex))
-        new_magn[0, at] = hx
-        new_magn[1, at] = hy
-        new_magn[2, at] = hz
-        side_x = (cols_magn[0, here, :] - curl_step * ez[0:1]) * inner_y
-        side_z = cols_magn[1, here, :] + curl_step * ex[0:1]
-        if at + 1 == deep:
-            side_z = side_z - jnp.where(at_end, curl_step * corner_up, 0.0)
-        side_z = side_z * inner_y
+        hz = magn[2, at] - curl_step * ((ey_next - ey) - (elec[0, at, 1 : cols + 1] - ex))
+        new_magn[0, inner] = hx
+        new_magn[1, inner] = hy
+        new_magn[2, inner] = hz
+        side_x = (cols_magn[0, line, :] - curl_step * ez[0:1]) * inner_y
+        side_z = cols_magn[1, line, :] + curl_step * ex[0:1]
+        if inner + 1 == deep:
+            side_z = side_z - jnp.where(at_end, corner_up, 0.0)
+        side[0, front - 1 : front, :] = side_x
+        side[1, front - 1 : front, :] = side_z * inner_y
+        side[0, front : front + cols, :] = hx
+        side[1, front : front + cols, :] = hz
+        hx_before, hz_before = side[0, front - 1 : front + cols - 1, :], side[1, front - 1 : front + cols - 1, :]
         keep, gain = ret[at], coup[at]
-        new_x = keep * ex + gain * ((hz - before(hz, 0, side_z)) - (hy - before(hy, 1)))
-        new_y = keep * ey + gain * ((hx - before(hx, 1)) - (hz - carried[1]))
-        new_z = keep * ez + gain * ((hy - carried[0]) - (hx - before(hx, 0, side_x)))
-        new_elec[0, at] = new_x
-        new_elec[1, at] = new_y
-        new_elec[2, at] = new_z
+        new_elec[0, inner] = keep * ex + gain * ((hz - hz_before) - (hy - before(hy, 1)))
+        new_elec[1, inner] = keep * ey + gain * ((hx - before(hx, 1)) - (hz - carried[1]))
+        new_elec[2, inner] = keep * ez + gain * ((hy - carried[0]) - (hx - hx_before))
         carried[0] = hy
         carried[1] = hz
-        packed = None
-        for which, value in enumerate((new_x, new_y, hx, hy)):
-            turned = moved(value, which - TOP_PLANE, 1)
-            packed = turned if packed is None else jnp.where(lane < which, packed, turned)
-        tops[step * deep + at] = packed.T[0:SUBLANES]
-
-    @pl.when(at_end)
-    def _():
-        for comp in range(4):
-            tangent = tops[:, comp, :]
-            for freq in range(real.shape[1]):
-                new_real[comp, freq] = real[comp, freq] + tangent * cosine[freq]
-                new_imag[comp, freq] = imag[comp, freq] - tangent * sine[freq]
-
-
-def yee(edge, place, cosine, sine, electric, magnetic, retention, coupling, halos, got, spectrum_real, spectrum_imag):
-    _, rows, cols, deep = electric.shape
-    slab = 2
-    steps = rows // slab
+
+
+def yee(fields, halos, got, trig, known, spectrum_real, spectrum_imag):
+    _, rows, cols, deep = fields[0].shape
+    slab, chunks = 2, 4
     vector = pl.BlockSpec((3, slab, cols, deep), lambda i: (0, i, 0, 0))
-    ahead = pl.BlockSpec((3, 1, cols, deep), lambda i: (0, jnp.minimum((i + 1) * slab, rows - 1), 0, 0))
-    scalar = pl.BlockSpec((slab, cols, deep), lambda i: (i, 0, 0))
     kind = jnp.float32
     return pl.pallas_call(
         yee_kernel,
-        grid=(steps,),
-        in_specs=[whole_smem()] * 4 + [vector, ahead, vector, scalar, scalar] + [whole_vmem()] * 7,
-        compiler_params=limited(),
+        grid=(rows // slab,),
+        in_specs=[pl.BlockSpec(memory_space=pl.ANY)] * 4 + [whole_vmem()] * 9,
+        compiler_params=limited(32),
         out_specs=[vector, vector, whole_vmem(), whole_vmem()],
         out_shape=[
-            jax.ShapeDtypeStruct(electric.shape, kind),
-            jax.ShapeDtypeStruct(magnetic.shape, kind),
+            jax.ShapeDtypeStruct(fields[0].shape, kind),
+            jax.ShapeDtypeStruct(fields[1].shape, kind),
             jax.ShapeDtypeStruct(spectrum_real.shape, kind),
             jax.ShapeDtypeStruct(spectrum_imag.shape, kind),
         ],
-        scratch_shapes=[pltpu.VMEM((2, cols, deep), kind), pltpu.VMEM((rows, SUBLANES, LANES), kind)],
-        cost_estimate=pl.CostEstimate(flops=60 * electric.size, bytes_accessed=20 * electric.size, transcendentals=0),
+        scratch_shapes=[
+            room((3, rows, cols + SUBLANES, deep)),
+            *(room(field.shape) for field in fields[1:]),
+            room((2, cols, deep)),
+            room((2, cols + SUBLANES, deep)),
+            pltpu.SemaphoreType.DMA((chunks, 8)),
+            room((2, cols, deep)),
+            room((2, cols, deep)),
+            room((2, rows, deep)),
+            room((2, rows, deep)),
+        ],
+        cost_estimate=pl.CostEstimate(flops=60 * fields[0].size, bytes_accessed=8 * fields[0].size, transcendentals=0),
         name="yee",
     )(
-        edge, place, cosine, sine,
-        *(far_kept(a) for a in (electric, electric, magnetic, retention, coupling)),
-        *(kept(halo) for halo in halos), kept(got), far_kept(spectrum_real), far_kept(spectrum_imag),
+        *(far_kept(field) for field in fields), *(kept(value) for value in (*halos, got, trig, known)),
+        far_kept(spectrum_real), far_kept(spectrum_imag),
     )
 
 
@@ -598,31 +734,19 @@
     comps, freqs, rows, cols = spectrum_real.shape
     along_x, along_y = lax.axis_size("gx"), lax.axis_size("gy")
     devices = along_x * along_y
-    cosine, sine = jnp.cos(phases), jnp.sin(phases)
-    at_x, at_y = lax.axis_index("gx"), lax.axis_index("gy")
-    here = lax.axis_index(BOTH)
-    inner = (at_x > 0, at_y > 0, (at_x + 1 < along_x) & (at_y > 0), (at_x > 0) & (at_y + 1 < along_y))
-    edge = jnp.stack(inner).astype(jnp.float32)
-    up, down = jnp.minimum(here + along_y - 1, devices - 1), jnp.maximum(here - along_y + 1, 0)
-    place = jnp.stack([here, up, down]).astype(jnp.int32)
-    sent, rows_elec, rows_magn, cols_elec, cols_magn = spread(
-        edge, electric, magnetic, retention, coupling, spectrum_real, spectrum_imag, cosine, sine
+    sent, rows_first, rows_second, cols_first, cols_second, trig, known = spread(
+        electric, magnetic, retention, coupling, spectrum_real, spectrum_imag, phases
     )
     got = lax.all_to_all(sent, BOTH, split_axis=0, concat_axis=0, tiled=True)
-    halos = (
-        passed_along(rows_elec, "gx", -1),
-        passed_along(rows_magn, "gx", 1),
-        passed_along(cols_elec, "gy", -1),
-        passed_along(cols_magn, "gy", 1),
-    )
-    mine, other = along_y_sums(place, cosine, sine, got, cols, along_x, along_y)
+    rows_traded = (traded(rows_first, "gx", 0), traded(rows_second, "gx", 1))
+    halos = (*rows_traded, traded(cols_first, "gy", 0), traded(cols_second, "gy", 1))
+    mine, other = along_y_sums(got, trig, cols, along_x, along_y)
     other = swapped(other, 1)
     scale = 1.0 / math.sqrt(rows * along_x * cols * along_y)
-    far = along_x_sums(place, mine, other, rows, scale, along_x, devices)
+    far = along_x_sums(mine, other, rows, scale, along_x, devices)
     far = lax.all_to_all(far, BOTH, split_axis=0, concat_axis=0, tiled=True)
     next_electric, next_magnetic, next_real, next_imag = yee(
-        edge, place, cosine, sine, electric, magnetic, retention, coupling, halos, got,
-        spectrum_real, spectrum_imag,
+        (electric, magnetic, retention, coupling), halos, got, trig, known, spectrum_real, spectrum_imag
     )
     far_field = placed_far(far, comps, freqs, WAVES // along_x, WAVES // along_y)
     return (next_electric, next_magnetic, next_real, next_imag, far_field)

time: 60.4 us -> 52.8 us (0.87)
  the two profiles are of different devices: /device:TPU:6 before, /device:TPU:0 now
where the time goes in v4:
time: 52.8 us; the launch traced here: 52.5 us
  blocking collectives  20.6 us (39%)
  Pallas kernels  17.3 us (33%)
  waiting for transfers between devices  8 us (15%)
  starting transfers between devices  5.83 us (11%)
  between operations  0.74 us (1%)
    all_to_all x1, blocking collectives, tiled_step(): got = lax.all_to_all(sent, BOTH, split_axis=0, concat_axis=0, tiled=True)  20.6 us
    pallas_call x1, Pallas kernels, yee(): pl.pallas_call(yee_kernel, grid=(rows // slab,), in_specs=[pl.BlockSpec(m...  8.53 us
    ppermute x4, waiting for transfers between devices, traded(): lax.ppermute(value, axis, [(i, to) for i, to in pairs if 0 <= to < devices])  6.76 us
    pallas_call x1, Pallas kernels, spread(): pl.pallas_call(spread_kernel, in_specs=[pl.BlockSpec(memory_space=pl.ANY)...  5.83 us
    ppermute x4, starting transfers between devices, traded(): lax.ppermute(value, axis, [(i, to) for i, to in pairs if 0 <= to < devices])  3.17 us
    all_to_all x1, starting transfers between devices, tiled_step(): far = lax.all_to_all(far, BOTH, split_axis=0, concat_axis=0, tiled=True)  2.59 us
    pallas_call x1, Pallas kernels, along_x_sums(): pl.pallas_call(lambda *refs: along_x_kernel(along_x, *refs), in_specs=[wh...  1.28 us
    ppermute x1, waiting for transfers between devices, swapped(): return lax.ppermute(value, BOTH, [(i, i ^ by) for i in range(devices)])  1.24 us
  transfers between devices with their start and end apart: 6, of which 3 were waited for; matrix products, arithmetic and copies ran while one was open for 0% of the time, Pallas kernels for 16%

profile of v4, /device:TPU:0, one launch (start us, length us, event | category | flops | bytes accessed | tf_op | source)
XLA Modules:
  0.0 52.5 jit_solution(8097093971243775658)
XLA Ops:
  0.6 0.0 copy-start
  0.6 0.0 copy-start.1
  0.7 0.0 copy-start.2
  0.7 0.0 copy-start.3
  0.7 5.8 %spread.1 = (f32[32,24,128]{2,1,0:T(8,128)}, f32[2,128,128]{2,1,0:T(8,128)S(1)}, f32[2,128,128]{2,1,0:T(8,128)S(1)}, f32[2,16,128]{2,1,0:T(8,128)S(1)}, f32[2,16...) custom-call(f32[4]{0:T(128)} %phases_far.1, f32[3,16,128,128]{3,2,1,0:T(8,128)} %elec_far.3, ...), custom_call_target="tpu_custom_call" | custom-call | tf_op jit(solution)/shard_map/spread/pallas_call | solution.py:369
  6.5 20.6 %all_to_all.10.got = f32[32,24,128]{2,1,0:T(8,128)S(1)} all-to-all(f32[32,24,128]{2,1,0:T(8,128)} %get-tuple-element.22), channel_id=1, replica_groups=mesh['gx'=8,'gy'=4] {'gx','gy'}, dimensions={0} | all-to-all | bytes 786432 | tf_op jit(solution)/shard_map/all_to_all | solution.py:740
  27.1 0.0 copy-done
  27.1 0.0 copy-done.1
  27.1 0.6 %along_y.1 = (f32[64,256]{1,0:T(8,128)S(1)}, f32[64,256]{1,0:T(8,128)S(1)}) custom-call(f32[8,4,24,128]{3,2,1,0:T(8,128)S(1)} %bitcast.2, f32[2,8,128]{2,1,0:T(8,128)S(1)} %get-tuple-element.23.trig, bf16[512,512]{1,0:T(8,128)(2,1)S(1)} %copy-done, bf16[512,512]{1,0:T(8,128)(2,1)S(1)} %copy-done.1), custom_call_target="tpu_custom_call" | custom-call | tf_op jit(solution)/shard_map/along_y/pallas_call | solution.py:486
  27.7 0.1 collective-permute-start.4
  27.8 1.2 %collective-permute-done.4.refs_1_ = f32[64,256]{1,0:T(8,128)S(1)} collective-permute-done((f32[64,256]{1,0:T(8,128)S(1)}, f32[64,256]{1,0:T(8,128)S(1)}, u32[]{:S(2)}, u32[]{:S(2)}) %collective-permute-start.4) | collective-permute-done | bytes 65568 | tf_op jit(solution)/shard_map/ppermute | solution.py:35
  29.0 0.0 copy-done.2
  29.0 0.0 copy-done.3
  29.0 1.3 %along_x.1 = f32[32,16,128]{2,1,0:T(8,128)} custom-call(f32[64,256]{1,0:T(8,128)S(1)} %get-tuple-element.29.refs_0_, f32[64,256]{1,0:T(8,128)S(1)} %collective-permute-done.4.refs_1_, bf16[512,128]{1,0:T(8,128)(2,1)S(1)} %copy-done.2, bf16[512,128]{1,0:T(8,128)(2,1)S(1)} %copy-done.3), custom_call_target="tpu_custom_call" | custom-call | tf_op jit(solution)/shard_map/along_x/pallas_call | solution.py:531
  30.3 2.6 %all-to-all-start.1 = ((f32[32,16,128]{2,1,0:T(8,128)}), f32[32,16,128]{2,1,0:T(8,128)S(1)}, u32[]{:S(2)}, u32[]{:S(2)}) async-start(f32[32,16,128]{2,1,0:T(8,128)} %along_x.1), calls=%async_computation.1 | async-start | bytes 524288 | tf_op jit(solution)/shard_map/all_to_all | solution.py:747
  32.9 1.8 %collective-permute-start = (f32[2,128,128]{2,1,0:T(8,128)S(1)}, f32[2,128,128]{2,1,0:T(8,128)S(1)}, u32[]{:S(2)}, u32[]{:S(2)}) collective-permute-start(f32[2,128,128]{2,1,0:T(8,128)S(1)} %get-tuple-element.18), channel_id=1, source_target_pairs={{0,4},{4,0},{8,12},{12,8},{16,20},{20,16},{24,28},{28,24},{1,5},{5... | collective-permute-start | bytes 393224 | tf_op jit(solution)/shard_map/ppermute | solution.py:30
  34.7 0.7 %collective-permute-start.1 = (f32[2,128,128]{2,1,0:T(8,128)S(1)}, f32[2,128,128]{2,1,0:T(8,128)S(1)}, u32[]{:S(2)}, u32[]{:S(2)}) collective-permute-start(f32[2,128,128]{2,1,0:T(8,128)S(1)} %get-tuple-element.19), channel_id=1, source_target_pairs={{4,8},{8,4},{12,16},{16,12},{20,24},{24,20},{5,9},{9,5},{13,17},{1... | collective-permute-start | bytes 393224 | tf_op jit(solution)/shard_map/ppermute | solution.py:30
  35.4 0.1 collective-permute-start.2
  35.4 0.7 %collective-permute-start.3 = (f32[2,16,128]{2,1,0:T(8,128)S(1)}, f32[2,16,128]{2,1,0:T(8,128)S(1)}, u32[]{:S(2)}, u32[]{:S(2)}) collective-permute-start(f32[2,16,128]{2,1,0:T(8,128)S(1)} %get-tuple-element.21), channel_id=1, source_target_pairs={{1,2},{2,1},{5,6},{6,5},{9,10},{10,9},{13,14},{14,13},{17,18},{18,... | collective-permute-start | bytes 49160 | tf_op jit(solution)/shard_map/ppermute | solution.py:30
  36.1 0.5 collective-permute-done.2.cols_first
  36.6 0.0 collective-permute-done.3.cols_second
  36.6 6.3 %collective-permute-done.rows_first = f32[2,128,128]{2,1,0:T(8,128)S(1)} collective-permute-done((f32[2,128,128]{2,1,0:T(8,128)S(1)}, f32[2,128,128]{2,1,0:T(8,128)S(1)}, u32[]{:S(2)}, u32[]{:S(2)}) %collective-permute-start) | collective-permute-done | bytes 131104 | tf_op jit(solution)/shard_map/ppermute | solution.py:30
  42.9 0.0 collective-permute-done.1.rows_second
  42.9 8.5 %yee.1 = (f32[3,16,128,128]{3,2,1,0:T(8,128)}, f32[3,16,128,128]{3,2,1,0:T(8,128)}, f32[4,4,16,128]{3,2,1,0:T(8,128)}, f32[4,4,16,128]{3,2,1,0:T(8,128)}) custom-call(f32[3,16,128,128]{3,2,1,0:T(8,128)} %elec_far.3, f32[3,16,128,128]{3,2,1,0:T(8,128)} %magn_far.3, f32[16,128,128]{2,1,0:T(8,128)} %ret_far.3, f32[16,128,128]{2,1,0:T(8,128)} %coup_far.3, ...), custom_call_target="tpu_custom_call" | custom-call | flops 47185920 | bytes 6291456 | tf_op jit(solution)/shard_map/yee/pallas_call | solution.py:702
  51.4 0.0 all-to-all-done.1.got
  51.4 1.1 %placed.1 = f32[2,16,32,64]{3,2,1,0:T(8,128)} custom-call(f32[32,16,128]{2,1,0:T(8,128)S(1)} %all-to-all-done.1.got), custom_call_target="tpu_custom_call" | custom-call | tf_op jit(solution)/shard_map/placed/pallas_call | solution.py:555
Async XLA Ops:
  0.6 26.5 %copy-start = (bf16[512,512]{1,0:T(8,128)(2,1)S(1)}, bf16[512,512]{1,0:T(8,128)(2,1)}, u32[]{:S(2)}) copy-start(bf16[512,512]{1,0:T(8,128)(2,1)} %constant.8.clone.high) | copy-start | bytes 1572868
  0.6 26.5 %copy-start.1 = (bf16[512,512]{1,0:T(8,128)(2,1)S(1)}, bf16[512,512]{1,0:T(8,128)(2,1)}, u32[]{:S(2)}) copy-start(bf16[512,512]{1,0:T(8,128)(2,1)} %constant.9.clone.low) | copy-start | bytes 1572868
  0.7 28.4 %copy-start.2 = (bf16[512,128]{1,0:T(8,128)(2,1)S(1)}, bf16[512,128]{1,0:T(8,128)(2,1)}, u32[]{:S(2)}) copy-start(bf16[512,128]{1,0:T(8,128)(2,1)} %constant.10.clone.refs_2_) | copy-start | bytes 393220
  0.7 28.4 %copy-start.3 = (bf16[512,128]{1,0:T(8,128)(2,1)S(1)}, bf16[512,128]{1,0:T(8,128)(2,1)}, u32[]{:S(2)}) copy-start(bf16[512,128]{1,0:T(8,128)(2,1)} %constant.11.clone.refs_3_) | copy-start | bytes 393220
  27.7 1.3 %collective-permute-start.4 = (f32[64,256]{1,0:T(8,128)S(1)}, f32[64,256]{1,0:T(8,128)S(1)}, u32[]{:S(2)}, u32[]{:S(2)}) collective-permute-start(f32[64,256]{1,0:T(8,128)S(1)} %get-tuple-element.30), channel_id=1, source_target_pairs={{0,1},{1,0},{2,3},{3,2},{4,5},{5,4},{6,7},{7,6},{8,9},{9,8},{10,11... | collective-permute-start | bytes 196616 | tf_op jit(solution)/shard_map/ppermute | solution.py:35
  30.3 21.1 %all-to-all-start.1 = ((f32[32,16,128]{2,1,0:T(8,128)}), f32[32,16,128]{2,1,0:T(8,128)S(1)}, u32[]{:S(2)}, u32[]{:S(2)}) async-start(f32[32,16,128]{2,1,0:T(8,128)} %along_x.1), calls=%async_computation.1 | async-start | bytes 524288 | tf_op jit(solution)/shard_map/all_to_all | solution.py:747
  32.9 10.0 %collective-permute-start = (f32[2,128,128]{2,1,0:T(8,128)S(1)}, f32[2,128,128]{2,1,0:T(8,128)S(1)}, u32[]{:S(2)}, u32[]{:S(2)}) collective-permute-start(f32[2,128,128]{2,1,0:T(8,128)S(1)} %get-tuple-element.18), channel_id=1, source_target_pairs={{0,4},{4,0},{8,12},{12,8},{16,20},{20,16},{24,28},{28,24},{1,5},{5... | collective-permute-start | bytes 393224 | tf_op jit(solution)/shard_map/ppermute | solution.py:30
  34.7 8.2 %collective-permute-start.1 = (f32[2,128,128]{2,1,0:T(8,128)S(1)}, f32[2,128,128]{2,1,0:T(8,128)S(1)}, u32[]{:S(2)}, u32[]{:S(2)}) collective-permute-start(f32[2,128,128]{2,1,0:T(8,128)S(1)} %get-tuple-element.19), channel_id=1, source_target_pairs={{4,8},{8,4},{12,16},{16,12},{20,24},{24,20},{5,9},{9,5},{13,17},{1... | collective-permute-start | bytes 393224 | tf_op jit(solution)/shard_map/ppermute | solution.py:30
  35.4 1.2 %collective-permute-start.2 = (f32[2,16,128]{2,1,0:T(8,128)S(1)}, f32[2,16,128]{2,1,0:T(8,128)S(1)}, u32[]{:S(2)}, u32[]{:S(2)}) collective-permute-start(f32[2,16,128]{2,1,0:T(8,128)S(1)} %get-tuple-element.20), channel_id=1, source_target_pairs={{0,1},{1,0},{2,3},{3,2},{4,5},{5,4},{6,7},{7,6},{8,9},{9,8},{10,11... | collective-permute-start | bytes 49160 | tf_op jit(solution)/shard_map/ppermute | solution.py:30
  35.4 1.2 %collective-permute-start.3 = (f32[2,16,128]{2,1,0:T(8,128)S(1)}, f32[2,16,128]{2,1,0:T(8,128)S(1)}, u32[]{:S(2)}, u32[]{:S(2)}) collective-permute-start(f32[2,16,128]{2,1,0:T(8,128)S(1)} %get-tuple-element.21), channel_id=1, source_target_pairs={{1,2},{2,1},{5,6},{6,5},{9,10},{10,9},{13,14},{14,13},{17,18},{18,... | collective-permute-start | bytes 49160 | tf_op jit(solution)/shard_map/ppermute | solution.py:30

commit v5 on v4

--- a/solution.py
+++ b/solution.py
@@ -14,6 +14,7 @@
 BOTH = ("gx", "gy")
 LANES = 128
 SUBLANES = 8
+SLABS = ((0, 4), (4, 4), (8, 4), (12, 2), (14, 2))
 
 curl_step = 0.5
 
@@ -198,8 +199,8 @@
 PICKED = ((0, -1, 3), (1, -1, 3), (2, -1, 2), (3, -1, 2), (4, -1, 2), (5, 0, 1), (6, 0, 1), (7, 0, 1))
 
 
-def arrivals(chunk, deep, sources, targets, arrived):
-    span = pl.ds(chunk * deep, deep)
+def arrivals(chunk, first, deep, sources, targets, arrived):
+    span = pl.ds(first, deep)
     pairs = []
     for source, target in zip(sources, targets):
         lead = [(i, span) for i in range(source.shape[0])] if len(source.shape) == 4 else [(span,)]
@@ -214,11 +215,11 @@
 ):
     chunks = arrived.shape[0]
     rows = ret.shape[0]
-    deep = rows // chunks
     freqs = real.shape[1]
 
     def copies(chunk):
-        return arrivals(chunk, deep, (elec_far, magn_far, ret_far, coup_far), (elec, magn, ret, coup), arrived)
+        first, count = SLABS[chunk]
+        return arrivals(chunk, first, count, (elec_far, magn_far, ret_far, coup_far), (elec, magn, ret, coup), arrived)
 
     extras = [
         pltpu.make_async_copy(phases_far, phases, small.at[0]),
@@ -242,9 +243,10 @@
 
     packed = None
     for at in range(rows):
-        if at % deep == 0:
-            for copy in copies(at // deep):
-                copy.wait()
+        for chunk, (first, _) in enumerate(SLABS):
+            if first == at:
+                for copy in copies(chunk):
+                    copy.wait()
         arrays = [elec[0, at], elec[1, at], elec[2, at], magn[0, at], magn[1, at], magn[2, at], ret[at], coup[at]]
         start = at % SUBLANES * PLACES
         for which, first, count in PICKED:
@@ -320,39 +322,43 @@
         lanes = lax.broadcasted_iota(jnp.int32, (SUBLANES, LANES), 1)
         pad = jnp.zeros((LANES - rows, LANES), jnp.float32)
 
-        def upright(lines):
-            block = None
-            for which, (value, column) in enumerate(lines):
-                value = moved(value, which - column, 1)
-                block = value if block is None else jnp.where(wide[0:rows] < which, block, value)
-            return jnp.concatenate([block, pad], axis=0).T[0:SUBLANES]
-
         end = LANES - 1
+        block = None
+        upright = ((col_left[0], 0), (col_left[1], 0), (col_left[2], 0), (col_right[0], end), (gain, end), (gain, 0))
+        for which, (value, column) in enumerate(upright):
+            value = moved(value, which - column, 1)
+            block = value if block is None else jnp.where(wide[0:rows] < which, block, value)
+        block = jnp.concatenate([block, pad], axis=0).T
+        left = [block[which : which + 1] for which in range(3)]
+        right, gain_end, gain_start = (moved(block[which + 2 : which + 3], which * rows, 1) for which in (1, 2, 3))
+        unit = jnp.where((lanes[0:1] >= 2 * rows) & (lanes[0:1] < 4 * rows), 1.0, 0.0)
+        columns = (
+            left[0] + right + gain_end + gain_start
+            + jnp.where(lanes[0:1] == 4 * rows, moved(-push[0:1], 4 * rows - end, 1), 0.0),
+            left[1] + gain_end + gain_start
+            + jnp.where(lanes[0:1] == 4 * rows, moved(curl_step * ex_p[rows - 1 :], 4 * rows, 1), 0.0),
+            left[2] + unit,
+            unit,
+        )
+        here = lax.axis_index(BOTH)
         extras[1].wait()
         extras[2].wait()
         departures = []
         for comp in range(4):
             factor = gain if comp < 2 else one
-            columns = upright([(col_left[comp], 0), (col_right[comp], end), (factor, end), (factor, 0)])
-            columns = sum(moved(columns[which : which + 1], which * rows, 1) for which in range(4))
-            if comp < 2:
-                spare = moved(-push[0:1], -end, 1) if comp == 0 else curl_step * ex_p[rows - 1 :]
-                columns = jnp.where(lanes[0:1] == 4 * rows, moved(spare, 4 * rows, 1), columns)
-            extra = jnp.where(tall == 0, row_up[comp][0:1], 0.0)
-            extra = jnp.where(tall == 1, row_down[comp][rows - 1 :], extra)
-            extra = jnp.where(tall == 2, factor[rows - 1 :], extra)
-            extra = jnp.where(tall == 3, factor[0:1], extra)
-            extra = jnp.where(tall == 4, columns, extra)
-            extra = jnp.where(tall == 5, corner_up, extra)
-            extra = jnp.where(tall == 6, corner_down, extra)
+            crossing = ((row_down[comp][rows - 1 :], factor[0:1]), (row_up[comp][0:1], factor[rows - 1 :]))
             for freq in range(freqs):
                 new_real = real[comp, freq] + tangent[comp] * trig[0, freq : freq + 1, :]
                 new_imag = imag[comp, freq] - tangent[comp] * trig[1, freq : freq + 1, :]
                 for half in range(2):
                     to = (comp * freqs + freq) * 2 + half
-                    out[to, 0:8] = new_real[half * 8 : half * 8 + 8]
-                    out[to, 8:16] = new_imag[half * 8 : half * 8 + 8]
-                    out[to, 16:24] = extra
+                    for group, value in enumerate((new_real, new_imag)):
+                        out[to, 2 * group] = value[half * 8 : half * 8 + 4]
+                        out[to, 2 * group + 1] = value[half * 8 + 4 : half * 8 + 8]
+                    corner = jnp.where(to > here, corner_down, corner_up)
+                    extra = jnp.where(tall == 0, crossing[half][0], crossing[half][1])
+                    extra = jnp.where(tall < 2, extra, jnp.where(tall == 2, columns[comp], corner))
+                    out[to, 4] = extra[0:4]
             span = pl.ds(comp * freqs * 2, freqs * 2)
             departures.append(pltpu.make_async_copy(out.at[span], out_far.at[span], leaving.at[comp]))
             departures[-1].start()
@@ -363,8 +369,8 @@
 def spread(electric, magnetic, retention, coupling, spectrum_real, spectrum_imag, phases):
     _, rows, cols, deep = electric.shape
     comps, freqs = spectrum_real.shape[:2]
-    chunks = 4
-    sent = (comps * freqs * 2, 24, cols)
+    chunks = len(SLABS)
+    sent = (comps * freqs * 2, 5, 4, cols)
     inputs = (phases, electric, magnetic, retention, coupling, spectrum_real, spectrum_imag)
     return pl.pallas_call(
         spread_kernel,
@@ -419,10 +425,8 @@
     freq = (at // 2) % freqs
     weight_real = trig[0, pl.ds(freq, 1), :]
     weight_imag = -trig[1, pl.ds(freq, 1), :]
-    is_last = jnp.where(half == 1, 1.0, 0.0)
-    is_first = jnp.where(half == 0, 1.0, 0.0)
-
-    packed = jnp.concatenate([got[x, :, 20, :] for x in range(along_x)], axis=0)
+
+    packed = jnp.concatenate([got[x, :, 4, 2, :] for x in range(along_x)], axis=0)
     block = spot((blocks, LANES), 0)
     lane = spot((blocks, LANES), 1)
     inner = block % along_y
@@ -446,20 +450,20 @@
 
     low_row = spot((SUBLANES, LANES), 0)
     low_lane = spot((SUBLANES, LANES), 1)
+    crossed = jnp.where(half == 1, SUBLANES - 1, 0)
     for x in range(along_x):
         for y in range(along_y):
             here = x * along_y + y
             delta = jnp.where(low_lane == LANES - 1, moved(cols, LANES - 1 - here, 1), 0.0)
             delta = delta + jnp.where(low_lane == 0, moved(cols, -blocks - here, 1), 0.0)
-            if x + 1 < along_x:
-                row = got[x, y, 18:19, :] * got[x + 1, y, 16:17, :] * is_last
-                delta = delta + jnp.where(low_row == SUBLANES - 1, row, 0.0)
-            if x > 0:
-                row = got[x, y, 19:20, :] * got[x - 1, y, 17:18, :] * is_first
-                delta = delta + jnp.where(low_row == 0, row, 0.0)
+            from_next = got[x + 1, y, 4, 0:1, :] if x + 1 < along_x else 0.0
+            from_last = got[x - 1, y, 4, 0:1, :] if x > 0 else 0.0
+            row = got[x, y, 4, 1:2, :] * jnp.where(half == 1, from_next, from_last)
+            delta = delta + jnp.where(low_row == crossed, row, 0.0)
             span = slice(y * LANES, (y + 1) * LANES)
-            lines[x * 16 : x * 16 + 8, span] = got[x, y, 0:8, :] + weight_real * delta
-            lines[x * 16 + 8 : x * 16 + 16, span] = got[x, y, 8:16, :] + weight_imag * delta
+            for group, weight in enumerate((weight_real, weight_imag)):
+                own = jnp.concatenate([got[x, y, 2 * group], got[x, y, 2 * group + 1]], axis=0)
+                lines[x * 16 + group * 8 : x * 16 + group * 8 + 8, span] = own + weight * delta
 
     lines_high, lines_low = split_high(lines[...])
     total = dot(lines_high, high[...]) + (dot(lines_low, high[...]) + dot(lines_high, low[...]))
@@ -491,7 +495,7 @@
         scratch_shapes=[room((along_x * 16, along_y * LANES))],
         compiler_params=limited(),
         name="along_y",
-    )(kept(got.reshape(along_x, along_y, 24, cols)), kept(trig), kept(high), kept(low))
+    )(kept(got.reshape(along_x, along_y, *got.shape[1:])), kept(trig), kept(high), kept(low))
 
 
 def along_x_kernel(along_x, mine, other, high, low, out):
@@ -579,8 +583,8 @@
     down = jnp.maximum(here - along_y + 1, 0)
     inner_x = jnp.where(at_x > 0, 1.0, 0.0)
     inner_y = jnp.where(at_y > 0, 1.0, 0.0)
-    corner_up = got[pl.ds(up, 1), 21, :] * jnp.where((at_x + 1 < along_x) & (at_y > 0), curl_step, 0.0)
-    corner_down = got[pl.ds(down, 1), 22, :] * jnp.where((at_x > 0) & (at_y + 1 < along_y), curl_step, 0.0)
+    corner_up = got[pl.ds(up, 1), 4, 3, :] * jnp.where((at_x + 1 < along_x) & (at_y > 0), curl_step, 0.0)
+    corner_down = got[pl.ds(down, 1), 4, 3, :] * jnp.where((at_x > 0) & (at_y + 1 < along_y), curl_step, 0.0)
     row = spot((LANES, LANES), 0)
     lane = spot((LANES, LANES), 1)
     chunks = arrived.shape[0]
@@ -589,7 +593,7 @@
 
     def copies(chunk):
         return arrivals(
-            chunk, thick, (elec_far, magn_far, ret_far, coup_far), (elec.at[:, :, 0:cols], magn, ret, coup), arrived
+            chunk, chunk * thick, thick, (elec_far, magn_far, ret_far, coup_far), (elec.at[:, :, 0:cols], magn, ret, coup), arrived
         )
 
     @pl.when(step == 0)

time: 52.8 us -> 51.7 us (0.979)
  blocking collectives: 20.6 us -> 19.4 us
    all_to_all x1, blocking collectives: 20.6 us -> 19.4 us  [tiled_step(): got = lax.all_to_all(sent, BOTH, split_axis=0, concat_axis=0, tiled=True)]
  transfers between devices with their start and end apart: 6 -> 6, of which waited for: 3 -> 3; matrix products, arithmetic and copies ran while one was open for 0% -> 0% of each run, Pallas kernels for 16% -> 17%
where the time goes in v5:
time: 51.7 us; the launch traced here: 51.3 us
  blocking collectives  19.4 us (38%)
  Pallas kernels  17.4 us (34%)
  waiting for transfers between devices  8.04 us (16%)
  starting transfers between devices  5.77 us (11%)
  between operations  0.74 us (1%)
    all_to_all x1, blocking collectives, tiled_step(): got = lax.all_to_all(sent, BOTH, split_axis=0, concat_axis=0, tiled=True)  19.4 us
    pallas_call x1, Pallas kernels, yee(): pl.pallas_call(yee_kernel, grid=(rows // slab,), in_specs=[pl.BlockSpec(m...  8.53 us
    ppermute x4, waiting for transfers between devices, traded(): lax.ppermute(value, axis, [(i, to) for i, to in pairs if 0 <= to < devices])  6.8 us
    pallas_call x1, Pallas kernels, spread(): pl.pallas_call(spread_kernel, in_specs=[pl.BlockSpec(memory_space=pl.ANY)...  5.89 us
    ppermute x4, starting transfers between devices, traded(): lax.ppermute(value, axis, [(i, to) for i, to in pairs if 0 <= to < devices])  3.11 us
    all_to_all x1, starting transfers between devices, tiled_step(): far = lax.all_to_all(far, BOTH, split_axis=0, concat_axis=0, tiled=True)  2.59 us
    pallas_call x1, Pallas kernels, along_x_sums(): pl.pallas_call(lambda *refs: along_x_kernel(along_x, *refs), in_specs=[wh...  1.28 us
    ppermute x1, waiting for transfers between devices, swapped(): return lax.ppermute(value, BOTH, [(i, i ^ by) for i in range(devices)])  1.24 us
  transfers between devices with their start and end apart: 6, of which 3 were waited for; matrix products, arithmetic and copies ran while one was open for 0% of the time, Pallas kernels for 17%

profile of v5, /device:TPU:0, one launch (start us, length us, event | category | flops | bytes accessed | tf_op | source)
XLA Modules:
  0.0 51.3 jit_solution(14485783948453769548)
XLA Ops:
  0.6 0.0 copy-start
  0.6 0.0 copy-start.1
  0.7 0.0 copy-start.2
  0.7 0.0 copy-start.3
  0.7 5.9 %spread.1 = (f32[32,5,4,128]{3,2,1,0:T(4,128)}, f32[2,128,128]{2,1,0:T(8,128)S(1)}, f32[2,128,128]{2,1,0:T(8,128)S(1)}, f32[2,16,128]{2,1,0:T(8,128)S(1)}, f32[2...) custom-call(f32[4]{0:T(128)} %phases_far.1, f32[3,16,128,128]{3,2,1,0:T(8,128)} %elec_far.3, ...), custom_call_target="tpu_custom_call" | custom-call | tf_op jit(solution)/shard_map/spread/pallas_call | solution.py:375
  6.6 19.4 %all_to_all.10.got = f32[32,5,4,128]{3,2,1,0:T(4,128)S(1)} all-to-all(f32[32,5,4,128]{3,2,1,0:T(4,128)} %get-tuple-element.22), channel_id=1, replica_groups=mesh['gx'=8,'gy'=4] {'gx','gy'}, dimensions={0} | all-to-all | bytes 655360 | tf_op jit(solution)/shard_map/all_to_all | solution.py:744
  26.0 0.0 copy-done
  26.0 0.0 copy-done.1
  26.0 0.6 %along_y.1 = (f32[64,256]{1,0:T(8,128)S(1)}, f32[64,256]{1,0:T(8,128)S(1)}) custom-call(f32[8,4,5,4,128]{4,3,2,1,0:T(4,128)S(1)} %bitcast.2, f32[2,8,128]{2,1,0:T(8,128)S(1)} %get-tuple-element.23.trig, bf16[512,512]{1,0:T(8,128)(2,1)S(1)} %copy-done, bf16[512,512]{1,0:T(8,128)(2,1)S(1)} %copy-done.1), custom_call_target="tpu_custom_call" | custom-call | tf_op jit(solution)/shard_map/along_y/pallas_call | solution.py:490
  26.6 0.1 collective-permute-start.4
  26.7 1.2 %collective-permute-done.4.refs_1_ = f32[64,256]{1,0:T(8,128)S(1)} collective-permute-done((f32[64,256]{1,0:T(8,128)S(1)}, f32[64,256]{1,0:T(8,128)S(1)}, u32[]{:S(2)}, u32[]{:S(2)}) %collective-permute-start.4) | collective-permute-done | bytes 65568 | tf_op jit(solution)/shard_map/ppermute | solution.py:36
  27.9 0.0 copy-done.2
  27.9 0.0 copy-done.3
  27.9 1.3 %along_x.1 = f32[32,16,128]{2,1,0:T(8,128)} custom-call(f32[64,256]{1,0:T(8,128)S(1)} %get-tuple-element.29.refs_0_, f32[64,256]{1,0:T(8,128)S(1)} %collective-permute-done.4.refs_1_, bf16[512,128]{1,0:T(8,128)(2,1)S(1)} %copy-done.2, bf16[512,128]{1,0:T(8,128)(2,1)S(1)} %copy-done.3), custom_call_target="tpu_custom_call" | custom-call | tf_op jit(solution)/shard_map/along_x/pallas_call | solution.py:535
  29.2 2.6 %all-to-all-start.1 = ((f32[32,16,128]{2,1,0:T(8,128)}), f32[32,16,128]{2,1,0:T(8,128)S(1)}, u32[]{:S(2)}, u32[]{:S(2)}) async-start(f32[32,16,128]{2,1,0:T(8,128)} %along_x.1), calls=%async_computation.1 | async-start | bytes 524288 | tf_op jit(solution)/shard_map/all_to_all | solution.py:751
  31.8 1.7 %collective-permute-start = (f32[2,128,128]{2,1,0:T(8,128)S(1)}, f32[2,128,128]{2,1,0:T(8,128)S(1)}, u32[]{:S(2)}, u32[]{:S(2)}) collective-permute-start(f32[2,128,128]{2,1,0:T(8,128)S(1)} %get-tuple-element.18), channel_id=1, source_target_pairs={{0,4},{4,0},{8,12},{12,8},{16,20},{20,16},{24,28},{28,24},{1,5},{5... | collective-permute-start | bytes 393224 | tf_op jit(solution)/shard_map/ppermute | solution.py:31
  33.5 0.7 %collective-permute-start.1 = (f32[2,128,128]{2,1,0:T(8,128)S(1)}, f32[2,128,128]{2,1,0:T(8,128)S(1)}, u32[]{:S(2)}, u32[]{:S(2)}) collective-permute-start(f32[2,128,128]{2,1,0:T(8,128)S(1)} %get-tuple-element.19), channel_id=1, source_target_pairs={{4,8},{8,4},{12,16},{16,12},{20,24},{24,20},{5,9},{9,5},{13,17},{1... | collective-permute-start | bytes 393224 | tf_op jit(solution)/shard_map/ppermute | solution.py:31
  34.2 0.1 collective-permute-start.2
  34.2 0.7 %collective-permute-start.3 = (f32[2,16,128]{2,1,0:T(8,128)S(1)}, f32[2,16,128]{2,1,0:T(8,128)S(1)}, u32[]{:S(2)}, u32[]{:S(2)}) collective-permute-start(f32[2,16,128]{2,1,0:T(8,128)S(1)} %get-tuple-element.21), channel_id=1, source_target_pairs={{1,2},{2,1},{5,6},{6,5},{9,10},{10,9},{13,14},{14,13},{17,18},{18,... | collective-permute-start | bytes 49160 | tf_op jit(solution)/shard_map/ppermute | solution.py:31
  34.9 0.5 collective-permute-done.2.cols_first
  35.4 0.0 collective-permute-done.3.cols_second
  35.4 6.3 %collective-permute-done.rows_first = f32[2,128,128]{2,1,0:T(8,128)S(1)} collective-permute-done((f32[2,128,128]{2,1,0:T(8,128)S(1)}, f32[2,128,128]{2,1,0:T(8,128)S(1)}, u32[]{:S(2)}, u32[]{:S(2)}) %collective-permute-start) | collective-permute-done | bytes 131104 | tf_op jit(solution)/shard_map/ppermute | solution.py:31
  41.7 0.0 collective-permute-done.1.rows_second
  41.7 8.5 %yee.1 = (f32[3,16,128,128]{3,2,1,0:T(8,128)}, f32[3,16,128,128]{3,2,1,0:T(8,128)}, f32[4,4,16,128]{3,2,1,0:T(8,128)}, f32[4,4,16,128]{3,2,1,0:T(8,128)}) custom-call(f32[3,16,128,128]{3,2,1,0:T(8,128)} %elec_far.3, f32[3,16,128,128]{3,2,1,0:T(8,128)} %magn_far.3, f32[16,128,128]{2,1,0:T(8,128)} %ret_far.3, f32[16,128,128]{2,1,0:T(8,128)} %coup_far.3, ...), custom_call_target="tpu_custom_call" | custom-call | flops 47185920 | bytes 6291456 | tf_op jit(solution)/shard_map/yee/pallas_call | solution.py:706
  50.3 0.0 all-to-all-done.1.got
  50.3 1.1 %placed.1 = f32[2,16,32,64]{3,2,1,0:T(8,128)} custom-call(f32[32,16,128]{2,1,0:T(8,128)S(1)} %all-to-all-done.1.got), custom_call_target="tpu_custom_call" | custom-call | tf_op jit(solution)/shard_map/placed/pallas_call | solution.py:559
Async XLA Ops:
  0.6 25.3 %copy-start = (bf16[512,512]{1,0:T(8,128)(2,1)S(1)}, bf16[512,512]{1,0:T(8,128)(2,1)}, u32[]{:S(2)}) copy-start(bf16[512,512]{1,0:T(8,128)(2,1)} %constant.8.clone.high) | copy-start | bytes 1572868
  0.6 25.3 %copy-start.1 = (bf16[512,512]{1,0:T(8,128)(2,1)S(1)}, bf16[512,512]{1,0:T(8,128)(2,1)}, u32[]{:S(2)}) copy-start(bf16[512,512]{1,0:T(8,128)(2,1)} %constant.9.clone.low) | copy-start | bytes 1572868
  0.7 27.3 %copy-start.2 = (bf16[512,128]{1,0:T(8,128)(2,1)S(1)}, bf16[512,128]{1,0:T(8,128)(2,1)}, u32[]{:S(2)}) copy-start(bf16[512,128]{1,0:T(8,128)(2,1)} %constant.10.clone.refs_2_) | copy-start | bytes 393220
  0.7 27.2 %copy-start.3 = (bf16[512,128]{1,0:T(8,128)(2,1)S(1)}, bf16[512,128]{1,0:T(8,128)(2,1)}, u32[]{:S(2)}) copy-start(bf16[512,128]{1,0:T(8,128)(2,1)} %constant.11.clone.refs_3_) | copy-start | bytes 393220
  26.6 1.3 %collective-permute-start.4 = (f32[64,256]{1,0:T(8,128)S(1)}, f32[64,256]{1,0:T(8,128)S(1)}, u32[]{:S(2)}, u32[]{:S(2)}) collective-permute-start(f32[64,256]{1,0:T(8,128)S(1)} %get-tuple-element.30), channel_id=1, source_target_pairs={{0,1},{1,0},{2,3},{3,2},{4,5},{5,4},{6,7},{7,6},{8,9},{9,8},{10,11... | collective-permute-start | bytes 196616 | tf_op jit(solution)/shard_map/ppermute | solution.py:36
  29.2 21.1 %all-to-all-start.1 = ((f32[32,16,128]{2,1,0:T(8,128)}), f32[32,16,128]{2,1,0:T(8,128)S(1)}, u32[]{:S(2)}, u32[]{:S(2)}) async-start(f32[32,16,128]{2,1,0:T(8,128)} %along_x.1), calls=%async_computation.1 | async-start | bytes 524288 | tf_op jit(solution)/shard_map/all_to_all | solution.py:751
  31.8 9.9 %collective-permute-start = (f32[2,128,128]{2,1,0:T(8,128)S(1)}, f32[2,128,128]{2,1,0:T(8,128)S(1)}, u32[]{:S(2)}, u32[]{:S(2)}) collective-permute-start(f32[2,128,128]{2,1,0:T(8,128)S(1)} %get-tuple-element.18), channel_id=1, source_target_pairs={{0,4},{4,0},{8,12},{12,8},{16,20},{20,16},{24,28},{28,24},{1,5},{5... | collective-permute-start | bytes 393224 | tf_op jit(solution)/shard_map/ppermute | solution.py:31
  33.5 8.2 %collective-permute-start.1 = (f32[2,128,128]{2,1,0:T(8,128)S(1)}, f32[2,128,128]{2,1,0:T(8,128)S(1)}, u32[]{:S(2)}, u32[]{:S(2)}) collective-permute-start(f32[2,128,128]{2,1,0:T(8,128)S(1)} %get-tuple-element.19), channel_id=1, source_target_pairs={{4,8},{8,4},{12,16},{16,12},{20,24},{24,20},{5,9},{9,5},{13,17},{1... | collective-permute-start | bytes 393224 | tf_op jit(solution)/shard_map/ppermute | solution.py:31
  34.2 1.2 %collective-permute-start.2 = (f32[2,16,128]{2,1,0:T(8,128)S(1)}, f32[2,16,128]{2,1,0:T(8,128)S(1)}, u32[]{:S(2)}, u32[]{:S(2)}) collective-permute-start(f32[2,16,128]{2,1,0:T(8,128)S(1)} %get-tuple-element.20), channel_id=1, source_target_pairs={{0,1},{1,0},{2,3},{3,2},{4,5},{5,4},{6,7},{7,6},{8,9},{9,8},{10,11... | collective-permute-start | bytes 49160 | tf_op jit(solution)/shard_map/ppermute | solution.py:31
  34.2 1.2 %collective-permute-start.3 = (f32[2,16,128]{2,1,0:T(8,128)S(1)}, f32[2,16,128]{2,1,0:T(8,128)S(1)}, u32[]{:S(2)}, u32[]{:S(2)}) collective-permute-start(f32[2,16,128]{2,1,0:T(8,128)S(1)} %get-tuple-element.21), channel_id=1, source_target_pairs={{1,2},{2,1},{5,6},{6,5},{9,10},{10,9},{13,14},{14,13},{17,18},{18,... | collective-permute-start | bytes 49160 | tf_op jit(solution)/shard_map/ppermute | solution.py:31

commit v6 on v5

--- a/solution.py
+++ b/solution.py
@@ -14,7 +14,7 @@
 BOTH = ("gx", "gy")
 LANES = 128
 SUBLANES = 8
-SLABS = ((0, 4), (4, 4), (8, 4), (12, 2), (14, 2))
+SLABS = ((0, 4), (4, 4), (8, 4), (12, 4))
 
 curl_step = 0.5
 
@@ -211,7 +211,7 @@
 def spread_kernel(
     phases_far, elec_far, magn_far, ret_far, coup_far, real_far, imag_far,
     out_far, rows_first, rows_second, cols_first, cols_second, trig, known,
-    elec, magn, ret, coup, cols_elec, cols_magn, planes, ends, out, real, imag, phases, arrived, small, leaving,
+    elec, magn, ret, coup, planes, out, real, imag, phases, arrived, small, leaving,
 ):
     chunks = arrived.shape[0]
     rows = ret.shape[0]
@@ -232,13 +232,6 @@
             copy.start()
     extras[1].start()
     extras[2].start()
-    extras[0].wait()
-    turn_row = spot((SUBLANES, LANES), 0)
-    angle = jnp.zeros((SUBLANES, LANES), jnp.float32)
-    for freq in range(freqs):
-        angle = jnp.where(turn_row == freq, phases[freq], angle)
-    trig[0] = jnp.cos(angle)
-    trig[1] = jnp.sin(angle)
     lane = spot((LANES, LANES), 1)
 
     packed = None
@@ -247,6 +240,14 @@
             if first == at:
                 for copy in copies(chunk):
                     copy.wait()
+        if at == SLABS[1][0]:
+            extras[0].wait()
+            turn_row = spot((SUBLANES, LANES), 0)
+            angle = jnp.zeros((SUBLANES, LANES), jnp.float32)
+            for freq in range(freqs):
+                angle = jnp.where(turn_row == freq, phases[freq], angle)
+            trig[0] = jnp.cos(angle)
+            trig[1] = jnp.sin(angle)
         arrays = [elec[0, at], elec[1, at], elec[2, at], magn[0, at], magn[1, at], magn[2, at], ret[at], coup[at]]
         start = at % SUBLANES * PLACES
         for which, first, count in PICKED:
@@ -256,32 +257,8 @@
         if at % SUBLANES == SUBLANES - 1:
             planes[at // SUBLANES] = packed.T
             packed = None
-        ends[0, at : at + 1, :] = elec[0, at, -1:, :]
-        ends[1, at : at + 1, :] = elec[1, at, -1:, :]
-        ends[2, at : at + 1, :] = magn[2, at, -1:, :]
-        cols_elec[0, at : at + 1, :] = elec[0, at, 0:1, :]
-        cols_elec[1, at : at + 1, :] = elec[2, at, 0:1, :]
-        line = elec[1, at, -1:, :]
-        cols_magn[0, at : at + 1, :] = (
-            magn[0, at, -1:, :] + curl_step * elec[2, at, -1:, :] + curl_step * (after(line, 1) - line)
-        )
 
     last = rows - 1
-    ex, ey, ez = elec[0, last], elec[1, last], elec[2, last]
-    upward = (elec[1, 0], elec[2, 0])
-    downward = (
-        magn[1, last] - curl_step * (after(ex, 1) - ex) - curl_step * ez,
-        magn[2, last] + curl_step * ey + curl_step * (after(ex, 0) - ex),
-    )
-    even = lax.axis_index("gx") % 2 == 0
-    for i in range(2):
-        rows_first[i] = jnp.where(even, downward[i], upward[i])
-        rows_second[i] = jnp.where(even, upward[i], downward[i])
-    end_x, end_y, end_z = ends[0], ends[1], ends[2]
-    cols_magn[1] = end_z - curl_step * (after(end_y, 0) - end_y) - curl_step * end_x
-    even = lax.axis_index("gy") % 2 == 0
-    cols_first[...] = jnp.where(even, cols_magn[...], cols_elec[...])
-    cols_second[...] = jnp.where(even, cols_elec[...], cols_magn[...])
     corner_up, corner_down = elec[1, 0, -1:, :], elec[0, last, 0:1, :]
 
     if rows:
@@ -302,8 +279,6 @@
             hx_p,
             hy_p,
         )
-        for which, value in enumerate((*tangent, gain)):
-            known[which] = value
         ez_jump = curl_step * (ez_p - ez_m)
         push = -curl_step * ey_p
         none = jnp.zeros_like(ex_p)
@@ -362,6 +337,30 @@
             span = pl.ds(comp * freqs * 2, freqs * 2)
             departures.append(pltpu.make_async_copy(out.at[span], out_far.at[span], leaving.at[comp]))
             departures[-1].start()
+
+        for which, value in enumerate((*tangent, gain)):
+            known[which] = value
+        first, final = 0, elec.shape[2] - 1
+        ex, ey, ez = elec[0, last], elec[1, last], elec[2, last]
+        upward = (elec[1, 0], elec[2, 0])
+        downward = (
+            magn[1, last] - curl_step * (after(ex, 1) - ex) - curl_step * ez,
+            magn[2, last] + curl_step * ey + curl_step * (after(ex, 0) - ex),
+        )
+        even = lax.axis_index("gx") % 2 == 0
+        for i in range(2):
+            rows_first[i] = jnp.where(even, downward[i], upward[i])
+            rows_second[i] = jnp.where(even, upward[i], downward[i])
+        end_x, end_y, end_z = (elec[i, :, final, :] for i in range(3))
+        leftward = (elec[0, :, first, :], elec[2, :, first, :])
+        rightward = (
+            magn[0, :, final, :] + curl_step * end_z + curl_step * (after(end_y, 1) - end_y),
+            magn[2, :, final, :] - curl_step * (after(end_y, 0) - end_y) - curl_step * end_x,
+        )
+        even = lax.axis_index("gy") % 2 == 0
+        for i in range(2):
+            cols_first[i] = jnp.where(even, rightward[i], leftward[i])
+            cols_second[i] = jnp.where(even, leftward[i], rightward[i])
         for departure in departures:
             departure.wait()
 
@@ -391,10 +390,7 @@
             room(magnetic.shape),
             room(retention.shape),
             room(coupling.shape),
-            room((2, rows, deep)),
-            room((2, rows, deep)),
             room((rows // SUBLANES, LANES, LANES)),
-            room((3, rows, LANES)),
             room(sent),
             room(spectrum_real.shape),
             room(spectrum_imag.shape),
@@ -498,7 +494,7 @@
     )(kept(got.reshape(along_x, along_y, *got.shape[1:])), kept(trig), kept(high), kept(low))
 
 
-def along_x_kernel(along_x, mine, other, high, low, out):
+def along_x_kernel(along_x, mine, other, high, low, out_far, out, leaving):
     half = lax.axis_index(BOTH) % 2
     lines = jnp.concatenate(
         [jnp.where(half == 0, mine[...], other[...]), jnp.where(half == 0, other[...], mine[...])], axis=0
@@ -516,6 +512,7 @@
     along_y = out.shape[0] // along_x
     wide = piece // along_y
     lane = spot((SUBLANES, LANES), 1)
+    departures = []
     for x in range(along_x):
         for part in range(2):
             tiles = [far[part][x * tall + q * 8 : x * tall + q * 8 + 8] for q in range(stacks)]
@@ -525,6 +522,11 @@
                     tile = moved(tiles[q], (q - y) * wide, 1)
                     block = tile if block is None else jnp.where(lane < q * wide, block, tile)
                 out[x * along_y + y, part * 8 : part * 8 + 8] = block
+        span = pl.ds(x * along_y, along_y)
+        departures.append(pltpu.make_async_copy(out.at[span], out_far.at[span], leaving.at[x]))
+        departures[-1].start()
+    for departure in departures:
+        departure.wait()
 
 
 def along_x_sums(mine, other, rows, scale, along_x, devices):
@@ -535,15 +537,18 @@
     return pl.pallas_call(
         lambda *refs: along_x_kernel(along_x, *refs),
         in_specs=[whole_vmem()] * 4,
-        out_specs=whole_vmem(),
+        out_specs=pl.BlockSpec(memory_space=pl.ANY),
         out_shape=pltpu.HBM((devices, 16, LANES), jnp.float32),
+        scratch_shapes=[room((devices, 16, LANES)), pltpu.SemaphoreType.DMA((along_x,))],
         compiler_params=limited(),
         name="along_x",
     )(kept(mine), kept(other), kept(high), kept(low))
 
 
-def placed_kernel(got, out):
+def placed_kernel(got, out_far, out, leaving):
     planes, tall, wide = out.shape[1:]
+    parts = leaving.shape[0]
+    departures = []
     piece = wide // 2
     lane = spot((SUBLANES, LANES), 1)
     for plane in range(planes):
@@ -553,14 +558,22 @@
             for q in range(tall // SUBLANES):
                 tile = jnp.where(lane < piece, moved(first, -q * piece, 1), moved(second, piece - q * piece, 1))
                 out[part, plane, q * 8 : q * 8 + 8, :] = tile[:, :wide]
+        if (plane + 1) % (planes // parts) == 0:
+            span = pl.ds(plane + 1 - planes // parts, planes // parts)
+            at = len(departures)
+            departures.append(pltpu.make_async_copy(out.at[:, span], out_far.at[:, span], leaving.at[at]))
+            departures[-1].start()
+    for departure in departures:
+        departure.wait()
 
 
 def placed_far(got, comps, freqs, tall, wide):
     far = pl.pallas_call(
         placed_kernel,
         in_specs=[whole_vmem()],
-        out_specs=whole_vmem(),
+        out_specs=pl.BlockSpec(memory_space=pl.ANY),
         out_shape=jax.ShapeDtypeStruct((2, comps * freqs, tall, wide), jnp.float32),
+        scratch_shapes=[room((2, comps * freqs, tall, wide)), pltpu.SemaphoreType.DMA((comps,))],
         compiler_params=limited(),
         name="placed",
     )(kept(got))

time: 51.7 us -> 51.4 us (level)
  no operation moved by 1% of the time
where the time goes in v6:
time: 51.4 us; the launch traced here: 51.1 us
  blocking collectives  19.4 us (38%)
  Pallas kernels  17.1 us (33%)
  waiting for transfers between devices  8.04 us (16%)
  starting transfers between devices  5.78 us (11%)
  between operations  0.75 us (1%)
    all_to_all x1, blocking collectives, tiled_step(): got = lax.all_to_all(sent, BOTH, split_axis=0, concat_axis=0, tiled=True)  19.4 us
    pallas_call x1, Pallas kernels, yee(): pl.pallas_call(yee_kernel, grid=(rows // slab,), in_specs=[pl.BlockSpec(m...  8.53 us
    ppermute x4, waiting for transfers between devices, traded(): lax.ppermute(value, axis, [(i, to) for i, to in pairs if 0 <= to < devices])  6.8 us
    pallas_call x1, Pallas kernels, spread(): pl.pallas_call(spread_kernel, in_specs=[pl.BlockSpec(memory_space=pl.ANY)...  5.78 us
    ppermute x4, starting transfers between devices, traded(): lax.ppermute(value, axis, [(i, to) for i, to in pairs if 0 <= to < devices])  3.11 us
    all_to_all x1, starting transfers between devices, tiled_step(): far = lax.all_to_all(far, BOTH, split_axis=0, concat_axis=0, tiled=True)  2.6 us
    pallas_call x1, Pallas kernels, along_x_sums(): pl.pallas_call(lambda *refs: along_x_kernel(along_x, *refs), in_specs=[wh...  1.26 us
    ppermute x1, waiting for transfers between devices, swapped(): return lax.ppermute(value, BOTH, [(i, i ^ by) for i in range(devices)])  1.24 us
  transfers between devices with their start and end apart: 6, of which 3 were waited for; matrix products, arithmetic and copies ran while one was open for 0% of the time, Pallas kernels for 17%

profile of v6, /device:TPU:0, one launch (start us, length us, event | category | flops | bytes accessed | tf_op | source)
XLA Modules:
  0.0 51.1 jit_solution(5952205590698506004)
XLA Ops:
  0.6 0.0 copy-start
  0.6 0.0 copy-start.1
  0.7 0.0 copy-start.2
  0.7 0.0 copy-start.3
  0.7 5.8 %spread.1 = (f32[32,5,4,128]{3,2,1,0:T(4,128)}, f32[2,128,128]{2,1,0:T(8,128)S(1)}, f32[2,128,128]{2,1,0:T(8,128)S(1)}, f32[2,16,128]{2,1,0:T(8,128)S(1)}, f32[2...) custom-call(f32[4]{0:T(128)} %phases_far.1, f32[3,16,128,128]{3,2,1,0:T(8,128)} %elec_far.3, ...), custom_call_target="tpu_custom_call" | custom-call | tf_op jit(solution)/shard_map/spread/pallas_call | solution.py:374
  6.5 19.4 %all_to_all.10.got = f32[32,5,4,128]{3,2,1,0:T(4,128)S(1)} all-to-all(f32[32,5,4,128]{3,2,1,0:T(4,128)} %get-tuple-element.22), channel_id=1, replica_groups=mesh['gx'=8,'gy'=4] {'gx','gy'}, dimensions={0} | all-to-all | bytes 655360 | tf_op jit(solution)/shard_map/all_to_all | solution.py:757
  25.9 0.0 copy-done
  25.9 0.0 copy-done.1
  25.9 0.6 %along_y.1 = (f32[64,256]{1,0:T(8,128)S(1)}, f32[64,256]{1,0:T(8,128)S(1)}) custom-call(f32[8,4,5,4,128]{4,3,2,1,0:T(4,128)S(1)} %bitcast.2, f32[2,8,128]{2,1,0:T(8,128)S(1)} %get-tuple-element.23.trig, bf16[512,512]{1,0:T(8,128)(2,1)S(1)} %copy-done, bf16[512,512]{1,0:T(8,128)(2,1)S(1)} %copy-done.1), custom_call_target="tpu_custom_call" | custom-call | tf_op jit(solution)/shard_map/along_y/pallas_call | solution.py:486
  26.5 0.1 collective-permute-start.4
  26.6 1.2 %collective-permute-done.4.refs_1_ = f32[64,256]{1,0:T(8,128)S(1)} collective-permute-done((f32[64,256]{1,0:T(8,128)S(1)}, f32[64,256]{1,0:T(8,128)S(1)}, u32[]{:S(2)}, u32[]{:S(2)}) %collective-permute-start.4) | collective-permute-done | bytes 65568 | tf_op jit(solution)/shard_map/ppermute | solution.py:36
  27.8 0.0 copy-done.2
  27.8 0.0 copy-done.3
  27.8 1.3 %along_x.1 = f32[32,16,128]{2,1,0:T(8,128)} custom-call(f32[64,256]{1,0:T(8,128)S(1)} %get-tuple-element.29.refs_0_, f32[64,256]{1,0:T(8,128)S(1)} %collective-permute-done.4.refs_1_, bf16[512,128]{1,0:T(8,128)(2,1)S(1)} %copy-done.2, bf16[512,128]{1,0:T(8,128)(2,1)S(1)} %copy-done.3), custom_call_target="tpu_custom_call" | custom-call | tf_op jit(solution)/shard_map/along_x/pallas_call | solution.py:537
  29.1 2.6 %all-to-all-start.1 = ((f32[32,16,128]{2,1,0:T(8,128)}), f32[32,16,128]{2,1,0:T(8,128)S(1)}, u32[]{:S(2)}, u32[]{:S(2)}) async-start(f32[32,16,128]{2,1,0:T(8,128)} %along_x.1), calls=%async_computation.1 | async-start | bytes 524288 | tf_op jit(solution)/shard_map/all_to_all | solution.py:764
  31.7 1.7 %collective-permute-start = (f32[2,128,128]{2,1,0:T(8,128)S(1)}, f32[2,128,128]{2,1,0:T(8,128)S(1)}, u32[]{:S(2)}, u32[]{:S(2)}) collective-permute-start(f32[2,128,128]{2,1,0:T(8,128)S(1)} %get-tuple-element.18), channel_id=1, source_target_pairs={{0,4},{4,0},{8,12},{12,8},{16,20},{20,16},{24,28},{28,24},{1,5},{5... | collective-permute-start | bytes 393224 | tf_op jit(solution)/shard_map/ppermute | solution.py:31
  33.4 0.7 %collective-permute-start.1 = (f32[2,128,128]{2,1,0:T(8,128)S(1)}, f32[2,128,128]{2,1,0:T(8,128)S(1)}, u32[]{:S(2)}, u32[]{:S(2)}) collective-permute-start(f32[2,128,128]{2,1,0:T(8,128)S(1)} %get-tuple-element.19), channel_id=1, source_target_pairs={{4,8},{8,4},{12,16},{16,12},{20,24},{24,20},{5,9},{9,5},{13,17},{1... | collective-permute-start | bytes 393224 | tf_op jit(solution)/shard_map/ppermute | solution.py:31
  34.1 0.1 collective-permute-start.2
  34.1 0.7 %collective-permute-start.3 = (f32[2,16,128]{2,1,0:T(8,128)S(1)}, f32[2,16,128]{2,1,0:T(8,128)S(1)}, u32[]{:S(2)}, u32[]{:S(2)}) collective-permute-start(f32[2,16,128]{2,1,0:T(8,128)S(1)} %get-tuple-element.21), channel_id=1, source_target_pairs={{1,2},{2,1},{5,6},{6,5},{9,10},{10,9},{13,14},{14,13},{17,18},{18,... | collective-permute-start | bytes 49160 | tf_op jit(solution)/shard_map/ppermute | solution.py:31
  34.8 0.5 collective-permute-done.2.cols_first
  35.3 0.0 collective-permute-done.3.cols_second
  35.3 6.3 %collective-permute-done.rows_first = f32[2,128,128]{2,1,0:T(8,128)S(1)} collective-permute-done((f32[2,128,128]{2,1,0:T(8,128)S(1)}, f32[2,128,128]{2,1,0:T(8,128)S(1)}, u32[]{:S(2)}, u32[]{:S(2)}) %collective-permute-start) | collective-permute-done | bytes 131104 | tf_op jit(solution)/shard_map/ppermute | solution.py:31
  41.6 0.0 collective-permute-done.1.rows_second
  41.6 8.5 %yee.1 = (f32[3,16,128,128]{3,2,1,0:T(8,128)}, f32[3,16,128,128]{3,2,1,0:T(8,128)}, f32[4,4,16,128]{3,2,1,0:T(8,128)}, f32[4,4,16,128]{3,2,1,0:T(8,128)}) custom-call(f32[3,16,128,128]{3,2,1,0:T(8,128)} %elec_far.3, f32[3,16,128,128]{3,2,1,0:T(8,128)} %magn_far.3, f32[16,128,128]{2,1,0:T(8,128)} %ret_far.3, f32[16,128,128]{2,1,0:T(8,128)} %coup_far.3, ...), custom_call_target="tpu_custom_call" | custom-call | flops 47185920 | bytes 6291456 | tf_op jit(solution)/shard_map/yee/pallas_call | solution.py:719
  50.1 0.0 all-to-all-done.1.got
  50.2 1.0 %placed.1 = f32[2,16,32,64]{3,2,1,0:T(8,128)} custom-call(f32[32,16,128]{2,1,0:T(8,128)S(1)} %all-to-all-done.1.got), custom_call_target="tpu_custom_call" | custom-call | tf_op jit(solution)/shard_map/placed/pallas_call | solution.py:571
Async XLA Ops:
  0.6 25.2 %copy-start = (bf16[512,512]{1,0:T(8,128)(2,1)S(1)}, bf16[512,512]{1,0:T(8,128)(2,1)}, u32[]{:S(2)}) copy-start(bf16[512,512]{1,0:T(8,128)(2,1)} %constant.8.clone.high) | copy-start | bytes 1572868
  0.6 25.2 %copy-start.1 = (bf16[512,512]{1,0:T(8,128)(2,1)S(1)}, bf16[512,512]{1,0:T(8,128)(2,1)}, u32[]{:S(2)}) copy-start(bf16[512,512]{1,0:T(8,128)(2,1)} %constant.9.clone.low) | copy-start | bytes 1572868
  0.7 27.1 %copy-start.2 = (bf16[512,128]{1,0:T(8,128)(2,1)S(1)}, bf16[512,128]{1,0:T(8,128)(2,1)}, u32[]{:S(2)}) copy-start(bf16[512,128]{1,0:T(8,128)(2,1)} %constant.10.clone.refs_2_) | copy-start | bytes 393220
  0.7 27.1 %copy-start.3 = (bf16[512,128]{1,0:T(8,128)(2,1)S(1)}, bf16[512,128]{1,0:T(8,128)(2,1)}, u32[]{:S(2)}) copy-start(bf16[512,128]{1,0:T(8,128)(2,1)} %constant.11.clone.refs_3_) | copy-start | bytes 393220
  26.5 1.3 %collective-permute-start.4 = (f32[64,256]{1,0:T(8,128)S(1)}, f32[64,256]{1,0:T(8,128)S(1)}, u32[]{:S(2)}, u32[]{:S(2)}) collective-permute-start(f32[64,256]{1,0:T(8,128)S(1)} %get-tuple-element.30), channel_id=1, source_target_pairs={{0,1},{1,0},{2,3},{3,2},{4,5},{5,4},{6,7},{7,6},{8,9},{9,8},{10,11... | collective-permute-start | bytes 196616 | tf_op jit(solution)/shard_map/ppermute | solution.py:36
  29.1 21.1 %all-to-all-start.1 = ((f32[32,16,128]{2,1,0:T(8,128)}), f32[32,16,128]{2,1,0:T(8,128)S(1)}, u32[]{:S(2)}, u32[]{:S(2)}) async-start(f32[32,16,128]{2,1,0:T(8,128)} %along_x.1), calls=%async_computation.1 | async-start | bytes 524288 | tf_op jit(solution)/shard_map/all_to_all | solution.py:764
  31.7 9.9 %collective-permute-start = (f32[2,128,128]{2,1,0:T(8,128)S(1)}, f32[2,128,128]{2,1,0:T(8,128)S(1)}, u32[]{:S(2)}, u32[]{:S(2)}) collective-permute-start(f32[2,128,128]{2,1,0:T(8,128)S(1)} %get-tuple-element.18), channel_id=1, source_target_pairs={{0,4},{4,0},{8,12},{12,8},{16,20},{20,16},{24,28},{28,24},{1,5},{5... | collective-permute-start | bytes 393224 | tf_op jit(solution)/shard_map/ppermute | solution.py:31
  33.4 8.2 %collective-permute-start.1 = (f32[2,128,128]{2,1,0:T(8,128)S(1)}, f32[2,128,128]{2,1,0:T(8,128)S(1)}, u32[]{:S(2)}, u32[]{:S(2)}) collective-permute-start(f32[2,128,128]{2,1,0:T(8,128)S(1)} %get-tuple-element.19), channel_id=1, source_target_pairs={{4,8},{8,4},{12,16},{16,12},{20,24},{24,20},{5,9},{9,5},{13,17},{1... | collective-permute-start | bytes 393224 | tf_op jit(solution)/shard_map/ppermute | solution.py:31
  34.1 1.2 %collective-permute-start.2 = (f32[2,16,128]{2,1,0:T(8,128)S(1)}, f32[2,16,128]{2,1,0:T(8,128)S(1)}, u32[]{:S(2)}, u32[]{:S(2)}) collective-permute-start(f32[2,16,128]{2,1,0:T(8,128)S(1)} %get-tuple-element.20), channel_id=1, source_target_pairs={{0,1},{1,0},{2,3},{3,2},{4,5},{5,4},{6,7},{7,6},{8,9},{9,8},{10,11... | collective-permute-start | bytes 49160 | tf_op jit(solution)/shard_map/ppermute | solution.py:31
  34.1 1.2 %collective-permute-start.3 = (f32[2,16,128]{2,1,0:T(8,128)S(1)}, f32[2,16,128]{2,1,0:T(8,128)S(1)}, u32[]{:S(2)}, u32[]{:S(2)}) collective-permute-start(f32[2,16,128]{2,1,0:T(8,128)S(1)} %get-tuple-element.21), channel_id=1, source_target_pairs={{1,2},{2,1},{5,6},{6,5},{9,10},{10,9},{13,14},{14,13},{17,18},{18,... | collective-permute-start | bytes 49160 | tf_op jit(solution)/shard_map/ppermute | solution.py:31
